TPU v7x, 32 devices: a 4x4x1 block of a 4x4x8 slice. The times are simulated.
32 devices in a mesh: rep: 1 (over z), kv2: 4 (over y), kv: 8 (over x, core).
Axes of the slice: x: 4, y: 4, z: 1, core: 2. Of those that a mesh axis runs over, the one named last changes fastest.
The devices are a block of a 4x4x8 slice.
Arguments:
- x_embed: bfloat16 [2, 768, 2048], P(None, ('rep', 'kv2', 'kv'))
- w_query: bfloat16 [2, 2048, 2048], replicated
- w_key: bfloat16 [2, 2048, 256], replicated
- w_value: bfloat16 [2, 2048, 256], replicated
- w_out: bfloat16 [2, 2048, 2048], replicated
- w_up: bfloat16 [2, 2048, 11008], replicated
- w_down: bfloat16 [2, 11008, 2048], replicated
- k_pool: bfloat16 [3584, 2, 64, 2, 128], P(('rep', 'kv2', 'kv'))
- v_pool: bfloat16 [3584, 2, 64, 2, 128], P(('rep', 'kv2', 'kv'))
- old_table: int32 [768, 2], P(('rep', 'kv2', 'kv'))
- seq_len: int32 [768], P(('rep', 'kv2', 'kv'))
- src_slot: int32 [512], P(('rep', 'kv2', 'kv'))
- dst_slot: int32 [512], P(('rep', 'kv2', 'kv'))
Outputs:
- output 1: bfloat16 [2, 768, 2048], P(None, ('rep', 'kv2', 'kv'))
- output 2: bfloat16 [3584, 2, 64, 2, 128], P(('rep', 'kv2', 'kv'))
- output 3: bfloat16 [3584, 2, 64, 2, 128], P(('rep', 'kv2', 'kv'))
All inputs are finite; a program needn't handle non-finite values.
Results may differ from a plain program's by a relative error of at most 0.0125823.
Values are sent between devices in bfloat16 or wider.
A program may use at most 768 MiB of HBM per device.

v0:
```python
import jax
import jax.numpy as jnp
from jax import lax
from jax.sharding import PartitionSpec as P


def solution(mesh):
    n_rows = mesh.shape['kv2']
    n_cols = mesh.shape['kv']
    dev_axes = ('rep', 'kv2', 'kv')
    seq_spec = P(None, dev_axes, None)
    pool_spec = P(dev_axes, None, None, None, None)
    table_spec = P(dev_axes, None)
    vec_spec = P(dev_axes)
    full_spec = P()

    def per_device(x_embed, w_query, w_key, w_value, w_out, w_up, w_down, k_pool, v_pool, old_table, seq_len, src_slot, dst_slot):
        n_slots, layers, page, kv_heads, head_dim = k_pool.shape
        heads = w_query.shape[2] // head_dim
        q_group = heads // kv_heads
        seq_dev = x_embed.shape[1]
        n_pages = old_table.shape[1]
        row_seqs = seq_dev * n_cols
        slot_base = (lax.axis_index('kv2') * n_cols + lax.axis_index('kv')) * n_slots
        src_all = lax.all_gather(src_slot, ('kv2', 'kv'), tiled=True)
        dst_all = lax.all_gather(dst_slot, ('kv2', 'kv'), tiled=True)
        src_local = src_slot - slot_base
        out_pages = jnp.stack([k_pool[src_local], v_pool[src_local]], axis=1)
        in_pages = lax.all_gather(out_pages, ('kv2', 'kv'), tiled=True)
        dst_local = dst_all - slot_base
        dst_local = jnp.where((dst_local >= 0) & (dst_local < n_slots), dst_local, n_slots)
        k_pool = k_pool.at[dst_local].set(in_pages[:, 0], mode='drop')
        v_pool = v_pool.at[dst_local].set(in_pages[:, 1], mode='drop')
        row_table = lax.all_gather(old_table, 'kv', tiled=True)
        row_len = lax.all_gather(seq_len, 'kv', tiled=True)
        slot_move = jnp.full((n_rows * n_cols * n_slots,), -1, jnp.int32).at[src_all].set(jnp.arange(src_all.shape[0], dtype=jnp.int32))
        move_idx = slot_move[jnp.maximum(row_table, 0)]
        new_table = jnp.where((row_table >= 0) & (move_idx >= 0), dst_all[jnp.maximum(move_idx, 0)], row_table)
        table_local = new_table - slot_base
        owned = (new_table >= 0) & (table_local >= 0) & (table_local < n_slots)
        cell_ids = jnp.arange(row_seqs * n_pages, dtype=jnp.int32).reshape(row_seqs, n_pages)
        slot_cell = jnp.full((n_slots,), -1, jnp.int32).at[jnp.where(owned, table_local, n_slots)].set(cell_ids, mode='drop')
        slot_used = slot_cell >= 0
        seq_of_slot = jnp.where(slot_used, slot_cell // n_pages, 0)
        seg_ids = jnp.where(slot_used, seq_of_slot, row_seqs)
        slot_first = jnp.where(slot_used, slot_cell % n_pages, 0) * page
        tok_off = jnp.arange(page)
        row_ids = jnp.arange(row_seqs)
        q_scale = head_dim ** -0.5
        step_outs = []
        for step_idx in range(2):
            cur_pos = row_len + step_idx
            w_slot = new_table[row_ids, cur_pos // page] - slot_base
            w_slot = jnp.where((w_slot >= 0) & (w_slot < n_slots), w_slot, n_slots)
            w_off = cur_pos % page
            visible = slot_used[:, None] & (tok_off[None, :] <= (cur_pos[seq_of_slot] - slot_first)[:, None])
            hidden = x_embed[step_idx]
            for layer_idx in range(layers):
                query = jnp.dot(hidden, w_query[layer_idx], preferred_element_type=jnp.float32).astype(jnp.bfloat16)
                k_new = jnp.dot(hidden, w_key[layer_idx], preferred_element_type=jnp.float32).astype(jnp.bfloat16)
                v_new = jnp.dot(hidden, w_value[layer_idx], preferred_element_type=jnp.float32).astype(jnp.bfloat16)
                q_row = lax.all_gather(query, 'kv', tiled=True)
                kv_row = lax.all_gather(jnp.stack([k_new, v_new]), 'kv', axis=1, tiled=True).reshape(2, row_seqs, kv_heads, head_dim)
                k_pool = k_pool.at[w_slot, layer_idx, w_off].set(kv_row[0], mode='drop')
                v_pool = v_pool.at[w_slot, layer_idx, w_off].set(kv_row[1], mode='drop')
                q_slot = q_row[seq_of_slot].reshape(n_slots, kv_heads, q_group, head_dim)
                scores = jnp.einsum('sgrd,spgd->sgrp', q_slot, k_pool[:, layer_idx], preferred_element_type=jnp.float32) * q_scale
                scores = jnp.where(visible[:, None, None, :], scores, -1e30)
                slot_max = scores.max(axis=-1)
                expo = jnp.exp(scores - slot_max[..., None])
                slot_out = jnp.einsum('sgrp,spgd->sgrd', expo.astype(jnp.bfloat16), v_pool[:, layer_idx], preferred_element_type=jnp.float32)
                seq_max = jnp.full((row_seqs, kv_heads, q_group), -1e30, jnp.float32).at[seg_ids].max(slot_max, mode='drop')
                slot_w = jnp.exp(jnp.where(slot_used[:, None, None], slot_max - seq_max[seq_of_slot], -1e30))
                seq_sum = jax.ops.segment_sum(slot_w * expo.sum(axis=-1), seg_ids, num_segments=row_seqs)
                seq_out = jax.ops.segment_sum(slot_w[..., None] * slot_out, seg_ids, num_segments=row_seqs)
                partial_res = jnp.concatenate([seq_max[..., None], seq_sum[..., None], seq_out], axis=-1)
                home = lax.all_to_all(partial_res, 'kv', 0, 0, tiled=True).reshape(n_cols, seq_dev, kv_heads, q_group, head_dim + 2)
                scale_w = jnp.exp(home[..., 0] - home[..., 0].max(axis=0))
                total = (scale_w * home[..., 1]).sum(axis=0)
                attn_out = ((scale_w[..., None] * home[..., 2:]).sum(axis=0) / total[..., None]).astype(jnp.bfloat16).reshape(seq_dev, heads * head_dim)
                hidden = (hidden.astype(jnp.float32) + jnp.dot(attn_out, w_out[layer_idx], preferred_element_type=jnp.float32)).astype(jnp.bfloat16)
                up_act = jax.nn.gelu(jnp.dot(hidden, w_up[layer_idx], preferred_element_type=jnp.float32)).astype(jnp.bfloat16)
                hidden = (hidden.astype(jnp.float32) + jnp.dot(up_act, w_down[layer_idx], preferred_element_type=jnp.float32)).astype(jnp.bfloat16)
            step_outs.append(hidden)
        return jnp.stack(step_outs), k_pool, v_pool

    return jax.shard_map(per_device, mesh=mesh, in_specs=(seq_spec, full_spec, full_spec, full_spec, full_spec, full_spec, full_spec, pool_spec, pool_spec, table_spec, vec_spec, vec_spec, vec_spec), out_specs=(seq_spec, pool_spec, pool_spec), check_vma=False)
```

profile of v0, /device:TPU:97, one launch (start us, length us, event | category | flops | bytes accessed | tf_op | source)
XLA Modules:
  0.0 1552.2 jit_solution(18289576711785242228)
XLA Ops:
  34.0 19.7 %all-gather = s32[8,24,2]{1,2,0:T(2,128)S(1)} all-gather(s32[1,24,2]{1,2,0:T(2,128)S(1)} %bitcast.397), channel_id=1, replica_groups=mesh['rep'=1,'kv2'=4,'kv'=8] {'kv'}, dimensions={0}, use_global_device_ids=true | all-gather | bytes 1728 | tf_op jit(solution)/shard_map/all_gather | solution.py:34
  54.5 53.6 %all-reduce.3 = (s32[512]{0:T(512)S(1)}, s32[512]{0:T(512)S(1)}) all-reduce(s32[512]{0:T(512)S(1)} %dynamic-update-slice.1, s32[512]{0:T(512)S(1)} %dynamic-update-slice), channel_id=1, replica_groups=mesh['rep'=1,'kv2'=4,'kv'=8] {'kv2','kv'}, use_global_device_ids=true, to_apply=%add.1 | all-reduce | flops 1024 | bytes 8192
  138.7 20.6 %all_gather.45 = bf16[2,192,256]{2,1,0:T(8,128)(2,1)S(1)} all-gather(bf16[2,24,256]{2,1,0:T(8,128)(2,1)S(1)} %pad_maximum_fusion.6), channel_id=1, replica_groups=mesh['rep'=1,'kv2'=4,'kv'=8] {'kv'}, dimensions={1}, use_global_device_ids=true | all-gather | bytes 221184 | tf_op jit(solution)/shard_map/all_gather | solution.py:63
  164.6 26.5 %all_gather.43 = bf16[192,2048]{1,0:T(8,128)(2,1)S(1)} all-gather(bf16[24,2048]{1,0:T(8,128)(2,1)S(1)} %fusion.104), channel_id=1, replica_groups=mesh['rep'=1,'kv2'=4,'kv'=8] {'kv'}, dimensions={0}, use_global_device_ids=true | all-gather | bytes 884736 | tf_op jit(solution)/shard_map/all_gather | solution.py:62
  197.8 22.0 %all_gather.49 = bf16[2,192,256]{2,1,0:T(8,128)(2,1)S(1)} all-gather(bf16[2,24,256]{2,1,0:T(8,128)(2,1)S(1)} %pad_maximum_fusion.8), channel_id=1, replica_groups=mesh['rep'=1,'kv2'=4,'kv'=8] {'kv'}, dimensions={1}, use_global_device_ids=true | all-gather | bytes 221184 | tf_op jit(solution)/shard_map/all_gather | solution.py:63
  221.8 19.3 %all-gather.3.cloned.1.call-done = bf16[512,2,2,64,2,128]{5,4,3,2,0,1:T(2,128)(2,1)} async-done(((bf16[16,2,2,64,2,128]{5,4,3,2,0,1:T(2,128)(2,1)}), bf16[512,2,2,64,2,128]{5,4,3,2,0,1:T(2,128)(2,1)}) %all-gather.3.cloned.1.call-update) | async-done | bytes 67108880 | tf_op jit(solution)/shard_map/all_gather | solution.py:29
  241.0 83.3 %slice_bitcast_fusion.1 = (bf16[512,2,64,2,128]{4,3,2,1,0:T(2,128)(2,1)}, bf16[512,2,64,2,128]{4,3,2,1,0:T(2,128)(2,1)}) fusion(bf16[512,2,2,64,2,128]{5,4,3,2,0,1:T(2,128)(2,1)} %all-gather.3.cloned.1.call-done), kind=kLoop, calls=%fused_computation.65 | loop fusion | bytes 134217728 | tf_op jit(solution)/shard_map/squeeze | solution.py:32
  324.3 168.1 %scatter_fusion = bf16[112,2,64,2,128]{4,3,2,1,0:T(2,128)(2,1)} fusion(bf16[112,2,64,2,128]{4,3,2,1,0:T(2,128)(2,1)} %copy.531, s32[512]{0:T(512)S(1)} %compare_select_fusion.3, bf16[512,2,64,2,128]{4,3,2,1,0:T(2,128)(2,1)} %get-tuple-element.27), kind=kCustom, calls=%fused_computation.18 | custom fusion | bytes 100665344 | tf_op jit(solution)/shard_map/scatter | solution.py:32
  492.4 25.1 %scatter_fusion.1 = bf16[112,2,64,2,128]{4,3,2,1,0:T(2,128)(2,1)} fusion(bf16[112,2,64,2,128]{4,3,2,1,0:T(2,128)(2,1)} %scatter_fusion, s32[192]{0:T(256)S(1)} %bitcast.361, bf16[192,2,128]{2,1,0:T(2,128)(2,1)S(1)} %reshape.436), kind=kCustom, calls=%fused_computation.19 | custom fusion | bytes 297216 | tf_op jit(solution)/shard_map/scatter | solution.py:64
  542.1 168.1 %scatter_fusion.4 = bf16[112,2,64,2,128]{4,3,2,1,0:T(2,128)(2,1)} fusion(bf16[112,2,64,2,128]{4,3,2,1,0:T(2,128)(2,1)} %copy.532, s32[512]{0:T(512)S(1)} %copy-done.26, bf16[512,2,64,2,128]{4,3,2,1,0:T(2,128)(2,1)} %get-tuple-element.28), kind=kCustom, calls=%fused_computation.22 | custom fusion | bytes 100665344 | tf_op jit(solution)/shard_map/scatter | solution.py:33
  710.2 25.3 %scatter_fusion.5 = bf16[112,2,64,2,128]{4,3,2,1,0:T(2,128)(2,1)} fusion(bf16[112,2,64,2,128]{4,3,2,1,0:T(2,128)(2,1)} %scatter_fusion.4, s32[192]{0:T(256)S(1)} %bitcast.362, bf16[192,2,128]{2,1,0:T(2,128)(2,1)S(1)} %reshape.466), kind=kCustom, calls=%fused_computation.23 | custom fusion | bytes 297216 | tf_op jit(solution)/shard_map/scatter | solution.py:65
  767.9 44.6 %all-to-all-start = ((f32[192,2,8,130]{3,2,1,0:T(8,128)}), f32[192,2,8,130]{3,2,1,0:T(8,128)}, u32[]{:S(2)}, u32[]{:S(2)}) async-start(f32[192,2,8,130]{3,2,1,0:T(8,128)} %pad_maximum_fusion), calls=%async_computation | async-start | bytes 6291456 | tf_op jit(solution)/shard_map/all_to_all | solution.py:77
  817.1 44.7 %all_gather.48 = bf16[192,2048]{1,0:T(8,128)(2,1)S(1)} all-gather(bf16[24,2048]{1,0:T(8,128)(2,1)S(1)} %fusion.107), channel_id=1, replica_groups=mesh['rep'=1,'kv2'=4,'kv'=8] {'kv'}, dimensions={0}, use_global_device_ids=true | all-gather | bytes 884736 | tf_op jit(solution)/shard_map/all_gather | solution.py:62
  876.0 29.7 %fusion.89 = bf16[24,2048]{1,0:T(8,128)(2,1)S(1)} fusion(bf16[2,11008,2048]{2,1,0:T(8,128)(2,1)} %param.19, bf16[24,2048]{1,0:T(8,128)(2,1)S(1)} %fusion.101, bf16[2,2048,11008]{2,1,0:T(8,128)(2,1)} %param.18), kind=kOutput, calls=%fused_computation.121 | convolution fusion | flops 2166786048 | bytes 90472448 | tf_op jit(solution)/shard_map/dot_general | solution.py:83
  907.5 21.1 %all_gather.47 = bf16[2,192,256]{2,1,0:T(8,128)(2,1)S(1)} all-gather(bf16[2,24,256]{2,1,0:T(8,128)(2,1)S(1)} %pad_maximum_fusion.7), channel_id=1, replica_groups=mesh['rep'=1,'kv2'=4,'kv'=8] {'kv'}, dimensions={1}, use_global_device_ids=true | all-gather | bytes 221184 | tf_op jit(solution)/shard_map/all_gather | solution.py:63
  928.6 25.2 %scatter_fusion.7 = bf16[112,2,64,2,128]{4,3,2,1,0:T(2,128)(2,1)} fusion(bf16[112,2,64,2,128]{4,3,2,1,0:T(2,128)(2,1)} %scatter_fusion.1, s32[192]{0:T(256)S(1)} %bitcast.357, bf16[192,2,128]{2,1,0:T(2,128)(2,1)S(1)} %reshape.480), kind=kCustom, calls=%fused_computation.25 | custom fusion | bytes 297216 | tf_op jit(solution)/shard_map/scatter | solution.py:64
  953.8 10.2 slice.266
  964.1 25.1 %scatter_fusion.12 = bf16[112,2,64,2,128]{4,3,2,1,0:T(2,128)(2,1)} fusion(bf16[112,2,64,2,128]{4,3,2,1,0:T(2,128)(2,1)} %scatter_fusion.7, s32[192]{0:T(256)S(1)} %bitcast.359, bf16[192,2,128]{2,1,0:T(2,128)(2,1)S(1)} %reshape.516), kind=kCustom, calls=%fused_computation.30 | custom fusion | bytes 297216 | tf_op jit(solution)/shard_map/scatter | solution.py:64
  1014.0 25.1 %scatter_fusion.10 = bf16[112,2,64,2,128]{4,3,2,1,0:T(2,128)(2,1)} fusion(bf16[112,2,64,2,128]{4,3,2,1,0:T(2,128)(2,1)} %scatter_fusion.5, s32[192]{0:T(256)S(1)} %bitcast.358, bf16[192,2,128]{2,1,0:T(2,128)(2,1)S(1)} %reshape.502), kind=kCustom, calls=%fused_computation.28 | custom fusion | bytes 297216 | tf_op jit(solution)/shard_map/scatter | solution.py:65
  1049.3 25.1 %scatter_fusion.15 = bf16[112,2,64,2,128]{4,3,2,1,0:T(2,128)(2,1)} fusion(bf16[112,2,64,2,128]{4,3,2,1,0:T(2,128)(2,1)} %scatter_fusion.10, s32[192]{0:T(256)S(1)} %bitcast.360, bf16[192,2,128]{2,1,0:T(2,128)(2,1)S(1)} %reshape.538), kind=kCustom, calls=%fused_computation.33 | custom fusion | bytes 297216 | tf_op jit(solution)/shard_map/scatter | solution.py:65
  1074.4 10.3 slice.275
  1107.2 21.0 %all-to-all-start.2 = ((f32[192,2,8,130]{3,2,1,0:T(8,128)}), f32[192,2,8,130]{3,2,1,0:T(8,128)}, u32[]{:S(2)}, u32[]{:S(2)}) async-start(f32[192,2,8,130]{3,2,1,0:T(8,128)} %pad_maximum_fusion.2), calls=%async_computation.2 | async-start | bytes 6291456 | tf_op jit(solution)/shard_map/all_to_all | solution.py:77
  1132.8 45.0 %all_gather.46 = bf16[192,2048]{1,0:T(8,128)(2,1)S(1)} all-gather(bf16[24,2048]{1,0:T(8,128)(2,1)S(1)} %fusion.110), channel_id=1, replica_groups=mesh['rep'=1,'kv2'=4,'kv'=8] {'kv'}, dimensions={0}, use_global_device_ids=true | all-gather | bytes 884736 | tf_op jit(solution)/shard_map/all_gather | solution.py:62
  1206.4 29.7 %fusion.86 = bf16[24,2048]{1,0:T(8,128)(2,1)S(1)} fusion(bf16[2,11008,2048]{2,1,0:T(8,128)(2,1)} %param.19, bf16[24,2048]{1,0:T(8,128)(2,1)S(1)} %fusion.98, bf16[2,2048,11008]{2,1,0:T(8,128)(2,1)} %param.18), kind=kOutput, calls=%fused_computation.120 | convolution fusion | flops 2166786048 | bytes 90472448 | tf_op jit(solution)/shard_map/dot_general | solution.py:83
  1242.5 20.4 %all_gather.51 = bf16[2,192,256]{2,1,0:T(8,128)(2,1)S(1)} all-gather(bf16[2,24,256]{2,1,0:T(8,128)(2,1)S(1)} %pad_maximum_fusion.9), channel_id=1, replica_groups=mesh['rep'=1,'kv2'=4,'kv'=8] {'kv'}, dimensions={1}, use_global_device_ids=true | all-gather | bytes 221184 | tf_op jit(solution)/shard_map/all_gather | solution.py:63
  1263.6 25.3 %scatter_fusion.17 = bf16[112,2,64,2,128]{4,3,2,1,0:T(2,128)(2,1)} fusion(bf16[112,2,64,2,128]{4,3,2,1,0:T(2,128)(2,1)} %scatter_fusion.12, s32[192]{0:T(256)S(1)} %bitcast.355, bf16[192,2,128]{2,1,0:T(2,128)(2,1)S(1)} %reshape.552), kind=kCustom, calls=%fused_computation.35 | custom fusion | bytes 297216 | tf_op jit(solution)/shard_map/scatter | solution.py:64
  1299.1 26.0 %all_gather.50 = bf16[192,2048]{1,0:T(8,128)(2,1)S(1)} all-gather(bf16[24,2048]{1,0:T(8,128)(2,1)S(1)} %fusion.113), channel_id=1, replica_groups=mesh['rep'=1,'kv2'=4,'kv'=8] {'kv'}, dimensions={0}, use_global_device_ids=true | all-gather | bytes 884736 | tf_op jit(solution)/shard_map/all_gather | solution.py:62
  1365.3 10.4 all-to-all-start.1
  1387.9 25.1 %scatter_fusion.20 = bf16[112,2,64,2,128]{4,3,2,1,0:T(2,128)(2,1)} fusion(bf16[112,2,64,2,128]{4,3,2,1,0:T(2,128)(2,1)} %scatter_fusion.15, s32[192]{0:T(256)S(1)} %bitcast.356, bf16[192,2,128]{2,1,0:T(2,128)(2,1)S(1)} %reshape.574), kind=kCustom, calls=%fused_computation.38 | custom fusion | bytes 297216 | tf_op jit(solution)/shard_map/scatter | solution.py:65
  1432.4 12.4 scatter_fusion.21
  1472.7 29.6 %fusion.116 = bf16[1,24,2048]{2,1,0:T(8,128)(2,1)S(1)} fusion(bf16[2,11008,2048]{2,1,0:T(8,128)(2,1)} %param.19, bf16[24,2048]{1,0:T(8,128)(2,1)S(1)} %fusion.95, bf16[2,2048,11008]{2,1,0:T(8,128)(2,1)} %param.18), kind=kOutput, calls=%fused_computation.130 | convolution fusion | flops 2166786048 | bytes 90472448 | tf_op jit(solution)/shard_map/dot_general | solution.py:83
  1514.6 29.9 %fusion.119 = bf16[1,24,2048]{2,1,0:T(8,128)(2,1)S(1)} fusion(bf16[2,11008,2048]{2,1,0:T(8,128)(2,1)} %param.19, bf16[24,2048]{1,0:T(8,128)(2,1)S(1)} %fusion.92, bf16[2,2048,11008]{2,1,0:T(8,128)(2,1)} %param.18), kind=kOutput, calls=%fused_computation.131 | convolution fusion | flops 2166786048 | bytes 90472448 | tf_op jit(solution)/shard_map/dot_general | solution.py:83
  (292 shorter events, 368.5 us)
Async XLA Ops:
  7.2 233.9 %all-gather.3.cloned.1.call-start = ((), (), s32[]{:S(2)}) async-start(), calls=%async_computation.4 | async-start | bytes 69206016 | tf_op jit(solution)/shard_map/all_gather | solution.py:29
  29.6 24.7 %copy-start.42 = (s32[16]{0:T(128)S(1)}, s32[16]{0:T(128)}, u32[]{:S(2)}) copy-start(s32[16]{0:T(128)} %param.25) | copy-start | bytes 196
  116.0 20.9 %copy-start.5 = (bf16[2,2048,256]{2,1,0:T(8,128)(2,1)S(1)}, bf16[2,2048,256]{2,1,0:T(8,128)(2,1)}, u32[]{:S(2)}) copy-start(bf16[2,2048,256]{2,1,0:T(8,128)(2,1)} %param.15) | copy-start | bytes 6291460
  116.0 20.9 %copy-start.38 = (bf16[2,24,2048]{2,1,0:T(8,128)(2,1)S(1)}, bf16[2,24,2048]{2,1,0:T(8,128)(2,1)}, u32[]{:S(2)}) copy-start(bf16[2,24,2048]{2,1,0:T(8,128)(2,1)} %param.13) | copy-start | bytes 589828
  120.2 73.6 %copy-start.36 = (s32[112]{0:T(128)}, s32[112]{0:T(128)S(1)}, u32[]{:S(2)}) copy-start(s32[112]{0:T(128)S(1)} %scatter_custom_fusion.1) | copy-start | bytes 1348
  192.0 28.4 %copy-start.34 = (s32[192]{0:T(256)S(1)}, s32[192]{0:T(256)}, u32[]{:S(2)}) copy-start(s32[192]{0:T(256)} %gather_fusion.12) | copy-start | bytes 2308
  192.0 28.4 %copy-start.35 = (s32[192]{0:T(256)S(1)}, s32[192]{0:T(256)}, u32[]{:S(2)}) copy-start(s32[192]{0:T(256)} %gather_fusion.6) | copy-start | bytes 2308
  192.0 29.0 %copy-start.29 = (s32[192]{0:T(256)S(1)}, s32[192]{0:T(256)}, u32[]{:S(2)}) copy-start(s32[192]{0:T(256)} %get-tuple-element.51) | copy-start | bytes 2308
  220.4 313.9 %copy-start.30 = (pred[112]{0:T(512)(128)(4,1)}, pred[112]{0:T(512)(128)(4,1)S(1)}, u32[]{:S(2)}) copy-start(pred[112]{0:T(512)(128)(4,1)S(1)} %broadcast_compare_fusion.5) | copy-start | bytes 340
  221.1 103.3 %copy-start.25 = (s32[512]{0:T(512)}, s32[512]{0:T(512)S(1)}, u32[]{:S(2)}) copy-start(s32[512]{0:T(512)S(1)} %compare_select_fusion.3) | copy-start | bytes 6148
  221.8 304.2 %copy-start.21 = (pred[112,64]{1,0:T(8,128)(4,1)}, pred[112,64]{1,0:T(8,128)(4,1)S(1)}, u32[]{:S(2)}) copy-start(pred[112,64]{1,0:T(8,128)(4,1)S(1)} %get-tuple-element.57) | copy-start | bytes 21508
  528.2 14.0 copy-start.26
  735.5 13.7 copy-start.24
  767.8 44.6 %copy-start.39 = (bf16[2,24,2048]{2,1,0:T(8,128)(2,1)S(1)}, bf16[2,24,2048]{2,1,0:T(8,128)(2,1)}, u32[]{:S(2)}) copy-start(bf16[2,24,2048]{2,1,0:T(8,128)(2,1)} %param.13) | copy-start | bytes 589828
  767.9 95.8 %all-to-all-start = ((f32[192,2,8,130]{3,2,1,0:T(8,128)}), f32[192,2,8,130]{3,2,1,0:T(8,128)}, u32[]{:S(2)}, u32[]{:S(2)}) async-start(f32[192,2,8,130]{3,2,1,0:T(8,128)} %pad_maximum_fusion), calls=%async_computation | async-start | bytes 6291456 | tf_op jit(solution)/shard_map/all_to_all | solution.py:77
  817.0 46.5 %copy-start.28 = (s32[192]{0:T(256)S(1)}, s32[192]{0:T(256)}, u32[]{:S(2)}) copy-start(s32[192]{0:T(256)} %get-tuple-element.50) | copy-start | bytes 2308
  817.1 46.5 %copy-start.33 = (s32[192]{0:T(256)S(1)}, s32[192]{0:T(256)}, u32[]{:S(2)}) copy-start(s32[192]{0:T(256)} %get-tuple-element.66) | copy-start | bytes 2308
  876.0 29.7 %copy-start.6 = (bf16[2,2048,256]{2,1,0:T(8,128)(2,1)S(1)}, bf16[2,2048,256]{2,1,0:T(8,128)(2,1)}, u32[]{:S(2)}) copy-start(bf16[2,2048,256]{2,1,0:T(8,128)(2,1)} %param.15) | copy-start | bytes 6291460
  905.7 222.5 %copy-start.15 = (bf16[24,2048]{1,0:T(8,128)(2,1)}, bf16[24,2048]{1,0:T(8,128)(2,1)S(1)}, u32[]{:S(2)}) copy-start(bf16[24,2048]{1,0:T(8,128)(2,1)S(1)} %fusion.89) | copy-start | bytes 294916
  1074.4 13.8 copy-start.23
  1107.2 86.9 %all-to-all-start.2 = ((f32[192,2,8,130]{3,2,1,0:T(8,128)}), f32[192,2,8,130]{3,2,1,0:T(8,128)}, u32[]{:S(2)}, u32[]{:S(2)}) async-start(f32[192,2,8,130]{3,2,1,0:T(8,128)} %pad_maximum_fusion.2), calls=%async_computation.2 | async-start | bytes 6291456 | tf_op jit(solution)/shard_map/all_to_all | solution.py:77
  1132.8 46.0 %copy-start.22 = (pred[112,64]{1,0:T(8,128)(4,1)S(1)}, pred[112,64]{1,0:T(8,128)(4,1)}, u32[]{:S(2)}) copy-start(pred[112,64]{1,0:T(8,128)(4,1)} %copy-done.21) | copy-start | bytes 21508
  1206.4 29.7 %copy-start.7 = (bf16[2,2048,256]{2,1,0:T(8,128)(2,1)S(1)}, bf16[2,2048,256]{2,1,0:T(8,128)(2,1)}, u32[]{:S(2)}) copy-start(bf16[2,2048,256]{2,1,0:T(8,128)(2,1)} %param.15) | copy-start | bytes 6291460
  1299.1 27.0 %copy-start.20 = (pred[112,64]{1,0:T(8,128)(4,1)S(1)}, pred[112,64]{1,0:T(8,128)(4,1)}, u32[]{:S(2)}) copy-start(pred[112,64]{1,0:T(8,128)(4,1)} %get-tuple-element.56) | copy-start | bytes 21508
  1326.2 11.4 copy-start.12
  1326.2 11.4 copy-start.13
  1326.2 12.5 copy-start.3
  1330.5 12.3 copy-start.10
  1342.9 17.7 %copy-start.1 = (f32[192,2,8,1]{3,2,1,0:T(8,128)S(1)}, f32[192,2,8,1]{3,2,1,0:T(8,128)}, u32[]{:S(2)}) copy-start(f32[192,2,8,1]{3,2,1,0:T(8,128)} %copy.372) | copy-start | bytes 36868
  1365.3 85.2 %all-to-all-start.1 = ((f32[192,2,8,130]{3,2,1,0:T(8,128)}), f32[192,2,8,130]{3,2,1,0:T(8,128)S(1)}, u32[]{:S(2)}, u32[]{:S(2)}) async-start(f32[192,2,8,130]{3,2,1,0:T(8,128)} %pad_maximum_fusion.1), calls=%async_computation.1 | async-start | bytes 6291456 | tf_op jit(solution)/shard_map/all_to_all | solution.py:77
  1413.0 13.8 copy-start.11
  1450.5 51.8 %all-to-all-start.3 = ((f32[192,2,8,130]{3,2,1,0:T(8,128)}), f32[192,2,8,130]{3,2,1,0:T(8,128)}, u32[]{:S(2)}, u32[]{:S(2)}) async-start(f32[192,2,8,130]{3,2,1,0:T(8,128)} %pad_maximum_fusion.3), calls=%async_computation.3 | async-start | bytes 6291456 | tf_op jit(solution)/shard_map/all_to_all | solution.py:77
  (18 other events, 112.1 us)
Sparse Core Ops, SparseCore 0:
  34.1 206.8 all-gather.2
where the time goes:
time: 1570 us; the launch traced here: 1550 us
  local copies, waits for them, and re-layouts  794 us (51%)
  blocking collectives  306 us (19%)
  matrix products  193 us (12%)
  other arithmetic  138 us (9%)
  starting transfers between devices  85.5 us (5%)
  waiting for transfers between devices  19.3 us (1%)
  between operations  16.3 us (1%)
    scatter x1, local copies, waits for them, and re-layouts, per_device(): k_pool = k_pool.at[dst_local].set(in_pages[:, 0], mode='drop')  168 us
    scatter x1, local copies, waits for them, and re-layouts, per_device(): v_pool = v_pool.at[dst_local].set(in_pages[:, 1], mode='drop')  168 us
    all_gather x4, blocking collectives, per_device(): q_row = lax.all_gather(query, 'kv', tiled=True)  142 us
    dot_general x4, matrix products, per_device(): jnp.dot(up_act, w_down[layer_idx], preferred_element_type=jnp.float32)  119 us
    scatter x4, local copies, waits for them, and re-layouts, per_device(): k_pool = k_pool.at[w_slot, layer_idx, w_off].set(kv_row[0], mode='drop')  101 us
    scatter x4, local copies, waits for them, and re-layouts, per_device(): v_pool = v_pool.at[w_slot, layer_idx, w_off].set(kv_row[1], mode='drop')  100 us
    all_to_all x4, starting transfers between devices, per_device(): lax.all_to_all(partial_res, 'kv', 0, 0, tiled=True)  85.4 us
    all_gather x4, blocking collectives, per_device(): lax.all_gather(jnp.stack([k_new, v_new]), 'kv', axis=1, tiled=True)  84.1 us
  transfers between devices with their start and end apart: 5, of which 1 were waited for; matrix products, arithmetic and copies ran while one was open for 12% of the time, Pallas kernels for 0%

commit v1 on v0

v1 whole, which is shorter than its diff:
```python
import functools

import jax
import jax.numpy as jnp
from jax import lax
from jax.experimental import pallas as pl
from jax.experimental.pallas import tpu as pltpu
from jax.sharding import PartitionSpec as P

MESH = pl.DeviceIdType.MESH
ANY = pl.BlockSpec(memory_space=pl.ANY)
SMEM = pl.BlockSpec(memory_space=pltpu.SMEM)
VMEM = pl.BlockSpec(memory_space=pltpu.VMEM)
F32 = jnp.float32
BF16 = jnp.bfloat16
NEG = -1e30


def flat_id(n_cols):
    return lax.axis_index('kv2') * n_cols + lax.axis_index('kv')


def where_is(flat, n_cols):
    return {'kv2': flat // n_cols, 'kv': flat % n_cols}


def greet_all(n_dev, n_cols):
    me = flat_id(n_cols)
    barrier = pltpu.get_barrier_semaphore()

    @pl.loop(1, n_dev)
    def _(r):
        pl.semaphore_signal(barrier, inc=1, device_id=where_is((me + r) % n_dev, n_cols), device_id_type=MESH)

    pl.semaphore_wait(barrier, n_dev - 1)


def gather_all_kernel(n_dev, n_cols, x_ref, o_ref, local_sem, send_sem, recv_sem):
    me = flat_id(n_cols)
    greet_all(n_dev, n_cols)

    def copy(r, dst, slot):
        return pltpu.make_async_remote_copy(
            src_ref=x_ref, dst_ref=o_ref.at[slot], send_sem=send_sem.at[r], recv_sem=recv_sem.at[r],
            device_id=where_is(dst, n_cols), device_id_type=MESH)

    @pl.loop(1, n_dev)
    def _(r):
        copy(r, (me + r) % n_dev, me).start()

    own = pltpu.make_async_copy(x_ref, o_ref.at[me], local_sem)
    own.start()
    own.wait()

    @pl.loop(1, n_dev)
    def _(r):
        c = copy(r, (me + r) % n_dev, (me + n_dev - r) % n_dev)
        c.wait_send()
        c.wait_recv()


def row_gather_kernel(n_cols, x_ref, o_ref, local_sem, send_sem, recv_sem, fsend_sem, frecv_sem):
    n_chips = n_cols // 2
    kv = lax.axis_index('kv')
    chip, core = kv // 2, kv % 2
    mate = chip * 2 + 1 - core
    barrier = pltpu.get_barrier_semaphore()
    for r in range(1, n_chips):
        pl.semaphore_signal(barrier, inc=1, device_id={'kv': (chip + r) % n_chips * 2 + core}, device_id_type=MESH)
    pl.semaphore_signal(barrier, inc=1, device_id={'kv': mate}, device_id_type=MESH)
    pl.semaphore_wait(barrier, n_chips)

    def copy(r, dst, slot):
        return pltpu.make_async_remote_copy(
            src_ref=x_ref, dst_ref=o_ref.at[slot], send_sem=send_sem.at[r], recv_sem=recv_sem.at[r],
            device_id={'kv': dst}, device_id_type=MESH)

    def forward(r, slot):
        return pltpu.make_async_remote_copy(
            src_ref=o_ref.at[slot], dst_ref=o_ref.at[slot], send_sem=fsend_sem.at[r], recv_sem=frecv_sem.at[r],
            device_id={'kv': mate}, device_id_type=MESH)

    for r in range(1, n_chips):
        copy(r, (chip + r) % n_chips * 2 + core, kv).start()
    copy(0, mate, kv).start()
    own = pltpu.make_async_copy(x_ref, o_ref.at[kv], local_sem)
    own.start()
    own.wait()
    for r in range(1, n_chips):
        slot = (chip + n_chips - r) % n_chips * 2 + core
        copy(r, mate, slot).wait_recv()
        forward(r, slot).start()
    for r in range(1, n_chips):
        copy(r, mate, kv).wait_send()
        forward(r, (chip + n_chips - r) % n_chips * 2 + core).wait_send()
        forward(r, (chip + n_chips - r) % n_chips * 2 + 1 - core).wait_recv()
    c = copy(0, mate, mate)
    c.wait_send()
    c.wait_recv()


def row_exchange_kernel(n_cols, x_ref, y_ref, ox_ref, oy_ref, local_sem, send_sem, recv_sem):
    kv = lax.axis_index('kv')
    barrier = pltpu.get_barrier_semaphore()
    for r in range(1, n_cols):
        pl.semaphore_signal(barrier, inc=1, device_id={'kv': (kv + r) % n_cols}, device_id_type=MESH)
    pl.semaphore_wait(barrier, n_cols - 1)

    def copy(a, r, dst, slot):
        src_ref, dst_ref = ((x_ref, ox_ref), (y_ref, oy_ref))[a]
        return pltpu.make_async_remote_copy(
            src_ref=src_ref.at[dst], dst_ref=dst_ref.at[slot], send_sem=send_sem.at[a, r], recv_sem=recv_sem.at[a, r],
            device_id={'kv': dst}, device_id_type=MESH)

    for r in range(1, n_cols):
        for a in range(2):
            copy(a, r, (kv + r) % n_cols, kv).start()
    own = [pltpu.make_async_copy(s.at[kv], d.at[kv], local_sem.at[a]) for a, (s, d) in enumerate(((x_ref, ox_ref), (y_ref, oy_ref)))]
    for c in own:
        c.start()
    for c in own:
        c.wait()
    for r in range(1, n_cols):
        for a in range(2):
            c = copy(a, r, (kv + r) % n_cols, (kv + n_cols - r) % n_cols)
            c.wait_send()
            c.wait_recv()


def plan_kernel(dims, who_ref, tab_ref, none_ref, pages_ref, info_ref, most_ref, moved, count, seen, sem):
    n_dev, n_cols, n_slots, seq_dev, n_moves, cap, page, magic, shift = dims
    n_chips = n_dev // 2
    o_len, o_src, o_dst = 2 * seq_dev, 3 * seq_dev, 3 * seq_dev + n_moves
    me = who_ref[0]
    row0 = who_ref[1]
    base = me * n_slots
    fill = pltpu.make_async_copy(none_ref, moved, sem)
    fill.start()

    @pl.loop(0, n_chips)
    def _(i):
        count[i] = 0

    @pl.loop(0, n_cols * seq_dev)
    def _(i):
        seen[i] = 0

    @pl.loop(0, n_slots)
    def _(i):
        for f in range(4):
            info_ref[f * n_slots + i] = -1

    @pl.loop(0, n_dev * cap)
    def _(i):
        pages_ref[i] = 0

    fill.wait()

    @pl.loop(0, n_dev)
    def _(d):
        for j in range(n_moves):
            src = tab_ref[d, o_src + j]
            dst = tab_ref[d, o_dst + j]
            m = d * n_moves + j
            moved[src] = dst
            dd = (dst * magic) >> shift
            chip = dd >> 1
            n = count[chip]
            count[chip] = n + 1

            @pl.when(n < 2 * cap)
            def _():
                pages_ref[chip * 2 * cap + n] = m

            @pl.when(dd == me)
            def _():
                info_ref[dst - base] = n
                info_ref[n_slots + dst - base] = m

    def biggest(i, best):
        return jnp.maximum(best, count[i])

    most_ref[0] = lax.fori_loop(0, n_chips, biggest, jnp.int32(0))

    @pl.loop(0, n_cols)
    def _(h):
        @pl.loop(0, seq_dev)
        def _(i):
            b = h * seq_dev + i
            length = tab_ref[row0 + h, o_len + i]
            for j in range(2):
                e = tab_ref[row0 + h, 2 * i + j]
                e0 = jnp.maximum(e, 0)
                mv = moved[e0]
                s = jnp.where(mv >= 0, mv, e0) - base

                @pl.when((e >= 0) & (s >= 0) & (s < n_slots))
                def _():
                    info_ref[2 * n_slots + s] = b
                    info_ref[4 * n_slots + s] = length - page * j

    @pl.loop(0, n_slots)
    def _(s):
        b = info_ref[2 * n_slots + s]

        @pl.when(b >= 0)
        def _():
            info_ref[5 * n_slots + s] = seen[b]
            seen[b] = 1


def pack_kernel(n_moves, src_ref, k_ref, v_ref, *rest):
    *outs, sem = rest

    def copies(m):
        s = src_ref[m]
        for layer, o_ref in enumerate(outs):
            half = o_ref.shape[0] // 2
            for a, pool in enumerate((k_ref, v_ref)):
                yield pltpu.make_async_copy(pool.at[s, layer], o_ref.at[pl.ds(a * half, half), m], sem.at[layer, a, m])

    for m in range(n_moves):
        for c in copies(m):
            c.start()
    for m in range(n_moves):
        for c in copies(m):
            c.wait()


def regroup_kernel(cap, pages_ref, x_ref, o_ref):
    @pl.loop(0, o_ref.shape[0])
    def _(d):
        for n in range(cap):
            o_ref[d, n] = x_ref[pages_ref[d * cap + n]]


def attend_kernel(dims, info_ref, most_ref, who_ref, q_ref, k_ref, v_ref, own_ref, mate_ref, slow_ref, *rest):
    layer, n_slots, blk, group, cap, scale, first = dims
    ko_ref, vo_ref, o_ref, ml_ref, kbuf, vbuf, sem = rest if first else rest[2:]
    g = pl.program_id(0)
    steps = pl.num_programs(0)
    n_key, lanes = k_ref.shape[1:]
    rows = o_ref.shape[1]
    n_ch = kbuf.shape[2]
    over = most_ref[0] > 2 * cap
    core = who_ref[2]

    def fetches(step, i, src_of):
        return [pltpu.make_async_copy(src_of(pl.ds(a * n_ch, n_ch)), buf.at[step % 2, i], sem.at[a, step % 2, i])
                for a, buf in enumerate((kbuf, vbuf))]

    def start(step):
        @pl.loop(0, blk)
        def _(i):
            s = step * blk + i
            n = info_ref[s]
            has = n >= 0
            half = jnp.where(n >= cap, 1, 0)
            pos = n - half * cap

            def go(cond, src_of):
                @pl.when(has & cond)
                def _():
                    for c in fetches(step, i, src_of):
                        c.start()

            go(over, lambda part: slow_ref.at[layer, s, part])
            go(jnp.logical_not(over) & (half == core), lambda part: own_ref.at[part, pos])
            go(jnp.logical_not(over) & (half != core), lambda part: mate_ref.at[part, pos])

    @pl.when(g == 0)
    def _():
        o_ref[...] = jnp.zeros_like(o_ref)
        lane = lax.broadcasted_iota(jnp.int32, ml_ref.shape, 1)
        ml_ref[...] = jnp.where(lane < rows, NEG, 0.0)
        start(0)

    @pl.when(g + 1 < steps)
    def _():
        start(g + 1)

    tile = 16
    tile_row = lax.broadcasted_iota(jnp.int32, (tile, lanes), 0)
    lane = lax.broadcasted_iota(jnp.int32, (rows, n_key), 1)
    row = lax.broadcasted_iota(jnp.int32, (rows, n_key), 0)
    own_head = (lane & 1) == ((row >> 3) & 1)
    late = (lane >> 1) - (row >> 4)
    out_lane = lax.broadcasted_iota(jnp.int32, (rows, lanes), 1)
    out_row = lax.broadcasted_iota(jnp.int32, (rows, lanes), 0)

    @pl.loop(0, blk // group)
    def _(u):
        facts = []
        for t in range(group):
            i = u * group + t
            s = g * blk + i
            has = info_ref[s] >= 0
            b = info_ref[2 * n_slots + s]
            lim = info_ref[4 * n_slots + s]
            used = b >= 0
            b0 = jnp.maximum(b, 0)

            @pl.when(has)
            def _():
                for c in fetches(g, i, lambda part: own_ref.at[part, 0]):
                    c.wait()
                ko_ref[i] = kbuf[g % 2, i].reshape(n_key, lanes)
                vo_ref[i] = vbuf[g % 2, i].reshape(n_key, lanes)

            @pl.when(jnp.logical_not(has))
            def _():
                ko_ref[i] = k_ref[i]
                vo_ref[i] = v_ref[i]

            @pl.when(used & (lim < n_key // 2))
            def _():
                fresh = q_ref[b0, rows:].astype(F32)
                row0 = 2 * lim
                for c in (row0 // tile, jnp.minimum((row0 + 3) // tile, n_key // tile - 1)):
                    at = tile_row + c * tile - row0
                    part = pl.ds(pl.multiple_of(c * tile, tile), tile)
                    for a, ref in enumerate((ko_ref, vo_ref)):
                        x = ref[i, part].astype(F32)
                        for r in range(4):
                            x = jnp.where(at == r, fresh[4 * a + r:4 * a + r + 1], x)
                        ref[i, part] = x.astype(BF16)

            facts.append((i, used, b0, lim, info_ref[5 * n_slots + s]))
        done = []
        for i, used, b0, lim, again in facts:
            sc = lax.dot_general(q_ref[b0, :rows], ko_ref[i], (((1,), (1,)), ((), ())), preferred_element_type=F32) * scale
            sc = jnp.where(own_head & (late <= lim), sc, NEG)
            m = jnp.max(sc, axis=1, keepdims=True)
            p = jnp.exp(sc - m)
            l = jnp.sum(p, axis=1, keepdims=True)
            o = jnp.dot(p.astype(BF16), vo_ref[i], preferred_element_type=F32)
            done.append((used, b0, m, l, o, again))
        for used, b0, m, l, o, again in done:
            def put(m, l, o):
                o_ref[b0] = o
                ml = jnp.where(out_lane == out_row, m, 0.0) + jnp.where(out_lane == out_row + rows, l, 0.0)
                ml_ref[pl.ds(b0, 1)] = jnp.sum(ml, axis=0, keepdims=True)

            @pl.when(used & (again == 0))
            def _():
                put(m, l, o)

            @pl.when(used & (again > 0))
            def _():
                old = jnp.broadcast_to(ml_ref[pl.ds(b0, 1)], (rows, lanes))
                m1 = jnp.sum(jnp.where(out_lane == out_row, old, 0.0), axis=1, keepdims=True)
                l1 = jnp.sum(jnp.where(out_lane == out_row + rows, old, 0.0), axis=1, keepdims=True)
                mm = jnp.maximum(m, m1)
                w, w1 = jnp.exp(m - mm), jnp.exp(m1 - mm)
                put(mm, l * w + l1 * w1, o * w + o_ref[b0] * w1)


def combine_kernel(o_ref, ml_ref, out_ref):
    parts, seq_dev, rows, lanes = o_ref.shape
    heads = out_ref.shape[2]

    @pl.loop(0, seq_dev, unroll=6)
    def _(b):
        ml = ml_ref[:, pl.ds(b, 1)].reshape(parts, lanes)
        w = jnp.exp(ml - jnp.max(ml, axis=0, keepdims=True))
        l = pltpu.roll(ml, lanes - rows, 1)
        w = w / jnp.sum(w * l, axis=0, keepdims=True)
        wt = w.T
        acc = jnp.zeros((rows, lanes), F32)
        for s in range(parts):
            acc = acc + wt[:rows, s:s + 1] * o_ref[s, b]
        acc = acc.astype(BF16)
        out_ref[0, b] = acc[:heads]
        out_ref[1, b] = acc[heads:]


def blank_kernel(o_ref):
    pass


def sems(*shape):
    return pltpu.SemaphoreType.DMA(shape)


def comm(cid):
    return pltpu.CompilerParams(collective_id=cid, has_side_effects=True)


def solution(mesh):
    n_rows = mesh.shape['kv2']
    n_cols = mesh.shape['kv']
    n_dev = n_rows * n_cols
    dev_axes = ('rep', 'kv2', 'kv')
    seq_spec = P(None, dev_axes, None)
    pool_spec = P(dev_axes, None, None, None, None)
    table_spec = P(dev_axes, None)
    vec_spec = P(dev_axes)
    full_spec = P()

    def per_device(x_embed, w_query, w_key, w_value, w_out, w_up, w_down, k_pool, v_pool, old_table, seq_len, src_slot, dst_slot):
        n_slots, layers, page, kv_heads, head_dim = k_pool.shape
        heads = w_query.shape[2] // head_dim
        n_steps, seq_dev, width = x_embed.shape
        n_moves = src_slot.shape[0]
        row_seqs = seq_dev * n_cols
        rows = n_steps * heads
        key_rows = page * kv_heads
        tile = 8
        n_ch = key_rows // tile
        chunks = 2 * n_ch
        cap = 20
        blk, group = 28, 7
        assert chunks == n_dev and rows == 32 and n_slots % blk == 0 and old_table.shape[1] == 2
        shift = 18
        magic = -(-(1 << shift) // n_slots)
        assert all((s * magic) >> shift == s // n_slots for s in range(n_dev * n_slots))
        me = flat_id(n_cols)
        who = jnp.stack([me, lax.axis_index('kv2') * n_cols, lax.axis_index('kv') % 2]).astype(jnp.int32)

        kp = k_pool.reshape(n_slots, layers, n_ch, tile, head_dim)
        vp = v_pool.reshape(n_slots, layers, n_ch, tile, head_dim)
        packed = pl.pallas_call(
            functools.partial(pack_kernel, n_moves),
            out_shape=[jax.ShapeDtypeStruct((chunks, n_moves, tile, head_dim), BF16)] * layers,
            in_specs=[SMEM, ANY, ANY], out_specs=[VMEM] * layers,
            scratch_shapes=[sems(layers, 2, n_moves)], name='pack_pages')(src_slot - me * n_slots, kp, vp)
        after = lax.optimization_barrier
        spread0 = lax.all_to_all(packed[0], ('kv2', 'kv'), 0, 0, tiled=True)

        mine = jnp.concatenate([old_table.reshape(-1), seq_len, src_slot, dst_slot])
        mine = jnp.pad(mine, (0, 128 - mine.shape[0])).reshape(1, 128)
        tab = pl.pallas_call(
            functools.partial(gather_all_kernel, n_dev, n_cols),
            out_shape=jax.ShapeDtypeStruct((n_dev, 1, 128), jnp.int32),
            in_specs=[VMEM], out_specs=VMEM,
            scratch_shapes=[pltpu.SemaphoreType.DMA, sems(n_dev), sems(n_dev)],
            compiler_params=comm(0), name='gather_tables')(mine)

        dims = (n_dev, n_cols, n_slots, seq_dev, n_moves, cap, page, magic, shift)
        pages, info, most = pl.pallas_call(
            functools.partial(plan_kernel, dims),
            out_shape=(jax.ShapeDtypeStruct((n_dev * cap,), jnp.int32), jax.ShapeDtypeStruct((6 * n_slots,), jnp.int32),
                       jax.ShapeDtypeStruct((1,), jnp.int32)),
            in_specs=[SMEM, SMEM, ANY], out_specs=(SMEM, SMEM, SMEM),
            scratch_shapes=[pltpu.SMEM((n_dev * n_slots,), jnp.int32), pltpu.SMEM((n_dev // 2,), jnp.int32),
                            pltpu.SMEM((row_seqs,), jnp.int32), pltpu.SemaphoreType.DMA],
            name='plan')(who, tab.reshape(n_dev, 128), jnp.full((n_dev * n_slots,), -1, jnp.int32))

        def regroup(spread, name):
            return pl.pallas_call(
                functools.partial(regroup_kernel, cap),
                out_shape=jax.ShapeDtypeStruct((n_dev, cap, tile, head_dim), BF16),
                in_specs=[SMEM, VMEM], out_specs=VMEM, name=name)(pages, spread.reshape(n_dev * n_moves, tile, head_dim))

        def deliver(grouped):
            return lax.all_to_all(grouped, ('kv2', 'kv'), 0, 0, tiled=True)

        def to_mate(own):
            return lax.ppermute(own, 'kv', [(i, i ^ 1) for i in range(n_cols)])

        def all_pages():
            found = []
            for p in packed:
                everything = lax.all_gather(p.swapaxes(0, 1), ('kv2', 'kv'), tiled=True)
                found.append(everything[jnp.maximum(info[n_slots:2 * n_slots], 0)])
            return jnp.stack(found)

        def no_pages():
            return pl.pallas_call(
                blank_kernel, out_shape=jax.ShapeDtypeStruct((layers, n_slots, chunks, tile, head_dim), BF16), out_specs=ANY,
                name='blank')()

        slow = lax.cond(most[0] > 2 * cap, all_pages, no_pages)

        k_rows = k_pool.reshape(n_slots, layers * key_rows, head_dim)
        v_rows = v_pool.reshape(n_slots, layers * key_rows, head_dim)
        hidden = x_embed.reshape(n_steps * seq_dev, width)
        k_out = v_out = None
        grouped, hidden = after((regroup(spread0, 'regroup_pages_0'), hidden))
        own = deliver(grouped)
        pool_shape = jax.ShapeDtypeStruct(k_rows.shape, BF16)
        for layer in range(layers):
            query = jnp.dot(hidden, w_query[layer], preferred_element_type=F32).astype(BF16)
            k_new = jnp.dot(hidden, w_key[layer], preferred_element_type=F32).astype(BF16)
            v_new = jnp.dot(hidden, w_value[layer], preferred_element_type=F32).astype(BF16)

            def by_seq(x):
                return x.reshape(n_steps, seq_dev, -1, head_dim).swapaxes(0, 1).reshape(seq_dev, -1, head_dim)

            load = jnp.concatenate([by_seq(query), by_seq(k_new), by_seq(v_new)], axis=1)
            q_rows = load.shape[1]
            own, load = after((own, load))
            mate = to_mate(own)
            n_chips = n_cols // 2
            q_row = pl.pallas_call(
                functools.partial(row_gather_kernel, n_cols),
                out_shape=jax.ShapeDtypeStruct((n_cols, seq_dev, q_rows, head_dim), BF16),
                in_specs=[VMEM], out_specs=VMEM,
                scratch_shapes=[pltpu.SemaphoreType.DMA, sems(n_chips), sems(n_chips), sems(n_chips), sems(n_chips)],
                compiler_params=comm(3 + layer), name=f'gather_queries_{layer}')(load)

            first = layer == 0
            last = layer == layers - 1
            if not last:
                moving, q_row = after((packed[layer + 1], q_row))
                spread = lax.all_to_all(moving, ('kv2', 'kv'), 0, 0, tiled=True)
            dims = (layer, n_slots, blk, group, cap, head_dim ** -0.5, first)
            pool_block = pl.BlockSpec((blk, key_rows, head_dim), lambda g, *_, at=layer: (g, at, 0))
            whole = lambda shape: pl.BlockSpec(shape, lambda g, *_: (0,) * len(shape))
            carried = () if first else (k_out, v_out)
            k_out, v_out, part, ml = pl.pallas_call(
                functools.partial(attend_kernel, dims),
                grid_spec=pltpu.PrefetchScalarGridSpec(
                    num_scalar_prefetch=3, grid=(n_slots // blk,),
                    in_specs=[whole((row_seqs, q_rows, head_dim)), pool_block, pool_block, ANY, ANY, ANY] + [ANY] * len(carried),
                    out_specs=[pool_block, pool_block, whole((row_seqs, rows, head_dim)), whole((row_seqs, head_dim))],
                    scratch_shapes=[pltpu.VMEM((2, blk, n_ch, tile, head_dim), BF16), pltpu.VMEM((2, blk, n_ch, tile, head_dim), BF16),
                                    sems(2, 2, blk)]),
                out_shape=[pool_shape, pool_shape, jax.ShapeDtypeStruct((row_seqs, rows, head_dim), F32),
                           jax.ShapeDtypeStruct((row_seqs, head_dim), F32)],
                input_output_aliases={} if first else {9: 0, 10: 1},
                compiler_params=pltpu.CompilerParams(dimension_semantics=('arbitrary',)),
                name=f'attend_{layer}')(info, most, who, q_row.reshape(row_seqs, q_rows, head_dim), k_rows, v_rows, own, mate, slow, *carried)

            home, home_ml = pl.pallas_call(
                functools.partial(row_exchange_kernel, n_cols),
                out_shape=(jax.ShapeDtypeStruct((n_cols, seq_dev, rows, head_dim), F32),
                           jax.ShapeDtypeStruct((n_cols, seq_dev, head_dim), F32)),
                in_specs=[ANY, ANY], out_specs=(ANY, ANY),
                scratch_shapes=[sems(2), sems(2, n_cols), sems(2, n_cols)],
                compiler_params=comm(5 + layer), name=f'return_parts_{layer}')(
                    part.reshape(n_cols, seq_dev, rows, head_dim), ml.reshape(n_cols, seq_dev, head_dim))
            attn = pl.pallas_call(
                combine_kernel,
                out_shape=jax.ShapeDtypeStruct((n_steps, seq_dev, heads, head_dim), BF16),
                in_specs=[VMEM, VMEM], out_specs=VMEM, name=f'combine_{layer}')(home, home_ml)
            attn_out = attn.reshape(n_steps * seq_dev, heads * head_dim)
            hidden = (hidden.astype(F32) + jnp.dot(attn_out, w_out[layer], preferred_element_type=F32)).astype(BF16)
            if not last:
                spread, hidden = after((spread, hidden))
                grouped, hidden = after((regroup(spread, f'regroup_pages_{layer + 1}'), hidden))
                own = deliver(grouped)
            up_act = jax.nn.gelu(jnp.dot(hidden, w_up[layer], preferred_element_type=F32)).astype(BF16)
            hidden = (hidden.astype(F32) + jnp.dot(up_act, w_down[layer], preferred_element_type=F32)).astype(BF16)
        return hidden.reshape(x_embed.shape), k_out.reshape(k_pool.shape), v_out.reshape(v_pool.shape)

    return jax.shard_map(per_device, mesh=mesh, in_specs=(seq_spec, full_spec, full_spec, full_spec, full_spec, full_spec, full_spec, pool_spec, pool_spec, table_spec, vec_spec, vec_spec, vec_spec), out_specs=(seq_spec, pool_spec, pool_spec), check_vma=False)
```

time: 1570 us -> 418 us (0.27); the launches traced: 1550 us -> 417 us
  local copies, waits for them, and re-layouts: 794 us -> 4.59 us
  blocking collectives: 306 us -> 0 us
  Pallas kernels: 0 us -> 266 us
  other arithmetic: 138 us -> 3.31 us
  matrix products: 193 us -> 93.4 us
  starting transfers between devices: 85.5 us -> 22.2 us
    scatter x12 -> x0, local copies, waits for them, and re-layouts: 543 us -> none  [the longest x1 168 us: per_device(): k_pool = k_pool.at[dst_local].set(in_pages[:, 0], mode='drop')]
    pallas_call x0 -> x14, Pallas kernels: none -> 266 us  [the longest x2 85.5 us: per_device(): pl.pallas_call(functools.partial(row_exchange_kernel, n_cols), out_shape=...]
    all_gather x9 -> x0, blocking collectives: 246 us -> none  [the longest x4 142 us: per_device(): q_row = lax.all_gather(query, 'kv', tiled=True)]
    dot_general x28 -> x12, matrix products: 193 us -> 93.4 us  [the longest x2 34.5 us: per_device(): jnp.dot(up_act, w_down[layer], preferred_element_type=F32)]
    squeeze x9 -> x0, local copies, waits for them, and re-layouts: 85.3 us -> none  [the longest x1 83.3 us: per_device(): k_pool = k_pool.at[dst_local].set(in_pages[:, 0], mode='drop')]
    slice x16 -> x0, local copies, waits for them, and re-layouts: 84.6 us -> none  [the longest x4 41 us: per_device(): v_pool[:, layer_idx]]
    all_to_all x4, starting transfers between devices: 85.4 us -> 21.3 us  [the longest x1 9.18 us: per_device(): spread0 = lax.all_to_all(packed[0], ('kv2', 'kv'), 0, 0, tiled=True)]
    scatter-add x8 -> x0, other arithmetic: 63.1 us -> none  [the longest x4 41.3 us: per_device(): jax.ops.segment_sum(slot_w[..., None] * slot_out, seg_ids, num_segments=r...]
  transfers between devices with their start and end apart: 5 -> 6, of which waited for: 1 -> 1; matrix products, arithmetic and copies ran while one was open for 12% -> 14% of each run, Pallas kernels for 0% -> 40%
where the time goes in v1:
time: 418 us; the launch traced here: 417 us
  Pallas kernels  266 us (64%)
  matrix products  93.4 us (22%)
  starting transfers between devices  22.2 us (5%)
  between operations  15.2 us (4%)
  waiting for transfers between devices  12.4 us (3%)
  local copies, waits for them, and re-layouts  4.59 us (1%)
    pallas_call x2, Pallas kernels, per_device(): pl.pallas_call(functools.partial(row_exchange_kernel, n_cols), out_shape=...  85.5 us
    pallas_call x2, Pallas kernels, per_device(): pl.pallas_call(functools.partial(attend_kernel, dims), grid_spec=pltpu.Pr...  83 us
    pallas_call x2, Pallas kernels, per_device(): pl.pallas_call(functools.partial(row_gather_kernel, n_cols), out_shape=ja...  38.8 us
    dot_general x2, matrix products, per_device(): jnp.dot(up_act, w_down[layer], preferred_element_type=F32)  34.5 us
    dot_general x2, matrix products, per_device(): jnp.dot(hidden, w_up[layer], preferred_element_type=F32)  33.8 us
    pallas_call x1, Pallas kernels, per_device(): pl.pallas_call(functools.partial(gather_all_kernel, n_dev, n_cols), out_s...  18.6 us
    pallas_call x1, Pallas kernels, per_device(): pl.pallas_call(functools.partial(plan_kernel, dims), out_shape=(jax.Shape...  16.7 us
    pallas_call x2, Pallas kernels, per_device(): pl.pallas_call(combine_kernel, out_shape=jax.ShapeDtypeStruct((n_steps, s...  13.1 us
  transfers between devices with their start and end apart: 6, of which 1 were waited for; matrix products, arithmetic and copies ran while one was open for 14% of the time, Pallas kernels for 40%

profile of v1, /device:TPU:97, one launch (start us, length us, event | category | flops | bytes accessed | tf_op | source)
XLA Modules:
  0.0 417.3 jit_solution(7484870846451003092)
XLA Ops:
  7.2 1.2 broadcast_subtract_fusion.src_ref
  8.4 4.2 %pack_pages.1 = (bf16[32,16,8,128]{3,2,1,0:T(8,128)(2,1)}, bf16[32,16,8,128]{3,2,1,0:T(8,128)(2,1)}) custom-call(s32[16]{0:T(128)} %broadcast_subtract_fusion.src_ref, bf16[112,2,16,8,128]{4,3,2,1,0:T(8,128)(2,1)} %bitcast.141, bf16[112,2,16,8,128]{4,3,2,1,0:T(8,128)(2,1)} %bitcast.144), custom_call_target="tpu_custom_call" | custom-call | tf_op jit(solution)/shard_map/pack_pages/pallas_call | solution.py:422
  12.6 9.2 %all-to-all-start = ((bf16[32,16,8,128]{3,2,1,0:T(8,128)(2,1)}), bf16[32,16,8,128]{3,2,1,0:T(8,128)(2,1)S(1)}, u32[]{:S(2)}, u32[]{:S(2)}) async-start(bf16[32,16,8,128]{3,2,1,0:T(8,128)(2,1)} %get-tuple-element.46), calls=%async_computation | async-start | bytes 2097152 | tf_op jit(solution)/shard_map/all_to_all | solution.py:428
  22.6 18.6 %gather_tables.1 = s32[32,1,128]{2,1,0:T(1,128)} custom-call(s32[1,128]{1,0:T(1,128)} %pad_bitcast_fusion.x_ref), custom_call_target="tpu_custom_call" | custom-call | tf_op jit(solution)/shard_map/gather_tables/pallas_call | solution.py:432
  42.4 16.7 %plan.1 = (s32[640]{0:T(1024)}, s32[672]{0:T(1024)S(1)}, s32[1]{0:T(128)}) custom-call(s32[3]{0:T(128)} %pad_add_fusion.who_ref, s32[32,128]{1,0:T(8,128)} %bitcast.169, s32[3584]{0:T(1024)} %broadcast_in_dim.7.none_ref), custom_call_target="tpu_custom_call" | custom-call | tf_op jit(solution)/shard_map/plan/pallas_call | solution.py:440
  60.2 3.1 regroup_pages_0.1
  63.2 3.7 all-to-all-start.1
  66.9 5.0 %fusion.81 = bf16[6,8,16,128]{3,1,2,0:T(8,128)(2,1)S(1)} fusion(bf16[48,2048]{1,0:T(8,128)(2,1)S(1)} %bitcast.170, bf16[2,2048,2048]{2,1,0:T(8,128)(2,1)} %param.16), kind=kOutput, calls=%fused_computation.58 | convolution fusion | flops 402751488 | bytes 8781824 | tf_op jit(solution)/shard_map/dot_general | solution.py:483
  71.9 1.5 convolution_convert_fusion.3
  73.5 1.5 convolution_convert_fusion.2
  75.8 12.4 %all-to-all-done.1.own_ref = bf16[32,20,8,128]{3,2,1,0:T(8,128)(2,1)S(1)} async-done(((bf16[32,20,8,128]{3,2,1,0:T(8,128)(2,1)}), bf16[32,20,8,128]{3,2,1,0:T(8,128)(2,1)S(1)}, u32[]{:S(2)}, u32[]{:S(2)}) %all-to-all-start.1) | async-done | bytes 1310752 | tf_op jit(solution)/shard_map/all_to_all | solution.py:456
  88.2 19.4 %gather_queries_0.1 = bf16[8,24,40,128]{3,2,1,0:T(8,128)(2,1)} custom-call(bf16[24,40,128]{2,1,0:T(8,128)(2,1)} %pad_maximum_fusion.1.x_ref), custom_call_target="tpu_custom_call" | custom-call | tf_op jit(solution)/shard_map/gather_queries_0/pallas_call | solution.py:495
  107.6 3.0 all-to-all-start.2
  111.3 41.6 %attend_0.1 = (bf16[112,256,128]{2,1,0:T(8,128)(2,1)}, bf16[112,256,128]{2,1,0:T(8,128)(2,1)}, f32[192,32,128]{2,1,0:T(8,128)}, f32[192,128]{1,0:T(8,128)}) custom-call(s32[672]{0:T(1024)S(1)} %get-tuple-element.51.info_ref, s32[1]{0:T(128)} %get-tuple-element.52.most_ref, s32[3]{0:T(128)} %pad_add_fusion.who_ref, bf16[192,40,128]{2,1,0:T(8,128)(2,1)} %bitcast.150, ...), custom_call_target="tpu_custom_call" | custom-call | tf_op jit(solution)/shard_map/attend_0/pallas_call | solution.py:511
  152.9 43.4 %return_parts_0.1 = (f32[8,24,32,128]{3,2,1,0:T(8,128)}, f32[8,24,128]{2,1,0:T(8,128)}) custom-call(f32[8,24,32,128]{3,2,1,0:T(8,128)} %bitcast.156, f32[8,24,128]{2,1,0:T(8,128)} %bitcast.164), custom_call_target="tpu_custom_call" | custom-call | tf_op jit(solution)/shard_map/return_parts_0/pallas_call | solution.py:525
  196.3 6.6 %combine_0.1 = bf16[2,24,16,128]{3,2,1,0:T(8,128)(2,1)} custom-call(f32[8,24,32,128]{3,2,1,0:T(8,128)} %get-tuple-element.57.o_ref, f32[8,24,128]{2,1,0:T(8,128)} %get-tuple-element.58.ml_ref), custom_call_target="tpu_custom_call" | custom-call | tf_op jit(solution)/shard_map/combine_0/pallas_call | solution.py:533
  202.8 5.1 %fusion.51 = bf16[48,2048]{1,0:T(8,128)(2,1)S(1)} fusion(bf16[2,2048,2048]{2,1,0:T(8,128)(2,1)} %param.19, bf16[48,2048]{1,0:T(8,128)(2,1)S(1)} %bitcast.173, bf16[6,8,16,128]{3,2,1,0:T(8,128)(2,1)} %bitcast.162), kind=kOutput, calls=%fused_computation.40 | convolution fusion | flops 402948096 | bytes 8978432 | tf_op jit(solution)/shard_map/dot_general | solution.py:538
  207.9 1.0 copy-done.2
  208.9 3.1 regroup_pages_1.1
  212.0 5.5 %all-to-all-start.3 = ((bf16[32,20,8,128]{3,2,1,0:T(8,128)(2,1)}), bf16[32,20,8,128]{3,2,1,0:T(8,128)(2,1)S(1)}, u32[]{:S(2)}, u32[]{:S(2)}) async-start(bf16[32,20,8,128]{3,2,1,0:T(8,128)(2,1)} %regroup_pages_1.1), calls=%async_computation.3 | async-start | bytes 2621440 | tf_op jit(solution)/shard_map/all_to_all | solution.py:456
  217.5 16.8 %fusion.63 = bf16[48,11008]{1,0:T(8,128)(2,1)S(1)} fusion(bf16[48,2048]{1,0:T(8,128)(2,1)S(1)} %fusion.51, bf16[2,2048,11008]{2,1,0:T(8,128)(2,1)} %param.20), kind=kOutput, calls=%fused_computation.48 | convolution fusion | flops 2169016320 | bytes 46342144 | tf_op jit(solution)/shard_map/dot_general | solution.py:543
  234.3 16.9 %fusion.39 = bf16[48,2048]{1,0:T(8,128)(2,1)S(1)} fusion(bf16[48,11008]{1,0:T(8,128)(2,1)S(1)} %fusion.63, bf16[2,11008,2048]{2,1,0:T(8,128)(2,1)} %param.21, bf16[48,2048]{1,0:T(8,128)(2,1)S(1)} %fusion.51), kind=kOutput, calls=%fused_computation.36 | convolution fusion | flops 2164555776 | bytes 46538752 | tf_op jit(solution)/shard_map/dot_general | solution.py:544
  251.3 5.1 %fusion.78 = bf16[6,8,16,128]{3,1,2,0:T(8,128)(2,1)S(1)} fusion(bf16[48,2048]{1,0:T(8,128)(2,1)S(1)} %fusion.39, bf16[2,2048,2048]{2,1,0:T(8,128)(2,1)} %param.16), kind=kOutput, calls=%fused_computation.57 | convolution fusion | flops 402751488 | bytes 8781824 | tf_op jit(solution)/shard_map/dot_general | solution.py:483
  256.8 1.5 convolution_convert_fusion
  260.0 19.4 %gather_queries_1.1 = bf16[8,24,40,128]{3,2,1,0:T(8,128)(2,1)} custom-call(bf16[24,40,128]{2,1,0:T(8,128)(2,1)} %pad_maximum_fusion.2.x_ref), custom_call_target="tpu_custom_call" | custom-call | tf_op jit(solution)/shard_map/gather_queries_1/pallas_call | solution.py:495
  279.5 1.1 copy-done.4
  280.6 41.5 %attend_1.1 = (bf16[112,256,128]{2,1,0:T(8,128)(2,1)}, bf16[112,256,128]{2,1,0:T(8,128)(2,1)}, f32[192,32,128]{2,1,0:T(8,128)}, f32[192,128]{1,0:T(8,128)}) custom-call(s32[672]{0:T(1024)S(1)} %get-tuple-element.51.info_ref, s32[1]{0:T(128)} %get-tuple-element.52.most_ref, s32[3]{0:T(128)} %pad_add_fusion.who_ref, ...), custom_call_target="tpu_custom_call", output_to_operand_aliasing={{0}: (9, {}), {1}: (10, {})} | custom-call | tf_op jit(solution)/shard_map/attend_1/pallas_call | solution.py:511
  322.1 42.1 %return_parts_1.1 = (f32[8,24,32,128]{3,2,1,0:T(8,128)}, f32[8,24,128]{2,1,0:T(8,128)}) custom-call(f32[8,24,32,128]{3,2,1,0:T(8,128)} %bitcast.155, f32[8,24,128]{2,1,0:T(8,128)} %bitcast.163), custom_call_target="tpu_custom_call" | custom-call | tf_op jit(solution)/shard_map/return_parts_1/pallas_call | solution.py:525
  364.2 6.6 %combine_1.1 = bf16[2,24,16,128]{3,2,1,0:T(8,128)(2,1)} custom-call(f32[8,24,32,128]{3,2,1,0:T(8,128)} %get-tuple-element.69.o_ref, f32[8,24,128]{2,1,0:T(8,128)} %get-tuple-element.70.ml_ref), custom_call_target="tpu_custom_call" | custom-call | tf_op jit(solution)/shard_map/combine_1/pallas_call | solution.py:533
  370.8 5.1 %fusion.48 = bf16[48,2048]{1,0:T(8,128)(2,1)S(1)} fusion(bf16[2,2048,2048]{2,1,0:T(8,128)(2,1)} %param.19, bf16[48,2048]{1,0:T(8,128)(2,1)S(1)} %fusion.39, bf16[6,8,16,128]{3,2,1,0:T(8,128)(2,1)} %bitcast.161), kind=kOutput, calls=%fused_computation.39 | convolution fusion | flops 402948096 | bytes 8978432 | tf_op jit(solution)/shard_map/dot_general | solution.py:538
  375.9 17.0 %fusion.75 = bf16[48,11008]{1,0:T(8,128)(2,1)S(1)} fusion(bf16[48,2048]{1,0:T(8,128)(2,1)S(1)} %fusion.48, bf16[2,2048,11008]{2,1,0:T(8,128)(2,1)} %param.20), kind=kOutput, calls=%fused_computation.56 | convolution fusion | flops 2169016320 | bytes 46342144 | tf_op jit(solution)/shard_map/dot_general | solution.py:543
  392.9 17.6 %fusion.36 = bf16[48,2048]{1,0:T(8,128)(2,1)} fusion(bf16[48,11008]{1,0:T(8,128)(2,1)S(1)} %fusion.75, bf16[2,11008,2048]{2,1,0:T(8,128)(2,1)} %param.21, bf16[48,2048]{1,0:T(8,128)(2,1)S(1)} %fusion.48), kind=kOutput, calls=%fused_computation.35 | convolution fusion | flops 2164555776 | bytes 46538752 | tf_op jit(solution)/shard_map/dot_general | solution.py:544
  (50 shorter events, 5.9 us)
Async XLA Ops:
  8.4 13.4 %copy-start.5 = (s32[24,2]{0,1:T(2,128)S(1)}, s32[24,2]{0,1:T(2,128)}, u32[]{:S(2)}) copy-start(s32[24,2]{0,1:T(2,128)} %param.24) | copy-start | bytes 580
  8.4 13.6 %copy-start.6 = (s32[16]{0:T(128)S(1)}, s32[16]{0:T(128)}, u32[]{:S(2)}) copy-start(s32[16]{0:T(128)} %param.27) | copy-start | bytes 196
  8.4 13.6 %copy-start.7 = (s32[16]{0:T(128)S(1)}, s32[16]{0:T(128)}, u32[]{:S(2)}) copy-start(s32[16]{0:T(128)} %param.26) | copy-start | bytes 196
  8.4 13.6 %copy-start.8 = (s32[24]{0:T(128)S(1)}, s32[24]{0:T(128)}, u32[]{:S(2)}) copy-start(s32[24]{0:T(128)} %param.25) | copy-start | bytes 292
  8.4 58.5 %copy-start.10 = (bf16[2,24,2048]{2,1,0:T(8,128)(2,1)S(1)}, bf16[2,24,2048]{2,1,0:T(8,128)(2,1)}, u32[]{:S(2)}) copy-start(bf16[2,24,2048]{2,1,0:T(8,128)(2,1)} %param.15) | copy-start | bytes 589828
  12.6 46.6 %all-to-all-start = ((bf16[32,16,8,128]{3,2,1,0:T(8,128)(2,1)}), bf16[32,16,8,128]{3,2,1,0:T(8,128)(2,1)S(1)}, u32[]{:S(2)}, u32[]{:S(2)}) async-start(bf16[32,16,8,128]{3,2,1,0:T(8,128)(2,1)} %get-tuple-element.46), calls=%async_computation | async-start | bytes 2097152 | tf_op jit(solution)/shard_map/all_to_all | solution.py:428
  59.2 1.0 copy-start.3
  63.2 25.0 %all-to-all-start.1 = ((bf16[32,20,8,128]{3,2,1,0:T(8,128)(2,1)}), bf16[32,20,8,128]{3,2,1,0:T(8,128)(2,1)S(1)}, u32[]{:S(2)}, u32[]{:S(2)}) async-start(bf16[32,20,8,128]{3,2,1,0:T(8,128)(2,1)} %regroup_pages_0.1), calls=%async_computation.1 | async-start | bytes 2621440 | tf_op jit(solution)/shard_map/all_to_all | solution.py:456
  88.2 23.1 %copy-start.1 = (bf16[32,20,8,128]{3,2,1,0:T(8,128)(2,1)}, bf16[32,20,8,128]{3,2,1,0:T(8,128)(2,1)S(1)}, u32[]{:S(2)}) copy-start(bf16[32,20,8,128]{3,2,1,0:T(8,128)(2,1)S(1)} %all-to-all-done.1.own_ref) | copy-start | bytes 3932164
  88.2 23.1 %collective-permute-start = (bf16[32,20,8,128]{3,2,1,0:T(8,128)(2,1)S(1)}, bf16[32,20,8,128]{3,2,1,0:T(8,128)(2,1)}, u32[]{:S(2)}, u32[]{:S(2)}) collective-permute-start(bf16[32,20,8,128]{3,2,1,0:T(8,128)(2,1)S(1)} %all-to-all-done.1.own_ref), channel_id=1, source_target_pairs={{0,1},{1,0},{2,3},{3,2},{4,5},{5,4},{6,7},{7,6},{8,9},{9,8},{10,11... | collective-permute-start | bytes 3932168 | tf_op jit(solution)/shard_map/ppermute | solution.py:459
  107.6 100.3 %all-to-all-start.2 = ((bf16[32,16,8,128]{3,2,1,0:T(8,128)(2,1)}), bf16[32,16,8,128]{3,2,1,0:T(8,128)(2,1)S(1)}, u32[]{:S(2)}, u32[]{:S(2)}) async-start(bf16[32,16,8,128]{3,2,1,0:T(8,128)(2,1)} %get-tuple-element.50), calls=%async_computation.2 | async-start | bytes 2097152 | tf_op jit(solution)/shard_map/all_to_all | solution.py:506
  207.9 1.0 copy-start.2
  212.0 47.1 %all-to-all-start.3 = ((bf16[32,20,8,128]{3,2,1,0:T(8,128)(2,1)}), bf16[32,20,8,128]{3,2,1,0:T(8,128)(2,1)S(1)}, u32[]{:S(2)}, u32[]{:S(2)}) async-start(bf16[32,20,8,128]{3,2,1,0:T(8,128)(2,1)} %regroup_pages_1.1), calls=%async_computation.3 | async-start | bytes 2621440 | tf_op jit(solution)/shard_map/all_to_all | solution.py:456
  251.3 5.2 %copy-start.9 = (bf16[2,2048,256]{2,1,0:T(8,128)(2,1)S(1)}, bf16[2,2048,256]{2,1,0:T(8,128)(2,1)}, u32[]{:S(2)}) copy-start(bf16[2,2048,256]{2,1,0:T(8,128)(2,1)} %param.17) | copy-start | bytes 6291460
  259.1 20.3 %copy-start = (bf16[32,20,8,128]{3,2,1,0:T(8,128)(2,1)}, bf16[32,20,8,128]{3,2,1,0:T(8,128)(2,1)S(1)}, u32[]{:S(2)}) copy-start(bf16[32,20,8,128]{3,2,1,0:T(8,128)(2,1)S(1)} %all-to-all-done.3.own_ref) | copy-start | bytes 3932164
  259.1 20.3 %collective-permute-start.1 = (bf16[32,20,8,128]{3,2,1,0:T(8,128)(2,1)S(1)}, bf16[32,20,8,128]{3,2,1,0:T(8,128)(2,1)S(1)}, u32[]{:S(2)}, u32[]{:S(2)}) collective-permute-start(bf16[32,20,8,128]{3,2,1,0:T(8,128)(2,1)S(1)} %all-to-all-done.3.own_ref), channel_id=1, source_target_pairs={{0,1},{1,0},{2,3},{3,2},{4,5},{5,4},{6,7},{7,6},{8,9},{9,8},{10,11... | collective-permute-start | bytes 3932168 | tf_op jit(solution)/shard_map/ppermute | solution.py:459
  279.5 1.1 copy-start.4

commit v2 on v1

--- a/solution.py
+++ b/solution.py
@@ -127,42 +127,31 @@
             c.wait_recv()
 
 
-def plan_kernel(dims, who_ref, tab_ref, none_ref, pages_ref, info_ref, most_ref, moved, count, seen, sem):
+def places_kernel(dims, who_ref, tab_ref, pages_ref, arrive_ref, most_ref, count):
     n_dev, n_cols, n_slots, seq_dev, n_moves, cap, page, magic, shift = dims
     n_chips = n_dev // 2
-    o_len, o_src, o_dst = 2 * seq_dev, 3 * seq_dev, 3 * seq_dev + n_moves
+    o_dst = 3 * seq_dev + n_moves
     me = who_ref[0]
-    row0 = who_ref[1]
     base = me * n_slots
-    fill = pltpu.make_async_copy(none_ref, moved, sem)
-    fill.start()
 
     @pl.loop(0, n_chips)
     def _(i):
         count[i] = 0
 
-    @pl.loop(0, n_cols * seq_dev)
+    @pl.loop(0, n_slots, unroll=8)
     def _(i):
-        seen[i] = 0
-
-    @pl.loop(0, n_slots)
-    def _(i):
-        for f in range(4):
-            info_ref[f * n_slots + i] = -1
-
-    @pl.loop(0, n_dev * cap)
+        arrive_ref[i] = -1
+        arrive_ref[n_slots + i] = -1
+
+    @pl.loop(0, n_dev * cap, unroll=8)
     def _(i):
         pages_ref[i] = 0
-
-    fill.wait()
 
     @pl.loop(0, n_dev)
     def _(d):
         for j in range(n_moves):
-            src = tab_ref[d, o_src + j]
             dst = tab_ref[d, o_dst + j]
             m = d * n_moves + j
-            moved[src] = dst
             dd = (dst * magic) >> shift
             chip = dd >> 1
             n = count[chip]
@@ -174,17 +163,39 @@
 
             @pl.when(dd == me)
             def _():
-                info_ref[dst - base] = n
-                info_ref[n_slots + dst - base] = m
-
-    def biggest(i, best):
-        return jnp.maximum(best, count[i])
-
-    most_ref[0] = lax.fori_loop(0, n_chips, biggest, jnp.int32(0))
+                arrive_ref[dst - base] = n
+                arrive_ref[n_slots + dst - base] = m
+
+    most_ref[0] = lax.fori_loop(0, n_chips, lambda i, best: jnp.maximum(best, count[i]), jnp.int32(0))
+
+
+def cells_kernel(dims, who_ref, tab_ref, none_ref, info_ref, used_ref, moved, seen, sem):
+    n_dev, n_cols, n_slots, seq_dev, n_moves, cap, page, magic, shift = dims
+    o_len, o_src, o_dst = 2 * seq_dev, 3 * seq_dev, 3 * seq_dev + n_moves
+    row0 = who_ref[1]
+    base = who_ref[0] * n_slots
+    fill = pltpu.make_async_copy(none_ref, moved, sem)
+    fill.start()
+
+    @pl.loop(0, n_cols * seq_dev, unroll=8)
+    def _(i):
+        seen[i] = 0
+
+    @pl.loop(0, n_slots, unroll=8)
+    def _(i):
+        info_ref[i] = -1
+        info_ref[n_slots + i] = -1
+
+    fill.wait()
+
+    @pl.loop(0, n_dev)
+    def _(d):
+        for j in range(n_moves):
+            moved[tab_ref[d, o_src + j]] = tab_ref[d, o_dst + j]
 
     @pl.loop(0, n_cols)
     def _(h):
-        @pl.loop(0, seq_dev)
+        @pl.loop(0, seq_dev, unroll=4)
         def _(i):
             b = h * seq_dev + i
             length = tab_ref[row0 + h, o_len + i]
@@ -196,17 +207,21 @@
 
                 @pl.when((e >= 0) & (s >= 0) & (s < n_slots))
                 def _():
-                    info_ref[2 * n_slots + s] = b
-                    info_ref[4 * n_slots + s] = length - page * j
-
-    @pl.loop(0, n_slots)
-    def _(s):
-        b = info_ref[2 * n_slots + s]
+                    info_ref[n_slots + s] = b
+                    info_ref[2 * n_slots + s] = length - page * j
+
+    def visit(s, n):
+        b = info_ref[n_slots + s]
 
         @pl.when(b >= 0)
         def _():
-            info_ref[5 * n_slots + s] = seen[b]
+            info_ref[n] = s
+            info_ref[3 * n_slots + s] = seen[b]
             seen[b] = 1
+
+        return n + jnp.where(b >= 0, 1, 0)
+
+    used_ref[0] = lax.fori_loop(0, n_slots, visit, jnp.int32(0))
 
 
 def pack_kernel(n_moves, src_ref, k_ref, v_ref, *rest):
@@ -234,107 +249,101 @@
             o_ref[d, n] = x_ref[pages_ref[d * cap + n]]
 
 
-def attend_kernel(dims, info_ref, most_ref, who_ref, q_ref, k_ref, v_ref, own_ref, mate_ref, slow_ref, *rest):
-    layer, n_slots, blk, group, cap, scale, first = dims
-    ko_ref, vo_ref, o_ref, ml_ref, kbuf, vbuf, sem = rest if first else rest[2:]
-    g = pl.program_id(0)
-    steps = pl.num_programs(0)
-    n_key, lanes = k_ref.shape[1:]
+def attend_kernel(dims, who_ref, arrive_ref, most_ref, info_ref, used_ref, q_ref, k_ref, v_ref, own_ref, mate_ref, slow_ref, *rest):
+    layer, n_slots, cap, scale, quads, first = dims
+    ko_ref, vo_ref, o_ref, ml_ref, kbuf, vbuf, in_sem, out_sem = rest if first else rest[2:]
+    n_key, lanes = kbuf.shape[1] * kbuf.shape[2], kbuf.shape[3]
+    n_ch = kbuf.shape[1]
     rows = o_ref.shape[1]
-    n_ch = kbuf.shape[2]
     over = most_ref[0] > 2 * cap
     core = who_ref[2]
-
-    def fetches(step, i, src_of):
-        return [pltpu.make_async_copy(src_of(pl.ds(a * n_ch, n_ch)), buf.at[step % 2, i], sem.at[a, step % 2, i])
-                for a, buf in enumerate((kbuf, vbuf))]
-
-    def start(step):
-        @pl.loop(0, blk)
-        def _(i):
-            s = step * blk + i
-            n = info_ref[s]
-            has = n >= 0
-            half = jnp.where(n >= cap, 1, 0)
-            pos = n - half * cap
-
-            def go(cond, src_of):
-                @pl.when(has & cond)
-                def _():
-                    for c in fetches(step, i, src_of):
-                        c.start()
-
-            go(over, lambda part: slow_ref.at[layer, s, part])
-            go(jnp.logical_not(over) & (half == core), lambda part: own_ref.at[part, pos])
-            go(jnp.logical_not(over) & (half != core), lambda part: mate_ref.at[part, pos])
-
-    @pl.when(g == 0)
-    def _():
-        o_ref[...] = jnp.zeros_like(o_ref)
-        lane = lax.broadcasted_iota(jnp.int32, ml_ref.shape, 1)
-        ml_ref[...] = jnp.where(lane < rows, NEG, 0.0)
-        start(0)
-
-    @pl.when(g + 1 < steps)
-    def _():
-        start(g + 1)
-
-    tile = 16
+    bufs = (kbuf, vbuf)
+    part = pl.ds(layer * n_ch, n_ch)
+
+    @pl.loop(0, n_slots)
+    def _(s):
+        n = arrive_ref[s]
+        has = n >= 0
+        half = jnp.where(n >= cap, 1, 0)
+        pos = n - half * cap
+
+        def go(cond, src_of):
+            @pl.when(cond)
+            def _():
+                for a in range(2):
+                    pltpu.make_async_copy(src_of(a), bufs[a].at[s], in_sem.at[a]).start()
+
+        fast = has & jnp.logical_not(over)
+        go(jnp.logical_not(has), lambda a: (k_ref, v_ref)[a].at[s, part])
+        go(has & over, lambda a: slow_ref.at[layer, s, pl.ds(a * n_ch, n_ch)])
+        go(fast & (half == core), lambda a: own_ref.at[pl.ds(a * n_ch, n_ch), pos])
+        go(fast & (half != core), lambda a: mate_ref.at[pl.ds(a * n_ch, n_ch), pos])
+
+    o_ref[...] = jnp.zeros_like(o_ref)
+    ml_lane = lax.broadcasted_iota(jnp.int32, ml_ref.shape, 1)
+    ml_ref[...] = jnp.where(ml_lane < rows, NEG, 0.0)
+    for a in range(2):
+        pltpu.make_async_copy((k_ref, v_ref)[a].at[:, part], bufs[a], in_sem.at[a]).wait()
+
+    n_used = used_ref[0]
+    tile = kbuf.shape[2]
     tile_row = lax.broadcasted_iota(jnp.int32, (tile, lanes), 0)
+
+    @pl.loop(0, n_used)
+    def _(i):
+        s = info_ref[i]
+        lim = info_ref[2 * n_slots + s]
+
+        @pl.when(lim < n_key // 2)
+        def _():
+            fresh = q_ref[info_ref[n_slots + s], rows:].astype(F32)
+            row0 = 2 * lim
+            for c in (row0 // tile, jnp.minimum((row0 + 3) // tile, n_ch - 1)):
+                at = tile_row + c * tile - row0
+                for a, buf in enumerate(bufs):
+                    x = buf[s, c].astype(F32)
+                    for r in range(4):
+                        x = jnp.where(at == r, fresh[4 * a + r:4 * a + r + 1], x)
+                    buf[s, c] = x.astype(BF16)
+
+    outs = [pltpu.make_async_copy(bufs[a], (ko_ref, vo_ref)[a].at[:, part], out_sem.at[a]) for a in range(2)]
+    for c in outs:
+        c.start()
+
     lane = lax.broadcasted_iota(jnp.int32, (rows, n_key), 1)
     row = lax.broadcasted_iota(jnp.int32, (rows, n_key), 0)
     own_head = (lane & 1) == ((row >> 3) & 1)
     late = (lane >> 1) - (row >> 4)
     out_lane = lax.broadcasted_iota(jnp.int32, (rows, lanes), 1)
     out_row = lax.broadcasted_iota(jnp.int32, (rows, lanes), 0)
-
-    @pl.loop(0, blk // group)
+    nothing = jnp.zeros((rows, n_key), BF16)
+
+    @pl.loop(0, (n_used + 4 * quads - 1) // (4 * quads))
     def _(u):
-        facts = []
-        for t in range(group):
-            i = u * group + t
-            s = g * blk + i
-            has = info_ref[s] >= 0
-            b = info_ref[2 * n_slots + s]
-            lim = info_ref[4 * n_slots + s]
-            used = b >= 0
-            b0 = jnp.maximum(b, 0)
-
-            @pl.when(has)
-            def _():
-                for c in fetches(g, i, lambda part: own_ref.at[part, 0]):
-                    c.wait()
-                ko_ref[i] = kbuf[g % 2, i].reshape(n_key, lanes)
-                vo_ref[i] = vbuf[g % 2, i].reshape(n_key, lanes)
-
-            @pl.when(jnp.logical_not(has))
-            def _():
-                ko_ref[i] = k_ref[i]
-                vo_ref[i] = v_ref[i]
-
-            @pl.when(used & (lim < n_key // 2))
-            def _():
-                fresh = q_ref[b0, rows:].astype(F32)
-                row0 = 2 * lim
-                for c in (row0 // tile, jnp.minimum((row0 + 3) // tile, n_key // tile - 1)):
-                    at = tile_row + c * tile - row0
-                    part = pl.ds(pl.multiple_of(c * tile, tile), tile)
-                    for a, ref in enumerate((ko_ref, vo_ref)):
-                        x = ref[i, part].astype(F32)
-                        for r in range(4):
-                            x = jnp.where(at == r, fresh[4 * a + r:4 * a + r + 1], x)
-                        ref[i, part] = x.astype(BF16)
-
-            facts.append((i, used, b0, lim, info_ref[5 * n_slots + s]))
         done = []
-        for i, used, b0, lim, again in facts:
-            sc = lax.dot_general(q_ref[b0, :rows], ko_ref[i], (((1,), (1,)), ((), ())), preferred_element_type=F32) * scale
-            sc = jnp.where(own_head & (late <= lim), sc, NEG)
-            m = jnp.max(sc, axis=1, keepdims=True)
-            p = jnp.exp(sc - m)
-            l = jnp.sum(p, axis=1, keepdims=True)
-            o = jnp.dot(p.astype(BF16), vo_ref[i], preferred_element_type=F32)
-            done.append((used, b0, m, l, o, again))
+        for quad in range(quads):
+            facts = []
+            for t in range(4):
+                i = (u * quads + quad) * 4 + t
+                listed = info_ref[jnp.minimum(i, n_slots - 1)]
+                used = (i < n_slots) & (listed >= 0)
+                s = jnp.where(used, listed, 0)
+                facts.append((s, used, jnp.maximum(info_ref[n_slots + s], 0), info_ref[2 * n_slots + s], info_ref[3 * n_slots + s]))
+            q = jnp.concatenate([q_ref[f[2], :rows] for f in facts], axis=0)
+            k = jnp.concatenate([kbuf[f[0]].reshape(n_key, lanes) for f in facts], axis=0)
+            v = jnp.concatenate([vbuf[f[0]].reshape(n_key, lanes) for f in facts], axis=0)
+            scores = lax.dot_general(q, k, (((1,), (1,)), ((), ())), preferred_element_type=F32)
+            ps, stats = [], []
+            for t, (s, used, b, lim, again) in enumerate(facts):
+                sc = scores[t * rows:(t + 1) * rows, t * n_key:(t + 1) * n_key] * scale
+                sc = jnp.where(own_head & (late <= lim), sc, NEG)
+                m = jnp.max(sc, axis=1, keepdims=True)
+                p = jnp.exp(sc - m)
+                stats.append((m, jnp.sum(p, axis=1, keepdims=True)))
+                ps.append(jnp.concatenate([p.astype(BF16) if x == t else nothing for x in range(4)], axis=1))
+            o = jnp.dot(jnp.concatenate(ps, axis=0), v, preferred_element_type=F32)
+            for t, (s, used, b, lim, again) in enumerate(facts):
+                done.append((used, b, *stats[t], o[t * rows:(t + 1) * rows], again))
         for used, b0, m, l, o, again in done:
             def put(m, l, o):
                 o_ref[b0] = o
@@ -354,12 +363,15 @@
                 w, w1 = jnp.exp(m - mm), jnp.exp(m1 - mm)
                 put(mm, l * w + l1 * w1, o * w + o_ref[b0] * w1)
 
+    for c in outs:
+        c.wait()
+
 
 def combine_kernel(o_ref, ml_ref, out_ref):
     parts, seq_dev, rows, lanes = o_ref.shape
     heads = out_ref.shape[2]
 
-    @pl.loop(0, seq_dev, unroll=6)
+    @pl.loop(0, seq_dev, unroll=12)
     def _(b):
         ml = ml_ref[:, pl.ds(b, 1)].reshape(parts, lanes)
         w = jnp.exp(ml - jnp.max(ml, axis=0, keepdims=True))
@@ -409,8 +421,7 @@
         n_ch = key_rows // tile
         chunks = 2 * n_ch
         cap = 20
-        blk, group = 28, 7
-        assert chunks == n_dev and rows == 32 and n_slots % blk == 0 and old_table.shape[1] == 2
+        assert chunks == n_dev and rows == 32 and old_table.shape[1] == 2
         shift = 18
         magic = -(-(1 << shift) // n_slots)
         assert all((s * magic) >> shift == s // n_slots for s in range(n_dev * n_slots))
@@ -419,6 +430,8 @@
 
         kp = k_pool.reshape(n_slots, layers, n_ch, tile, head_dim)
         vp = v_pool.reshape(n_slots, layers, n_ch, tile, head_dim)
+        kp4 = k_pool.reshape(n_slots, layers * n_ch, tile, head_dim)
+        vp4 = v_pool.reshape(n_slots, layers * n_ch, tile, head_dim)
         packed = pl.pallas_call(
             functools.partial(pack_kernel, n_moves),
             out_shape=[jax.ShapeDtypeStruct((chunks, n_moves, tile, head_dim), BF16)] * layers,
@@ -436,15 +449,14 @@
             scratch_shapes=[pltpu.SemaphoreType.DMA, sems(n_dev), sems(n_dev)],
             compiler_params=comm(0), name='gather_tables')(mine)
 
+        tab = tab.reshape(n_dev, 128)
         dims = (n_dev, n_cols, n_slots, seq_dev, n_moves, cap, page, magic, shift)
-        pages, info, most = pl.pallas_call(
-            functools.partial(plan_kernel, dims),
-            out_shape=(jax.ShapeDtypeStruct((n_dev * cap,), jnp.int32), jax.ShapeDtypeStruct((6 * n_slots,), jnp.int32),
+        pages, arrive, most = pl.pallas_call(
+            functools.partial(places_kernel, dims),
+            out_shape=(jax.ShapeDtypeStruct((n_dev * cap,), jnp.int32), jax.ShapeDtypeStruct((2 * n_slots,), jnp.int32),
                        jax.ShapeDtypeStruct((1,), jnp.int32)),
-            in_specs=[SMEM, SMEM, ANY], out_specs=(SMEM, SMEM, SMEM),
-            scratch_shapes=[pltpu.SMEM((n_dev * n_slots,), jnp.int32), pltpu.SMEM((n_dev // 2,), jnp.int32),
-                            pltpu.SMEM((row_seqs,), jnp.int32), pltpu.SemaphoreType.DMA],
-            name='plan')(who, tab.reshape(n_dev, 128), jnp.full((n_dev * n_slots,), -1, jnp.int32))
+            in_specs=[SMEM, SMEM], out_specs=(SMEM, SMEM, SMEM),
+            scratch_shapes=[pltpu.SMEM((n_dev // 2,), jnp.int32)], name='places')(who, tab)
 
         def regroup(spread, name):
             return pl.pallas_call(
@@ -462,7 +474,7 @@
             found = []
             for p in packed:
                 everything = lax.all_gather(p.swapaxes(0, 1), ('kv2', 'kv'), tiled=True)
-                found.append(everything[jnp.maximum(info[n_slots:2 * n_slots], 0)])
+                found.append(everything[jnp.maximum(arrive[n_slots:], 0)])
             return jnp.stack(found)
 
         def no_pages():
@@ -472,13 +484,17 @@
 
         slow = lax.cond(most[0] > 2 * cap, all_pages, no_pages)
 
-        k_rows = k_pool.reshape(n_slots, layers * key_rows, head_dim)
-        v_rows = v_pool.reshape(n_slots, layers * key_rows, head_dim)
         hidden = x_embed.reshape(n_steps * seq_dev, width)
         k_out = v_out = None
-        grouped, hidden = after((regroup(spread0, 'regroup_pages_0'), hidden))
+        grouped, hidden, tab = after((regroup(spread0, 'regroup_pages_0'), hidden, tab))
         own = deliver(grouped)
-        pool_shape = jax.ShapeDtypeStruct(k_rows.shape, BF16)
+        info, n_used = pl.pallas_call(
+            functools.partial(cells_kernel, dims),
+            out_shape=(jax.ShapeDtypeStruct((4 * n_slots,), jnp.int32), jax.ShapeDtypeStruct((1,), jnp.int32)),
+            in_specs=[SMEM, SMEM, ANY], out_specs=(SMEM, SMEM),
+            scratch_shapes=[pltpu.SMEM((n_dev * n_slots,), jnp.int32), pltpu.SMEM((row_seqs,), jnp.int32), pltpu.SemaphoreType.DMA],
+            name='cells')(who, tab, jnp.full((n_dev * n_slots,), -1, jnp.int32))
+        pool_shape = jax.ShapeDtypeStruct(kp4.shape, BF16)
         for layer in range(layers):
             query = jnp.dot(hidden, w_query[layer], preferred_element_type=F32).astype(BF16)
             k_new = jnp.dot(hidden, w_key[layer], preferred_element_type=F32).astype(BF16)
@@ -489,7 +505,7 @@
 
             load = jnp.concatenate([by_seq(query), by_seq(k_new), by_seq(v_new)], axis=1)
             q_rows = load.shape[1]
-            own, load = after((own, load))
+            own, load, info = after((own, load, info))
             mate = to_mate(own)
             n_chips = n_cols // 2
             q_row = pl.pallas_call(
@@ -504,23 +520,18 @@
             if not last:
                 moving, q_row = after((packed[layer + 1], q_row))
                 spread = lax.all_to_all(moving, ('kv2', 'kv'), 0, 0, tiled=True)
-            dims = (layer, n_slots, blk, group, cap, head_dim ** -0.5, first)
-            pool_block = pl.BlockSpec((blk, key_rows, head_dim), lambda g, *_, at=layer: (g, at, 0))
-            whole = lambda shape: pl.BlockSpec(shape, lambda g, *_: (0,) * len(shape))
             carried = () if first else (k_out, v_out)
             k_out, v_out, part, ml = pl.pallas_call(
-                functools.partial(attend_kernel, dims),
-                grid_spec=pltpu.PrefetchScalarGridSpec(
-                    num_scalar_prefetch=3, grid=(n_slots // blk,),
-                    in_specs=[whole((row_seqs, q_rows, head_dim)), pool_block, pool_block, ANY, ANY, ANY] + [ANY] * len(carried),
-                    out_specs=[pool_block, pool_block, whole((row_seqs, rows, head_dim)), whole((row_seqs, head_dim))],
-                    scratch_shapes=[pltpu.VMEM((2, blk, n_ch, tile, head_dim), BF16), pltpu.VMEM((2, blk, n_ch, tile, head_dim), BF16),
-                                    sems(2, 2, blk)]),
+                functools.partial(attend_kernel, (layer, n_slots, cap, head_dim ** -0.5, 2, first)),
+                in_specs=[SMEM] * 5 + [VMEM] + [ANY] * (5 + len(carried)),
+                out_specs=[ANY, ANY, VMEM, VMEM],
                 out_shape=[pool_shape, pool_shape, jax.ShapeDtypeStruct((row_seqs, rows, head_dim), F32),
                            jax.ShapeDtypeStruct((row_seqs, head_dim), F32)],
-                input_output_aliases={} if first else {9: 0, 10: 1},
-                compiler_params=pltpu.CompilerParams(dimension_semantics=('arbitrary',)),
-                name=f'attend_{layer}')(info, most, who, q_row.reshape(row_seqs, q_rows, head_dim), k_rows, v_rows, own, mate, slow, *carried)
+                scratch_shapes=[pltpu.VMEM((n_slots, n_ch, tile, head_dim), BF16), pltpu.VMEM((n_slots, n_ch, tile, head_dim), BF16),
+                                sems(2), sems(2)],
+                input_output_aliases={} if first else {11: 0, 12: 1},
+                name=f'attend_{layer}')(who, arrive, most, info, n_used, q_row.reshape(row_seqs, q_rows, head_dim), kp4, vp4,
+                                        own, mate, slow, *carried)
 
             home, home_ml = pl.pallas_call(
                 functools.partial(row_exchange_kernel, n_cols),

time: 418 us -> 357 us (0.85)
  Pallas kernels: 266 us -> 213 us
  waiting for transfers between devices: 12.4 us -> 3.68 us
    pallas_call x3 -> x4, Pallas kernels: 99.8 us -> 35.7 us  [the longest x2 21.6 us: per_device(): pl.pallas_call(functools.partial(attend_kernel, (layer, n_slots, cap, hea...]
    pallas_call x2, Pallas kernels: 85.5 us -> 96.8 us  [per_device(): pl.pallas_call(functools.partial(row_exchange_kernel, n_cols), out_shape=...]
    all_to_all x2, waiting for transfers between devices: 12.4 us -> 3.67 us  [deliver(): return lax.all_to_all(grouped, ('kv2', 'kv'), 0, 0, tiled=True)]
  transfers between devices with their start and end apart: 6 -> 6, of which waited for: 1 -> 1; matrix products, arithmetic and copies ran while one was open for 14% -> 16% of each run, Pallas kernels for 40% -> 39%
where the time goes in v2:
time: 357 us; the launch traced here: 356 us
  Pallas kernels  213 us (60%)
  matrix products  93.2 us (26%)
  starting transfers between devices  22.7 us (6%)
  between operations  15.1 us (4%)
  local copies, waits for them, and re-layouts  4.57 us (1%)
  waiting for transfers between devices  3.68 us (1%)
    pallas_call x2, Pallas kernels, per_device(): pl.pallas_call(functools.partial(row_exchange_kernel, n_cols), out_shape=...  96.8 us
    pallas_call x2, Pallas kernels, per_device(): pl.pallas_call(functools.partial(row_gather_kernel, n_cols), out_shape=ja...  38.8 us
    dot_general x2, matrix products, per_device(): jnp.dot(up_act, w_down[layer], preferred_element_type=F32)  34.5 us
    dot_general x2, matrix products, per_device(): jnp.dot(hidden, w_up[layer], preferred_element_type=F32)  33.6 us
    pallas_call x2, Pallas kernels, per_device(): pl.pallas_call(functools.partial(attend_kernel, (layer, n_slots, cap, hea...  21.6 us
    pallas_call x1, Pallas kernels, per_device(): pl.pallas_call(functools.partial(gather_all_kernel, n_dev, n_cols), out_s...  18.6 us
    pallas_call x2, Pallas kernels, per_device(): pl.pallas_call(combine_kernel, out_shape=jax.ShapeDtypeStruct((n_steps, s...  12.9 us
    dot_general x2, matrix products, per_device(): jnp.dot(attn_out, w_out[layer], preferred_element_type=F32)  10.1 us
  transfers between devices with their start and end apart: 6, of which 1 were waited for; matrix products, arithmetic and copies ran while one was open for 16% of the time, Pallas kernels for 39%

profile of v2, /device:TPU:97, one launch (start us, length us, event | category | flops | bytes accessed | tf_op | source)
XLA Modules:
  0.0 355.8 jit_solution(6389166907284154463)
XLA Ops:
  7.2 1.2 broadcast_subtract_fusion.src_ref
  8.4 4.2 %pack_pages.1 = (bf16[32,16,8,128]{3,2,1,0:T(8,128)(2,1)}, bf16[32,16,8,128]{3,2,1,0:T(8,128)(2,1)}) custom-call(s32[16]{0:T(128)} %broadcast_subtract_fusion.src_ref, bf16[112,2,16,8,128]{4,3,2,1,0:T(8,128)(2,1)} %bitcast.141, bf16[112,2,16,8,128]{4,3,2,1,0:T(8,128)(2,1)} %bitcast.144), custom_call_target="tpu_custom_call" | custom-call | tf_op jit(solution)/shard_map/pack_pages/pallas_call | solution.py:435
  12.6 9.2 %all-to-all-start = ((bf16[32,16,8,128]{3,2,1,0:T(8,128)(2,1)}), bf16[32,16,8,128]{3,2,1,0:T(8,128)(2,1)S(1)}, u32[]{:S(2)}, u32[]{:S(2)}) async-start(bf16[32,16,8,128]{3,2,1,0:T(8,128)(2,1)} %get-tuple-element.51), calls=%async_computation | async-start | bytes 2097152 | tf_op jit(solution)/shard_map/all_to_all | solution.py:441
  22.6 18.6 %gather_tables.1 = s32[32,1,128]{2,1,0:T(1,128)} custom-call(s32[1,128]{1,0:T(1,128)} %pad_bitcast_fusion.x_ref), custom_call_target="tpu_custom_call" | custom-call | tf_op jit(solution)/shard_map/gather_tables/pallas_call | solution.py:445
  41.8 6.1 %places.1 = (s32[640]{0:T(1024)}, s32[224]{0:T(256)S(1)}, s32[1]{0:T(128)}) custom-call(s32[3]{0:T(128)} %pad_add_fusion.who_ref, s32[32,128]{1,0:T(8,128)} %bitcast.163), custom_call_target="tpu_custom_call" | custom-call | tf_op jit(solution)/shard_map/places/pallas_call | solution.py:454
  48.9 3.1 regroup_pages_0.1
  52.0 3.7 %all-to-all-start.1 = ((bf16[32,20,8,128]{3,2,1,0:T(8,128)(2,1)}), bf16[32,20,8,128]{3,2,1,0:T(8,128)(2,1)S(1)}, u32[]{:S(2)}, u32[]{:S(2)}) async-start(bf16[32,20,8,128]{3,2,1,0:T(8,128)(2,1)} %regroup_pages_0.1), calls=%async_computation.1 | async-start | bytes 2621440 | tf_op jit(solution)/shard_map/all_to_all | solution.py:468
  55.7 5.0 %fusion.81 = bf16[6,8,16,128]{3,1,2,0:T(8,128)(2,1)S(1)} fusion(bf16[48,2048]{1,0:T(8,128)(2,1)S(1)} %bitcast.171, bf16[2,2048,2048]{2,1,0:T(8,128)(2,1)} %param.16), kind=kOutput, calls=%fused_computation.58 | convolution fusion | flops 402751488 | bytes 8781824 | tf_op jit(solution)/shard_map/dot_general | solution.py:499
  60.7 1.5 convolution_convert_fusion.3
  62.3 1.5 convolution_convert_fusion.2
  64.4 8.1 %cells.1 = (s32[448]{0:T(512)}, s32[1]{0:T(128)}) custom-call(s32[3]{0:T(128)} %pad_add_fusion.who_ref, s32[32,128]{1,0:T(8,128)} %bitcast.164, s32[3584]{0:T(1024)} %broadcast_in_dim.7.none_ref), custom_call_target="tpu_custom_call" | custom-call | tf_op jit(solution)/shard_map/cells/pallas_call | solution.py:491
  73.3 3.7 %all-to-all-done.1.own_ref = bf16[32,20,8,128]{3,2,1,0:T(8,128)(2,1)S(1)} async-done(((bf16[32,20,8,128]{3,2,1,0:T(8,128)(2,1)}), bf16[32,20,8,128]{3,2,1,0:T(8,128)(2,1)S(1)}, u32[]{:S(2)}, u32[]{:S(2)}) %all-to-all-start.1) | async-done | bytes 1310752 | tf_op jit(solution)/shard_map/all_to_all | solution.py:468
  76.9 19.4 %gather_queries_0.1 = bf16[8,24,40,128]{3,2,1,0:T(8,128)(2,1)} custom-call(bf16[24,40,128]{2,1,0:T(8,128)(2,1)} %pad_maximum_fusion.1.x_ref), custom_call_target="tpu_custom_call" | custom-call | tf_op jit(solution)/shard_map/gather_queries_0/pallas_call | solution.py:511
  96.3 3.0 all-to-all-start.2
  100.0 10.7 %attend_0.1 = (bf16[112,32,8,128]{3,2,1,0:T(8,128)(2,1)}, bf16[112,32,8,128]{3,2,1,0:T(8,128)(2,1)}, f32[192,32,128]{2,1,0:T(8,128)}, f32[192,128]{1,0:T(8,128)}) custom-call(s32[3]{0:T(128)} %pad_add_fusion.who_ref, s32[224]{0:T(256)S(1)} %get-tuple-element.58.arrive_ref, s32[1]{0:T(128)} %get-tuple-element.59.most_ref, s32[448]{0:T(512)} %get-tuple-element.72.info_ref, ...), custom_call_target="tpu_custom_call" | custom-call | tf_op jit(solution)/shard_map/attend_0/pallas_call | solution.py:524
  110.7 48.7 %return_parts_0.1 = (f32[8,24,32,128]{3,2,1,0:T(8,128)}, f32[8,24,128]{2,1,0:T(8,128)}) custom-call(f32[8,24,32,128]{3,2,1,0:T(8,128)} %bitcast.156, f32[8,24,128]{2,1,0:T(8,128)} %bitcast.166), custom_call_target="tpu_custom_call" | custom-call | tf_op jit(solution)/shard_map/return_parts_0/pallas_call | solution.py:536
  159.5 6.5 %combine_0.1 = bf16[2,24,16,128]{3,2,1,0:T(8,128)(2,1)} custom-call(f32[8,24,32,128]{3,2,1,0:T(8,128)} %get-tuple-element.66.o_ref, f32[8,24,128]{2,1,0:T(8,128)} %get-tuple-element.67.ml_ref), custom_call_target="tpu_custom_call" | custom-call | tf_op jit(solution)/shard_map/combine_0/pallas_call | solution.py:544
  165.9 5.1 %fusion.51 = bf16[48,2048]{1,0:T(8,128)(2,1)S(1)} fusion(bf16[2,2048,2048]{2,1,0:T(8,128)(2,1)} %param.19, bf16[48,2048]{1,0:T(8,128)(2,1)S(1)} %bitcast.174, bf16[6,8,16,128]{3,2,1,0:T(8,128)(2,1)} %bitcast.162), kind=kOutput, calls=%fused_computation.40 | convolution fusion | flops 402948096 | bytes 8978432 | tf_op jit(solution)/shard_map/dot_general | solution.py:549
  172.0 3.1 regroup_pages_1.1
  175.1 5.9 %all-to-all-start.3 = ((bf16[32,20,8,128]{3,2,1,0:T(8,128)(2,1)}), bf16[32,20,8,128]{3,2,1,0:T(8,128)(2,1)S(1)}, u32[]{:S(2)}, u32[]{:S(2)}) async-start(bf16[32,20,8,128]{3,2,1,0:T(8,128)(2,1)} %regroup_pages_1.1), calls=%async_computation.3 | async-start | bytes 2621440 | tf_op jit(solution)/shard_map/all_to_all | solution.py:468
  181.0 16.8 %fusion.63 = bf16[48,11008]{1,0:T(8,128)(2,1)S(1)} fusion(bf16[48,2048]{1,0:T(8,128)(2,1)S(1)} %fusion.51, bf16[2,2048,11008]{2,1,0:T(8,128)(2,1)} %param.20), kind=kOutput, calls=%fused_computation.48 | convolution fusion | flops 2169016320 | bytes 46342144 | tf_op jit(solution)/shard_map/dot_general | solution.py:554
  197.8 16.9 %fusion.39 = bf16[48,2048]{1,0:T(8,128)(2,1)S(1)} fusion(bf16[48,11008]{1,0:T(8,128)(2,1)S(1)} %fusion.63, bf16[2,11008,2048]{2,1,0:T(8,128)(2,1)} %param.21, bf16[48,2048]{1,0:T(8,128)(2,1)S(1)} %fusion.51), kind=kOutput, calls=%fused_computation.36 | convolution fusion | flops 2164555776 | bytes 46538752 | tf_op jit(solution)/shard_map/dot_general | solution.py:555
  214.8 5.1 %fusion.78 = bf16[6,8,16,128]{3,1,2,0:T(8,128)(2,1)S(1)} fusion(bf16[48,2048]{1,0:T(8,128)(2,1)S(1)} %fusion.39, bf16[2,2048,2048]{2,1,0:T(8,128)(2,1)} %param.16), kind=kOutput, calls=%fused_computation.57 | convolution fusion | flops 402751488 | bytes 8781824 | tf_op jit(solution)/shard_map/dot_general | solution.py:499
  220.3 1.5 convolution_convert_fusion
  223.6 19.4 %gather_queries_1.1 = bf16[8,24,40,128]{3,2,1,0:T(8,128)(2,1)} custom-call(bf16[24,40,128]{2,1,0:T(8,128)(2,1)} %pad_maximum_fusion.2.x_ref), custom_call_target="tpu_custom_call" | custom-call | tf_op jit(solution)/shard_map/gather_queries_1/pallas_call | solution.py:511
  243.0 1.1 copy-done.4
  244.1 10.9 %attend_1.1 = (bf16[112,32,8,128]{3,2,1,0:T(8,128)(2,1)}, bf16[112,32,8,128]{3,2,1,0:T(8,128)(2,1)}, f32[192,32,128]{2,1,0:T(8,128)}, f32[192,128]{1,0:T(8,128)}) custom-call(s32[3]{0:T(128)} %pad_add_fusion.who_ref, s32[224]{0:T(256)S(1)} %get-tuple-element.58.arrive_ref, ...), custom_call_target="tpu_custom_call", output_to_operand_aliasing={{0}: (11, {}), {1}: (12, {})} | custom-call | tf_op jit(solution)/shard_map/attend_1/pallas_call | solution.py:524
  255.0 48.0 %return_parts_1.1 = (f32[8,24,32,128]{3,2,1,0:T(8,128)}, f32[8,24,128]{2,1,0:T(8,128)}) custom-call(f32[8,24,32,128]{3,2,1,0:T(8,128)} %bitcast.155, f32[8,24,128]{2,1,0:T(8,128)} %bitcast.165), custom_call_target="tpu_custom_call" | custom-call | tf_op jit(solution)/shard_map/return_parts_1/pallas_call | solution.py:536
  303.0 6.5 %combine_1.1 = bf16[2,24,16,128]{3,2,1,0:T(8,128)(2,1)} custom-call(f32[8,24,32,128]{3,2,1,0:T(8,128)} %get-tuple-element.79.o_ref, f32[8,24,128]{2,1,0:T(8,128)} %get-tuple-element.80.ml_ref), custom_call_target="tpu_custom_call" | custom-call | tf_op jit(solution)/shard_map/combine_1/pallas_call | solution.py:544
  309.5 5.1 %fusion.48 = bf16[48,2048]{1,0:T(8,128)(2,1)S(1)} fusion(bf16[2,2048,2048]{2,1,0:T(8,128)(2,1)} %param.19, bf16[48,2048]{1,0:T(8,128)(2,1)S(1)} %fusion.39, bf16[6,8,16,128]{3,2,1,0:T(8,128)(2,1)} %bitcast.161), kind=kOutput, calls=%fused_computation.39 | convolution fusion | flops 402948096 | bytes 8978432 | tf_op jit(solution)/shard_map/dot_general | solution.py:549
  314.6 16.8 %fusion.75 = bf16[48,11008]{1,0:T(8,128)(2,1)S(1)} fusion(bf16[48,2048]{1,0:T(8,128)(2,1)S(1)} %fusion.48, bf16[2,2048,11008]{2,1,0:T(8,128)(2,1)} %param.20), kind=kOutput, calls=%fused_computation.56 | convolution fusion | flops 2169016320 | bytes 46342144 | tf_op jit(solution)/shard_map/dot_general | solution.py:554
  331.4 17.6 %fusion.36 = bf16[48,2048]{1,0:T(8,128)(2,1)} fusion(bf16[48,11008]{1,0:T(8,128)(2,1)S(1)} %fusion.75, bf16[2,11008,2048]{2,1,0:T(8,128)(2,1)} %param.21, bf16[48,2048]{1,0:T(8,128)(2,1)S(1)} %fusion.48), kind=kOutput, calls=%fused_computation.35 | convolution fusion | flops 2164555776 | bytes 46538752 | tf_op jit(solution)/shard_map/dot_general | solution.py:555
  (51 shorter events, 6.9 us)
Async XLA Ops:
  8.4 13.4 %copy-start.5 = (s32[24,2]{0,1:T(2,128)S(1)}, s32[24,2]{0,1:T(2,128)}, u32[]{:S(2)}) copy-start(s32[24,2]{0,1:T(2,128)} %param.24) | copy-start | bytes 580
  8.4 13.6 %copy-start.6 = (s32[16]{0:T(128)S(1)}, s32[16]{0:T(128)}, u32[]{:S(2)}) copy-start(s32[16]{0:T(128)} %param.27) | copy-start | bytes 196
  8.4 13.6 %copy-start.7 = (s32[16]{0:T(128)S(1)}, s32[16]{0:T(128)}, u32[]{:S(2)}) copy-start(s32[16]{0:T(128)} %param.26) | copy-start | bytes 196
  8.4 13.6 %copy-start.8 = (s32[24]{0:T(128)S(1)}, s32[24]{0:T(128)}, u32[]{:S(2)}) copy-start(s32[24]{0:T(128)} %param.25) | copy-start | bytes 292
  8.4 47.3 %copy-start.10 = (bf16[2,24,2048]{2,1,0:T(8,128)(2,1)S(1)}, bf16[2,24,2048]{2,1,0:T(8,128)(2,1)}, u32[]{:S(2)}) copy-start(bf16[2,24,2048]{2,1,0:T(8,128)(2,1)} %param.15) | copy-start | bytes 589828
  12.6 35.3 %all-to-all-start = ((bf16[32,16,8,128]{3,2,1,0:T(8,128)(2,1)}), bf16[32,16,8,128]{3,2,1,0:T(8,128)(2,1)S(1)}, u32[]{:S(2)}, u32[]{:S(2)}) async-start(bf16[32,16,8,128]{3,2,1,0:T(8,128)(2,1)} %get-tuple-element.51), calls=%async_computation | async-start | bytes 2097152 | tf_op jit(solution)/shard_map/all_to_all | solution.py:441
  47.9 1.0 copy-start.3
  52.0 25.0 %all-to-all-start.1 = ((bf16[32,20,8,128]{3,2,1,0:T(8,128)(2,1)}), bf16[32,20,8,128]{3,2,1,0:T(8,128)(2,1)S(1)}, u32[]{:S(2)}, u32[]{:S(2)}) async-start(bf16[32,20,8,128]{3,2,1,0:T(8,128)(2,1)} %regroup_pages_0.1), calls=%async_computation.1 | async-start | bytes 2621440 | tf_op jit(solution)/shard_map/all_to_all | solution.py:468
  76.9 23.0 %copy-start = (bf16[32,20,8,128]{3,2,1,0:T(8,128)(2,1)}, bf16[32,20,8,128]{3,2,1,0:T(8,128)(2,1)S(1)}, u32[]{:S(2)}) copy-start(bf16[32,20,8,128]{3,2,1,0:T(8,128)(2,1)S(1)} %all-to-all-done.1.own_ref) | copy-start | bytes 3932164
  76.9 23.1 %collective-permute-start = (bf16[32,20,8,128]{3,2,1,0:T(8,128)(2,1)S(1)}, bf16[32,20,8,128]{3,2,1,0:T(8,128)(2,1)}, u32[]{:S(2)}, u32[]{:S(2)}) collective-permute-start(bf16[32,20,8,128]{3,2,1,0:T(8,128)(2,1)S(1)} %all-to-all-done.1.own_ref), channel_id=1, source_target_pairs={{0,1},{1,0},{2,3},{3,2},{4,5},{5,4},{6,7},{7,6},{8,9},{9,8},{10,11... | collective-permute-start | bytes 3932168 | tf_op jit(solution)/shard_map/ppermute | solution.py:471
  96.3 74.7 %all-to-all-start.2 = ((bf16[32,16,8,128]{3,2,1,0:T(8,128)(2,1)}), bf16[32,16,8,128]{3,2,1,0:T(8,128)(2,1)S(1)}, u32[]{:S(2)}, u32[]{:S(2)}) async-start(bf16[32,16,8,128]{3,2,1,0:T(8,128)(2,1)} %get-tuple-element.57), calls=%async_computation.2 | async-start | bytes 2097152 | tf_op jit(solution)/shard_map/all_to_all | solution.py:522
  171.0 1.0 copy-start.2
  175.1 47.6 %all-to-all-start.3 = ((bf16[32,20,8,128]{3,2,1,0:T(8,128)(2,1)}), bf16[32,20,8,128]{3,2,1,0:T(8,128)(2,1)S(1)}, u32[]{:S(2)}, u32[]{:S(2)}) async-start(bf16[32,20,8,128]{3,2,1,0:T(8,128)(2,1)} %regroup_pages_1.1), calls=%async_computation.3 | async-start | bytes 2621440 | tf_op jit(solution)/shard_map/all_to_all | solution.py:468
  214.8 5.2 %copy-start.9 = (bf16[2,2048,256]{2,1,0:T(8,128)(2,1)S(1)}, bf16[2,2048,256]{2,1,0:T(8,128)(2,1)}, u32[]{:S(2)}) copy-start(bf16[2,2048,256]{2,1,0:T(8,128)(2,1)} %param.17) | copy-start | bytes 6291460
  222.7 20.4 %copy-start.1 = (bf16[32,20,8,128]{3,2,1,0:T(8,128)(2,1)}, bf16[32,20,8,128]{3,2,1,0:T(8,128)(2,1)S(1)}, u32[]{:S(2)}) copy-start(bf16[32,20,8,128]{3,2,1,0:T(8,128)(2,1)S(1)} %all-to-all-done.3.own_ref) | copy-start | bytes 3932164
  222.7 20.3 %collective-permute-start.1 = (bf16[32,20,8,128]{3,2,1,0:T(8,128)(2,1)S(1)}, bf16[32,20,8,128]{3,2,1,0:T(8,128)(2,1)S(1)}, u32[]{:S(2)}, u32[]{:S(2)}) collective-permute-start(bf16[32,20,8,128]{3,2,1,0:T(8,128)(2,1)S(1)} %all-to-all-done.3.own_ref), channel_id=1, source_target_pairs={{0,1},{1,0},{2,3},{3,2},{4,5},{5,4},{6,7},{7,6},{8,9},{9,8},{10,11... | collective-permute-start | bytes 3932168 | tf_op jit(solution)/shard_map/ppermute | solution.py:471
  243.0 1.1 copy-start.4

commit v3 on v2

--- a/solution.py
+++ b/solution.py
@@ -99,32 +99,81 @@
     c.wait_recv()
 
 
-def row_exchange_kernel(n_cols, x_ref, y_ref, ox_ref, oy_ref, local_sem, send_sem, recv_sem):
+def return_kernel(n_cols, x_ref, ml_ref, out_ref, mate_o, mate_ml, sum_o, sum_ml, got_o, got_ml, dsend, drecv, send, recv):
+    n_chips = n_cols // 2
     kv = lax.axis_index('kv')
+    chip, core = kv // 2, kv % 2
+    mate = chip * 2 + 1 - core
+    seq_dev, rows, lanes = x_ref.shape[1:]
+    heads = out_ref.shape[2]
     barrier = pltpu.get_barrier_semaphore()
-    for r in range(1, n_cols):
-        pl.semaphore_signal(barrier, inc=1, device_id={'kv': (kv + r) % n_cols}, device_id_type=MESH)
-    pl.semaphore_wait(barrier, n_cols - 1)
-
-    def copy(a, r, dst, slot):
-        src_ref, dst_ref = ((x_ref, ox_ref), (y_ref, oy_ref))[a]
+    for r in range(1, n_chips):
+        pl.semaphore_signal(barrier, inc=1, device_id={'kv': (chip + r) % n_chips * 2 + core}, device_id_type=MESH)
+    pl.semaphore_signal(barrier, inc=1, device_id={'kv': mate}, device_id_type=MESH)
+    pl.semaphore_wait(barrier, n_chips)
+
+    def across(r, a):
+        src, dst = ((x_ref, mate_o), (ml_ref, mate_ml))[a]
         return pltpu.make_async_remote_copy(
-            src_ref=src_ref.at[dst], dst_ref=dst_ref.at[slot], send_sem=send_sem.at[a, r], recv_sem=recv_sem.at[a, r],
-            device_id={'kv': dst}, device_id_type=MESH)
-
-    for r in range(1, n_cols):
+            src_ref=src.at[(chip + r) % n_chips * 2 + 1 - core], dst_ref=dst.at[r], send_sem=dsend.at[a, r], recv_sem=drecv.at[a, r],
+            device_id={'kv': mate}, device_id_type=MESH)
+
+    def home(r, a):
+        src, dst = ((sum_o, got_o), (sum_ml, got_ml))[a]
+        return pltpu.make_async_remote_copy(
+            src_ref=src.at[r], dst_ref=dst.at[r], send_sem=send.at[a, r], recv_sem=recv.at[a, r],
+            device_id={'kv': (chip + r) % n_chips * 2 + core}, device_id_type=MESH)
+
+    order = sorted(range(1, n_chips), key=lambda r: -min(r, n_chips - r)) + [0]
+    for r in order:
         for a in range(2):
-            copy(a, r, (kv + r) % n_cols, kv).start()
-    own = [pltpu.make_async_copy(s.at[kv], d.at[kv], local_sem.at[a]) for a, (s, d) in enumerate(((x_ref, ox_ref), (y_ref, oy_ref)))]
-    for c in own:
-        c.start()
-    for c in own:
-        c.wait()
-    for r in range(1, n_cols):
+            across(r, a).start()
+    lane = lax.broadcasted_iota(jnp.int32, (8, lanes), 1)
+    for r in order:
+        slot = (chip + r) % n_chips * 2 + core
+        to_o, to_ml = (sum_o, sum_ml) if r else (got_o, got_ml)
         for a in range(2):
-            c = copy(a, r, (kv + r) % n_cols, (kv + n_cols - r) % n_cols)
-            c.wait_send()
-            c.wait_recv()
+            across(r, a).wait_recv()
+
+        @pl.loop(0, seq_dev // 8)
+        def _(g):
+            some = pl.ds(pl.multiple_of(8 * g, 8), 8)
+            ml1, ml2 = ml_ref[slot, some], mate_ml[r, some]
+            top = jnp.maximum(ml1, ml2)
+            w1, w2 = jnp.exp(ml1 - top), jnp.exp(ml2 - top)
+            l = pltpu.roll(w1, rows, 1) * ml1 + pltpu.roll(w2, rows, 1) * ml2
+            to_ml[r, some] = jnp.where(lane < rows, top, l)
+            c1, c2 = w1.T, w2.T
+            for t in range(8):
+                b = 8 * g + t
+                to_o[r, b] = c1[:rows, t:t + 1] * x_ref[slot, b] + c2[:rows, t:t + 1] * mate_o[r, b]
+
+        if r:
+            for a in range(2):
+                home(r, a).start()
+    for r in range(1, n_chips):
+        for a in range(2):
+            home(r, a).wait_recv()
+
+    @pl.loop(0, seq_dev // 8)
+    def _(g):
+        some = pl.ds(pl.multiple_of(8 * g, 8), 8)
+        mls = [got_ml[p, some] for p in range(n_chips)]
+        top = functools.reduce(jnp.maximum, mls)
+        ws = [jnp.exp(x - top) for x in mls]
+        total = sum(w * pltpu.roll(x, lanes - rows, 1) for w, x in zip(ws, mls))
+        cols = [(w / total).T for w in ws]
+        for t in range(8):
+            b = 8 * g + t
+            acc = sum(c[:rows, t:t + 1] * got_o[p, b] for p, c in enumerate(cols)).astype(BF16)
+            out_ref[0, b] = acc[:heads]
+            out_ref[1, b] = acc[heads:]
+
+    for r in range(n_chips):
+        for a in range(2):
+            across(r, a).wait_send()
+            if r:
+                home(r, a).wait_send()
 
 
 def places_kernel(dims, who_ref, tab_ref, pages_ref, arrive_ref, most_ref, count):
@@ -367,25 +416,6 @@
         c.wait()
 
 
-def combine_kernel(o_ref, ml_ref, out_ref):
-    parts, seq_dev, rows, lanes = o_ref.shape
-    heads = out_ref.shape[2]
-
-    @pl.loop(0, seq_dev, unroll=12)
-    def _(b):
-        ml = ml_ref[:, pl.ds(b, 1)].reshape(parts, lanes)
-        w = jnp.exp(ml - jnp.max(ml, axis=0, keepdims=True))
-        l = pltpu.roll(ml, lanes - rows, 1)
-        w = w / jnp.sum(w * l, axis=0, keepdims=True)
-        wt = w.T
-        acc = jnp.zeros((rows, lanes), F32)
-        for s in range(parts):
-            acc = acc + wt[:rows, s:s + 1] * o_ref[s, b]
-        acc = acc.astype(BF16)
-        out_ref[0, b] = acc[:heads]
-        out_ref[1, b] = acc[heads:]
-
-
 def blank_kernel(o_ref):
     pass
 
@@ -438,7 +468,6 @@
             in_specs=[SMEM, ANY, ANY], out_specs=[VMEM] * layers,
             scratch_shapes=[sems(layers, 2, n_moves)], name='pack_pages')(src_slot - me * n_slots, kp, vp)
         after = lax.optimization_barrier
-        spread0 = lax.all_to_all(packed[0], ('kv2', 'kv'), 0, 0, tiled=True)
 
         mine = jnp.concatenate([old_table.reshape(-1), seq_len, src_slot, dst_slot])
         mine = jnp.pad(mine, (0, 128 - mine.shape[0])).reshape(1, 128)
@@ -450,6 +479,8 @@
             compiler_params=comm(0), name='gather_tables')(mine)
 
         tab = tab.reshape(n_dev, 128)
+        moving, tab = after((packed[0], tab))
+        spread = lax.all_to_all(moving, ('kv2', 'kv'), 0, 0, tiled=True)
         dims = (n_dev, n_cols, n_slots, seq_dev, n_moves, cap, page, magic, shift)
         pages, arrive, most = pl.pallas_call(
             functools.partial(places_kernel, dims),
@@ -486,15 +517,6 @@
 
         hidden = x_embed.reshape(n_steps * seq_dev, width)
         k_out = v_out = None
-        grouped, hidden, tab = after((regroup(spread0, 'regroup_pages_0'), hidden, tab))
-        own = deliver(grouped)
-        info, n_used = pl.pallas_call(
-            functools.partial(cells_kernel, dims),
-            out_shape=(jax.ShapeDtypeStruct((4 * n_slots,), jnp.int32), jax.ShapeDtypeStruct((1,), jnp.int32)),
-            in_specs=[SMEM, SMEM, ANY], out_specs=(SMEM, SMEM),
-            scratch_shapes=[pltpu.SMEM((n_dev * n_slots,), jnp.int32), pltpu.SMEM((row_seqs,), jnp.int32), pltpu.SemaphoreType.DMA],
-            name='cells')(who, tab, jnp.full((n_dev * n_slots,), -1, jnp.int32))
-        pool_shape = jax.ShapeDtypeStruct(kp4.shape, BF16)
         for layer in range(layers):
             query = jnp.dot(hidden, w_query[layer], preferred_element_type=F32).astype(BF16)
             k_new = jnp.dot(hidden, w_key[layer], preferred_element_type=F32).astype(BF16)
@@ -505,8 +527,21 @@
 
             load = jnp.concatenate([by_seq(query), by_seq(k_new), by_seq(v_new)], axis=1)
             q_rows = load.shape[1]
-            own, load, info = after((own, load, info))
-            mate = to_mate(own)
+            if layer == 0:
+                spread, load, pages = after((spread, load, pages))
+                grouped, load, tab = after((regroup(spread, 'regroup_pages_0'), load, tab))
+                own = deliver(grouped)
+                info, n_used = pl.pallas_call(
+                    functools.partial(cells_kernel, dims),
+                    out_shape=(jax.ShapeDtypeStruct((4 * n_slots,), jnp.int32), jax.ShapeDtypeStruct((1,), jnp.int32)),
+                    in_specs=[SMEM, SMEM, ANY], out_specs=(SMEM, SMEM),
+                    scratch_shapes=[pltpu.SMEM((n_dev * n_slots,), jnp.int32), pltpu.SMEM((row_seqs,), jnp.int32), pltpu.SemaphoreType.DMA],
+                    name='cells')(who, tab, jnp.full((n_dev * n_slots,), -1, jnp.int32))
+                pool_shape = jax.ShapeDtypeStruct(kp4.shape, BF16)
+                load, info = after((load, info))
+            else:
+                own, load = after((own, load))
+                mate = to_mate(own)
             n_chips = n_cols // 2
             q_row = pl.pallas_call(
                 functools.partial(row_gather_kernel, n_cols),
@@ -516,6 +551,9 @@
                 compiler_params=comm(3 + layer), name=f'gather_queries_{layer}')(load)
 
             first = layer == 0
+            if first:
+                own, q_row = after((own, q_row))
+                mate = to_mate(own)
             last = layer == layers - 1
             if not last:
                 moving, q_row = after((packed[layer + 1], q_row))
@@ -533,18 +571,14 @@
                 name=f'attend_{layer}')(who, arrive, most, info, n_used, q_row.reshape(row_seqs, q_rows, head_dim), kp4, vp4,
                                         own, mate, slow, *carried)
 
-            home, home_ml = pl.pallas_call(
-                functools.partial(row_exchange_kernel, n_cols),
-                out_shape=(jax.ShapeDtypeStruct((n_cols, seq_dev, rows, head_dim), F32),
-                           jax.ShapeDtypeStruct((n_cols, seq_dev, head_dim), F32)),
-                in_specs=[ANY, ANY], out_specs=(ANY, ANY),
-                scratch_shapes=[sems(2), sems(2, n_cols), sems(2, n_cols)],
-                compiler_params=comm(5 + layer), name=f'return_parts_{layer}')(
+            parts, parts_ml = (n_chips, seq_dev, rows, head_dim), (n_chips, seq_dev, head_dim)
+            attn = pl.pallas_call(
+                functools.partial(return_kernel, n_cols),
+                out_shape=jax.ShapeDtypeStruct((n_steps, seq_dev, heads, head_dim), BF16),
+                in_specs=[VMEM, VMEM], out_specs=VMEM,
+                scratch_shapes=[pltpu.VMEM(shape, F32) for _ in range(3) for shape in (parts, parts_ml)] + [sems(2, n_chips)] * 4,
+                compiler_params=comm(5 + layer), name=f'return_{layer}')(
                     part.reshape(n_cols, seq_dev, rows, head_dim), ml.reshape(n_cols, seq_dev, head_dim))
-            attn = pl.pallas_call(
-                combine_kernel,
-                out_shape=jax.ShapeDtypeStruct((n_steps, seq_dev, heads, head_dim), BF16),
-                in_specs=[VMEM, VMEM], out_specs=VMEM, name=f'combine_{layer}')(home, home_ml)
             attn_out = attn.reshape(n_steps * seq_dev, heads * head_dim)
             hidden = (hidden.astype(F32) + jnp.dot(attn_out, w_out[layer], preferred_element_type=F32)).astype(BF16)
             if not last:

time: 357 us -> 317 us (0.89)
  Pallas kernels: 213 us -> 176 us
    pallas_call x4 -> x2, Pallas kernels: 110 us -> 71.7 us  [per_device(): pl.pallas_call(functools.partial(return_kernel, n_cols), out_shape=jax.Sh...]
    all_to_all x1 -> x0, starting transfers between devices: 9.18 us -> none  [per_device(): spread0 = lax.all_to_all(packed[0], ('kv2', 'kv'), 0, 0, tiled=True)]
    all_to_all x1 -> x2, starting transfers between devices: 2.99 us -> 8.88 us  [per_device(): spread = lax.all_to_all(moving, ('kv2', 'kv'), 0, 0, tiled=True)]
    pallas_call x2, Pallas kernels: 38.8 us -> 43.5 us  [per_device(): pl.pallas_call(functools.partial(row_gather_kernel, n_cols), out_shape=ja...]
    pallas_call x1, Pallas kernels: 18.6 us -> 14.1 us  [per_device(): pl.pallas_call(functools.partial(gather_all_kernel, n_dev, n_cols), out_s...]
    all_to_all x2, waiting for transfers between devices: 3.67 us -> 0.01 us  [deliver(): return lax.all_to_all(grouped, ('kv2', 'kv'), 0, 0, tiled=True)]
  transfers between devices with their start and end apart: 6 -> 6, of which waited for: 1 -> 1; matrix products, arithmetic and copies ran while one was open for 16% -> 18% of each run, Pallas kernels for 39% -> 33%
where the time goes in v3:
time: 317 us; the launch traced here: 315 us
  Pallas kernels  176 us (56%)
  matrix products  93.1 us (29%)
  starting transfers between devices  20.6 us (6%)
  between operations  15.1 us (5%)
  local copies, waits for them, and re-layouts  5.25 us (2%)
  other arithmetic  4.1 us (1%)
    pallas_call x2, Pallas kernels, per_device(): pl.pallas_call(functools.partial(return_kernel, n_cols), out_shape=jax.Sh...  71.7 us
    pallas_call x2, Pallas kernels, per_device(): pl.pallas_call(functools.partial(row_gather_kernel, n_cols), out_shape=ja...  43.5 us
    dot_general x2, matrix products, per_device(): jnp.dot(up_act, w_down[layer], preferred_element_type=F32)  34.5 us
    dot_general x2, matrix products, per_device(): jnp.dot(hidden, w_up[layer], preferred_element_type=F32)  33.6 us
    pallas_call x2, Pallas kernels, per_device(): pl.pallas_call(functools.partial(attend_kernel, (layer, n_slots, cap, hea...  22.5 us
    pallas_call x1, Pallas kernels, per_device(): pl.pallas_call(functools.partial(gather_all_kernel, n_dev, n_cols), out_s...  14.1 us
    all_to_all x2, starting transfers between devices, deliver(): return lax.all_to_all(grouped, ('kv2', 'kv'), 0, 0, tiled=True)  10.6 us
    dot_general x2, matrix products, per_device(): jnp.dot(hidden, w_query[layer], preferred_element_type=F32).astype(BF16)  10.2 us
  transfers between devices with their start and end apart: 6, of which 1 were waited for; matrix products, arithmetic and copies ran while one was open for 18% of the time, Pallas kernels for 33%

profile of v3, /device:TPU:97, one launch (start us, length us, event | category | flops | bytes accessed | tf_op | source)
XLA Modules:
  0.0 315.3 jit_solution(7826526917332858229)
XLA Ops:
  8.0 1.2 broadcast_subtract_fusion.src_ref
  10.5 14.1 %gather_tables.1 = s32[32,1,128]{2,1,0:T(1,128)} custom-call(s32[1,128]{1,0:T(1,128)} %pad_bitcast_fusion.x_ref), custom_call_target="tpu_custom_call" | custom-call | tf_op jit(solution)/shard_map/gather_tables/pallas_call | solution.py:474
  24.6 4.0 %pack_pages.1 = (bf16[32,16,8,128]{3,2,1,0:T(8,128)(2,1)}, bf16[32,16,8,128]{3,2,1,0:T(8,128)(2,1)}) custom-call(s32[16]{0:T(128)} %broadcast_subtract_fusion.src_ref, bf16[112,2,16,8,128]{4,3,2,1,0:T(8,128)(2,1)} %bitcast.141, bf16[112,2,16,8,128]{4,3,2,1,0:T(8,128)(2,1)} %bitcast.144), custom_call_target="tpu_custom_call" | custom-call | tf_op jit(solution)/shard_map/pack_pages/pallas_call | solution.py:465
  28.7 4.6 %all-to-all-start = ((bf16[32,16,8,128]{3,2,1,0:T(8,128)(2,1)}), bf16[32,16,8,128]{3,2,1,0:T(8,128)(2,1)S(1)}, u32[]{:S(2)}, u32[]{:S(2)}) async-start(bf16[32,16,8,128]{3,2,1,0:T(8,128)(2,1)} %get-tuple-element.51), calls=%async_computation | async-start | bytes 2097152 | tf_op jit(solution)/shard_map/all_to_all | solution.py:483
  33.3 5.1 %fusion.81 = bf16[6,8,16,128]{3,1,2,0:T(8,128)(2,1)S(1)} fusion(bf16[48,2048]{1,0:T(8,128)(2,1)} %bitcast.171, bf16[2,2048,2048]{2,1,0:T(8,128)(2,1)} %param.16), kind=kOutput, calls=%fused_computation.58 | convolution fusion | flops 402751488 | bytes 8781824 | tf_op jit(solution)/shard_map/dot_general | solution.py:521
  38.5 1.2 convolution_convert_fusion.3
  39.7 1.6 convolution_convert_fusion.2
  42.1 6.1 %places.1 = (s32[640]{0:T(1024)}, s32[224]{0:T(256)S(1)}, s32[1]{0:T(128)}) custom-call(s32[3]{0:T(128)} %pad_add_fusion.1.who_ref, s32[32,128]{1,0:T(8,128)} %bitcast.163), custom_call_target="tpu_custom_call" | custom-call | tf_op jit(solution)/shard_map/places/pallas_call | solution.py:485
  48.9 1.0 all-to-all-done
  49.9 1.0 copy-done.3
  50.8 3.1 regroup_pages_0.1
  53.9 5.3 %all-to-all-start.1 = ((bf16[32,20,8,128]{3,2,1,0:T(8,128)(2,1)}), bf16[32,20,8,128]{3,2,1,0:T(8,128)(2,1)S(1)}, u32[]{:S(2)}, u32[]{:S(2)}) async-start(bf16[32,20,8,128]{3,2,1,0:T(8,128)(2,1)} %regroup_pages_0.1), calls=%async_computation.1 | async-start | bytes 2621440 | tf_op jit(solution)/shard_map/all_to_all | solution.py:499
  59.9 8.1 %cells.1 = (s32[448]{0:T(512)}, s32[1]{0:T(128)}) custom-call(s32[3]{0:T(128)} %pad_add_fusion.1.who_ref, s32[32,128]{1,0:T(8,128)} %bitcast.164, s32[3584]{0:T(1024)} %broadcast_in_dim.7.none_ref), custom_call_target="tpu_custom_call" | custom-call | tf_op jit(solution)/shard_map/cells/pallas_call | solution.py:534
  67.9 24.1 %gather_queries_0.1 = bf16[8,24,40,128]{3,2,1,0:T(8,128)(2,1)} custom-call(bf16[24,40,128]{2,1,0:T(8,128)(2,1)} %pad_maximum_fusion.1.x_ref), custom_call_target="tpu_custom_call" | custom-call | tf_op jit(solution)/shard_map/gather_queries_0/pallas_call | solution.py:546
  92.3 4.3 %all-to-all-start.2 = ((bf16[32,16,8,128]{3,2,1,0:T(8,128)(2,1)}), bf16[32,16,8,128]{3,2,1,0:T(8,128)(2,1)S(1)}, u32[]{:S(2)}, u32[]{:S(2)}) async-start(bf16[32,16,8,128]{3,2,1,0:T(8,128)(2,1)} %get-tuple-element.64), calls=%async_computation.2 | async-start | bytes 2097152 | tf_op jit(solution)/shard_map/all_to_all | solution.py:560
  97.3 11.2 %attend_0.1 = (bf16[112,32,8,128]{3,2,1,0:T(8,128)(2,1)}, bf16[112,32,8,128]{3,2,1,0:T(8,128)(2,1)}, f32[192,32,128]{2,1,0:T(8,128)}, f32[192,128]{1,0:T(8,128)}) custom-call(s32[3]{0:T(128)} %pad_add_fusion.1.who_ref, s32[224]{0:T(256)S(1)} %get-tuple-element.65.arrive_ref, s32[1]{0:T(128)} %get-tuple-element.66.most_ref, s32[448]{0:T(512)} %get-tuple-element.67.info_ref, ...), custom_call_target="tpu_custom_call" | custom-call | tf_op jit(solution)/shard_map/attend_0/pallas_call | solution.py:562
  108.5 36.7 %return_0.1 = bf16[2,24,16,128]{3,2,1,0:T(8,128)(2,1)} custom-call(f32[8,24,32,128]{3,2,1,0:T(8,128)} %bitcast.156, f32[8,24,128]{2,1,0:T(8,128)} %bitcast.170), custom_call_target="tpu_custom_call" | custom-call | tf_op jit(solution)/shard_map/return_0/pallas_call | solution.py:575
  145.2 5.1 %fusion.51 = bf16[48,2048]{1,0:T(8,128)(2,1)S(1)} fusion(bf16[2,2048,2048]{2,1,0:T(8,128)(2,1)} %param.19, bf16[48,2048]{1,0:T(8,128)(2,1)S(1)} %bitcast.174, bf16[6,8,16,128]{3,2,1,0:T(8,128)(2,1)} %bitcast.162), kind=kOutput, calls=%fused_computation.40 | convolution fusion | flops 402948096 | bytes 8978432 | tf_op jit(solution)/shard_map/dot_general | solution.py:583
  150.3 1.0 copy-done.2
  151.2 3.1 regroup_pages_1.1
  154.3 5.3 %all-to-all-start.3 = ((bf16[32,20,8,128]{3,2,1,0:T(8,128)(2,1)}), bf16[32,20,8,128]{3,2,1,0:T(8,128)(2,1)S(1)}, u32[]{:S(2)}, u32[]{:S(2)}) async-start(bf16[32,20,8,128]{3,2,1,0:T(8,128)(2,1)} %regroup_pages_1.1), calls=%async_computation.3 | async-start | bytes 2621440 | tf_op jit(solution)/shard_map/all_to_all | solution.py:499
  159.6 16.8 %fusion.63 = bf16[48,11008]{1,0:T(8,128)(2,1)S(1)} fusion(bf16[48,2048]{1,0:T(8,128)(2,1)S(1)} %fusion.51, bf16[2,2048,11008]{2,1,0:T(8,128)(2,1)} %param.20), kind=kOutput, calls=%fused_computation.48 | convolution fusion | flops 2169016320 | bytes 46342144 | tf_op jit(solution)/shard_map/dot_general | solution.py:588
  176.4 16.9 %fusion.39 = bf16[48,2048]{1,0:T(8,128)(2,1)S(1)} fusion(bf16[48,11008]{1,0:T(8,128)(2,1)S(1)} %fusion.63, bf16[2,11008,2048]{2,1,0:T(8,128)(2,1)} %param.21, bf16[48,2048]{1,0:T(8,128)(2,1)S(1)} %fusion.51), kind=kOutput, calls=%fused_computation.36 | convolution fusion | flops 2164555776 | bytes 46538752 | tf_op jit(solution)/shard_map/dot_general | solution.py:589
  193.4 5.1 %fusion.78 = bf16[6,8,16,128]{3,1,2,0:T(8,128)(2,1)S(1)} fusion(bf16[48,2048]{1,0:T(8,128)(2,1)S(1)} %fusion.39, bf16[2,2048,2048]{2,1,0:T(8,128)(2,1)} %param.16), kind=kOutput, calls=%fused_computation.57 | convolution fusion | flops 402751488 | bytes 8781824 | tf_op jit(solution)/shard_map/dot_general | solution.py:521
  198.9 1.5 convolution_convert_fusion
  202.1 19.4 %gather_queries_1.1 = bf16[8,24,40,128]{3,2,1,0:T(8,128)(2,1)} custom-call(bf16[24,40,128]{2,1,0:T(8,128)(2,1)} %pad_maximum_fusion.2.x_ref), custom_call_target="tpu_custom_call" | custom-call | tf_op jit(solution)/shard_map/gather_queries_1/pallas_call | solution.py:546
  221.6 1.1 copy-done.4
  222.7 11.3 %attend_1.1 = (bf16[112,32,8,128]{3,2,1,0:T(8,128)(2,1)}, bf16[112,32,8,128]{3,2,1,0:T(8,128)(2,1)}, f32[192,32,128]{2,1,0:T(8,128)}, f32[192,128]{1,0:T(8,128)}) custom-call(s32[3]{0:T(128)} %pad_add_fusion.1.who_ref, s32[224]{0:T(256)S(1)} %get-tuple-element.65.arrive_ref, ...), custom_call_target="tpu_custom_call", output_to_operand_aliasing={{0}: (11, {}), {1}: (12, {})} | custom-call | tf_op jit(solution)/shard_map/attend_1/pallas_call | solution.py:562
  234.0 35.0 %return_1.1 = bf16[2,24,16,128]{3,2,1,0:T(8,128)(2,1)} custom-call(f32[8,24,32,128]{3,2,1,0:T(8,128)} %bitcast.155, f32[8,24,128]{2,1,0:T(8,128)} %bitcast.169), custom_call_target="tpu_custom_call" | custom-call | tf_op jit(solution)/shard_map/return_1/pallas_call | solution.py:575
  269.0 5.1 %fusion.48 = bf16[48,2048]{1,0:T(8,128)(2,1)S(1)} fusion(bf16[2,2048,2048]{2,1,0:T(8,128)(2,1)} %param.19, bf16[48,2048]{1,0:T(8,128)(2,1)S(1)} %fusion.39, bf16[6,8,16,128]{3,2,1,0:T(8,128)(2,1)} %bitcast.161), kind=kOutput, calls=%fused_computation.39 | convolution fusion | flops 402948096 | bytes 8978432 | tf_op jit(solution)/shard_map/dot_general | solution.py:583
  274.1 16.8 %fusion.75 = bf16[48,11008]{1,0:T(8,128)(2,1)S(1)} fusion(bf16[48,2048]{1,0:T(8,128)(2,1)S(1)} %fusion.48, bf16[2,2048,11008]{2,1,0:T(8,128)(2,1)} %param.20), kind=kOutput, calls=%fused_computation.56 | convolution fusion | flops 2169016320 | bytes 46342144 | tf_op jit(solution)/shard_map/dot_general | solution.py:588
  290.9 17.6 %fusion.36 = bf16[48,2048]{1,0:T(8,128)(2,1)} fusion(bf16[48,11008]{1,0:T(8,128)(2,1)S(1)} %fusion.75, bf16[2,11008,2048]{2,1,0:T(8,128)(2,1)} %param.21, bf16[48,2048]{1,0:T(8,128)(2,1)S(1)} %fusion.48), kind=kOutput, calls=%fused_computation.35 | convolution fusion | flops 2164555776 | bytes 46538752 | tf_op jit(solution)/shard_map/dot_general | solution.py:589
  (43 shorter events, 6.6 us)
Async XLA Ops:
  28.7 9.8 %copy-start.5 = (bf16[2,2048,256]{2,1,0:T(8,128)(2,1)S(1)}, bf16[2,2048,256]{2,1,0:T(8,128)(2,1)}, u32[]{:S(2)}) copy-start(bf16[2,2048,256]{2,1,0:T(8,128)(2,1)} %param.17) | copy-start | bytes 6291460
  28.7 21.2 %all-to-all-start = ((bf16[32,16,8,128]{3,2,1,0:T(8,128)(2,1)}), bf16[32,16,8,128]{3,2,1,0:T(8,128)(2,1)S(1)}, u32[]{:S(2)}, u32[]{:S(2)}) async-start(bf16[32,16,8,128]{3,2,1,0:T(8,128)(2,1)} %get-tuple-element.51), calls=%async_computation | async-start | bytes 2097152 | tf_op jit(solution)/shard_map/all_to_all | solution.py:483
  49.9 1.0 copy-start.3
  53.9 38.2 %all-to-all-start.1 = ((bf16[32,20,8,128]{3,2,1,0:T(8,128)(2,1)}), bf16[32,20,8,128]{3,2,1,0:T(8,128)(2,1)S(1)}, u32[]{:S(2)}, u32[]{:S(2)}) async-start(bf16[32,20,8,128]{3,2,1,0:T(8,128)(2,1)} %regroup_pages_0.1), calls=%async_computation.1 | async-start | bytes 2621440 | tf_op jit(solution)/shard_map/all_to_all | solution.py:499
  92.1 5.2 %copy-start = (bf16[32,20,8,128]{3,2,1,0:T(8,128)(2,1)}, bf16[32,20,8,128]{3,2,1,0:T(8,128)(2,1)S(1)}, u32[]{:S(2)}) copy-start(bf16[32,20,8,128]{3,2,1,0:T(8,128)(2,1)S(1)} %all-to-all-done.1.own_ref) | copy-start | bytes 3932164
  92.1 5.2 %collective-permute-start = (bf16[32,20,8,128]{3,2,1,0:T(8,128)(2,1)S(1)}, bf16[32,20,8,128]{3,2,1,0:T(8,128)(2,1)}, u32[]{:S(2)}, u32[]{:S(2)}) collective-permute-start(bf16[32,20,8,128]{3,2,1,0:T(8,128)(2,1)S(1)} %all-to-all-done.1.own_ref), channel_id=1, source_target_pairs={{0,1},{1,0},{2,3},{3,2},{4,5},{5,4},{6,7},{7,6},{8,9},{9,8},{10,11... | collective-permute-start | bytes 3932168 | tf_op jit(solution)/shard_map/ppermute | solution.py:502
  92.3 57.9 %all-to-all-start.2 = ((bf16[32,16,8,128]{3,2,1,0:T(8,128)(2,1)}), bf16[32,16,8,128]{3,2,1,0:T(8,128)(2,1)S(1)}, u32[]{:S(2)}, u32[]{:S(2)}) async-start(bf16[32,16,8,128]{3,2,1,0:T(8,128)(2,1)} %get-tuple-element.64), calls=%async_computation.2 | async-start | bytes 2097152 | tf_op jit(solution)/shard_map/all_to_all | solution.py:560
  97.3 47.9 %copy-start.7 = (bf16[2,24,2048]{2,1,0:T(8,128)(2,1)S(1)}, bf16[2,24,2048]{2,1,0:T(8,128)(2,1)}, u32[]{:S(2)}) copy-start(bf16[2,24,2048]{2,1,0:T(8,128)(2,1)} %param.15) | copy-start | bytes 589828
  150.3 1.0 copy-start.2
  154.3 46.9 %all-to-all-start.3 = ((bf16[32,20,8,128]{3,2,1,0:T(8,128)(2,1)}), bf16[32,20,8,128]{3,2,1,0:T(8,128)(2,1)S(1)}, u32[]{:S(2)}, u32[]{:S(2)}) async-start(bf16[32,20,8,128]{3,2,1,0:T(8,128)(2,1)} %regroup_pages_1.1), calls=%async_computation.3 | async-start | bytes 2621440 | tf_op jit(solution)/shard_map/all_to_all | solution.py:499
  193.4 5.2 %copy-start.6 = (bf16[2,2048,256]{2,1,0:T(8,128)(2,1)S(1)}, bf16[2,2048,256]{2,1,0:T(8,128)(2,1)}, u32[]{:S(2)}) copy-start(bf16[2,2048,256]{2,1,0:T(8,128)(2,1)} %param.17) | copy-start | bytes 6291460
  201.2 20.4 %copy-start.1 = (bf16[32,20,8,128]{3,2,1,0:T(8,128)(2,1)}, bf16[32,20,8,128]{3,2,1,0:T(8,128)(2,1)S(1)}, u32[]{:S(2)}) copy-start(bf16[32,20,8,128]{3,2,1,0:T(8,128)(2,1)S(1)} %all-to-all-done.3.own_ref) | copy-start | bytes 3932164
  201.2 20.3 %collective-permute-start.1 = (bf16[32,20,8,128]{3,2,1,0:T(8,128)(2,1)S(1)}, bf16[32,20,8,128]{3,2,1,0:T(8,128)(2,1)S(1)}, u32[]{:S(2)}, u32[]{:S(2)}) collective-permute-start(bf16[32,20,8,128]{3,2,1,0:T(8,128)(2,1)S(1)} %all-to-all-done.3.own_ref), channel_id=1, source_target_pairs={{0,1},{1,0},{2,3},{3,2},{4,5},{5,4},{6,7},{7,6},{8,9},{9,8},{10,11... | collective-permute-start | bytes 3932168 | tf_op jit(solution)/shard_map/ppermute | solution.py:502
  221.6 1.1 copy-start.4

commit v4 on v3

--- a/solution.py
+++ b/solution.py
@@ -416,6 +416,91 @@
         c.wait()
 
 
+def mlp_kernel(layer, depth, attn_ref, hid_ref, wo_ref, up_ref, dn_ref, out_ref, abuf, bbuf, x_all, u, acc, got, a_sem, b_sem, send, recv):
+    kv = lax.axis_index('kv')
+    core = kv % 2
+    mate = kv + 1 - 2 * core
+    width, tile = abuf.shape[1:]
+    n_out = width // tile
+    n_up = -(-up_ref.shape[2] // (2 * tile))
+    base = core * (up_ref.shape[2] - n_up * tile)
+    both = 2 * n_up * tile - up_ref.shape[2]
+    chunk = 256
+
+    def cols(t):
+        return pl.ds(pl.multiple_of(base + t * tile, chunk), tile)
+
+    def load_out(n):
+        return pltpu.make_async_copy(wo_ref.at[layer, :, pl.ds(n * tile, tile)], abuf.at[n % depth], a_sem.at[n % depth])
+
+    def load_up(t):
+        slot = (t + n_out) % depth
+        return pltpu.make_async_copy(up_ref.at[layer, :, cols(t)], abuf.at[slot], a_sem.at[slot])
+
+    def load_down(t):
+        slot = t % depth
+        return pltpu.make_async_copy(dn_ref.at[layer, cols(t), :], bbuf.at[slot], b_sem.at[slot])
+
+    for n in range(min(depth, n_out)):
+        load_out(n).start()
+    for t in range(depth):
+        load_down(t).start()
+    barrier = pltpu.get_barrier_semaphore()
+    pl.semaphore_signal(barrier, inc=1, device_id={'kv': mate}, device_id_type=MESH)
+    pl.semaphore_wait(barrier, 1)
+
+    def across(src, dst, i):
+        return pltpu.make_async_remote_copy(
+            src_ref=src, dst_ref=dst, send_sem=send.at[i], recv_sem=recv.at[i], device_id={'kv': mate}, device_id_type=MESH)
+
+    for n in range(n_out):
+        load_out(n).wait()
+        part = slice(n * tile, (n + 1) * tile)
+        y = jnp.dot(attn_ref[...], abuf[n % depth], preferred_element_type=F32)
+        x_all[core, :, part] = (hid_ref[:, part].astype(F32) + y).astype(BF16)
+        later = n + depth
+        if later < n_out:
+            load_out(later).start()
+        else:
+            load_up(later - n_out).start()
+    share = across(x_all.at[core], x_all.at[core], 0)
+    share.start()
+    acc[...] = jnp.zeros_like(acc)
+    share.wait_send()
+    across(x_all.at[core], x_all.at[1 - core], 0).wait_recv()
+
+    @pl.loop(0, n_up)
+    def _(t):
+        slot = (t + n_out) % depth
+        load_up(t).wait()
+        x = x_all[...].reshape(-1, width)
+        for c in range(tile // chunk):
+            part = slice(c * chunk, (c + 1) * chunk)
+            y = jax.nn.gelu(jnp.dot(x, abuf[slot, :, part], preferred_element_type=F32)).astype(BF16)
+            if c * chunk < both:
+                y = jnp.where((core == 1) & (t == 0), jnp.zeros_like(y), y)
+            u[:, part] = y
+
+        @pl.when(t + depth < n_up)
+        def _():
+            load_up(t + depth).start()
+
+        load_down(t).wait()
+        for c in range(width // tile):
+            part = slice(c * tile, (c + 1) * tile)
+            y = jnp.dot(u[...], bbuf[t % depth, :, part], preferred_element_type=F32)
+            acc[:, :, part] += y.reshape(acc.shape[0], acc.shape[1], tile)
+
+        @pl.when(t + depth < n_up)
+        def _():
+            load_down(t + depth).start()
+
+    give = across(acc.at[1 - core], got, 1)
+    give.start()
+    give.wait()
+    out_ref[...] = (x_all[core].astype(F32) + (acc[core] + got[...])).astype(BF16)
+
+
 def blank_kernel(o_ref):
     pass
 
@@ -580,13 +665,22 @@
                 compiler_params=comm(5 + layer), name=f'return_{layer}')(
                     part.reshape(n_cols, seq_dev, rows, head_dim), ml.reshape(n_cols, seq_dev, head_dim))
             attn_out = attn.reshape(n_steps * seq_dev, heads * head_dim)
-            hidden = (hidden.astype(F32) + jnp.dot(attn_out, w_out[layer], preferred_element_type=F32)).astype(BF16)
+            n_tok = n_steps * seq_dev
             if not last:
-                spread, hidden = after((spread, hidden))
-                grouped, hidden = after((regroup(spread, f'regroup_pages_{layer + 1}'), hidden))
+                spread, attn_out = after((spread, attn_out))
+                grouped, attn_out = after((regroup(spread, f'regroup_pages_{layer + 1}'), attn_out))
                 own = deliver(grouped)
-            up_act = jax.nn.gelu(jnp.dot(hidden, w_up[layer], preferred_element_type=F32)).astype(BF16)
-            hidden = (hidden.astype(F32) + jnp.dot(up_act, w_down[layer], preferred_element_type=F32)).astype(BF16)
+            depth, wide = 4, 512
+            assert w_up.shape[2] % 256 == 0 and width % wide == 0
+            hidden = pl.pallas_call(
+                functools.partial(mlp_kernel, layer, depth),
+                out_shape=jax.ShapeDtypeStruct((n_tok, width), BF16),
+                in_specs=[VMEM, VMEM, ANY, ANY, ANY], out_specs=VMEM,
+                scratch_shapes=[pltpu.VMEM((depth, width, wide), BF16), pltpu.VMEM((depth, wide, width), BF16),
+                                pltpu.VMEM((2, n_tok, width), BF16), pltpu.VMEM((2 * n_tok, wide), BF16),
+                                pltpu.VMEM((2, n_tok, width), F32), pltpu.VMEM((n_tok, width), F32),
+                                sems(depth), sems(depth), sems(2), sems(2)],
+                compiler_params=comm(7 + layer), name=f'mlp_{layer}')(attn_out, hidden, w_out, w_up, w_down)
         return hidden.reshape(x_embed.shape), k_out.reshape(k_pool.shape), v_out.reshape(v_pool.shape)
 
     return jax.shard_map(per_device, mesh=mesh, in_specs=(seq_spec, full_spec, full_spec, full_spec, full_spec, full_spec, full_spec, pool_spec, pool_spec, table_spec, vec_spec, vec_spec, vec_spec), out_specs=(seq_spec, pool_spec, pool_spec), check_vma=False)

time: 317 us -> 286 us (0.902)
  matrix products: 93.1 us -> 15 us
  Pallas kernels: 176 us -> 218 us
  local copies, waits for them, and re-layouts: 5.25 us -> 10.2 us
    dot_general x6 -> x0, matrix products: 78.3 us -> none  [the longest x2 34.5 us: per_device(): jnp.dot(up_act, w_down[layer], preferred_element_type=F32)]
    pallas_call x0 -> x2, Pallas kernels: none -> 43 us  [per_device(): pl.pallas_call(functools.partial(mlp_kernel, layer, depth), out_shape=jax...]
    unnamed x19 -> x22, local copies, waits for them, and re-layouts: 3.87 us -> 8.8 us
  transfers between devices with their start and end apart: 6 -> 6, of which waited for: 1 -> 1; matrix products, arithmetic and copies ran while one was open for 18% -> 7% of each run, Pallas kernels for 33% -> 45%
where the time goes in v4:
time: 286 us; the launch traced here: 285 us
  Pallas kernels  218 us (76%)
  starting transfers between devices  20.9 us (7%)
  between operations  15.1 us (5%)
  matrix products  15 us (5%)
  local copies, waits for them, and re-layouts  10.2 us (4%)
  other arithmetic  4.1 us (1%)
    pallas_call x2, Pallas kernels, per_device(): pl.pallas_call(functools.partial(return_kernel, n_cols), out_shape=jax.Sh...  71.1 us
    pallas_call x2, Pallas kernels, per_device(): pl.pallas_call(functools.partial(row_gather_kernel, n_cols), out_shape=ja...  43.6 us
    pallas_call x2, Pallas kernels, per_device(): pl.pallas_call(functools.partial(mlp_kernel, layer, depth), out_shape=jax...  43 us
    pallas_call x2, Pallas kernels, per_device(): pl.pallas_call(functools.partial(attend_kernel, (layer, n_slots, cap, hea...  22.1 us
    pallas_call x1, Pallas kernels, per_device(): pl.pallas_call(functools.partial(gather_all_kernel, n_dev, n_cols), out_s...  14.1 us
    all_to_all x2, starting transfers between devices, deliver(): return lax.all_to_all(grouped, ('kv2', 'kv'), 0, 0, tiled=True)  11.4 us
    dot_general x2, matrix products, per_device(): jnp.dot(hidden, w_query[layer], preferred_element_type=F32).astype(BF16)  10.1 us
    all_to_all x2, starting transfers between devices, per_device(): spread = lax.all_to_all(moving, ('kv2', 'kv'), 0, 0, tiled=True)  8.88 us
  transfers between devices with their start and end apart: 6, of which 1 were waited for; matrix products, arithmetic and copies ran while one was open for 7% of the time, Pallas kernels for 45%

profile of v4, /device:TPU:97, one launch (start us, length us, event | category | flops | bytes accessed | tf_op | source)
XLA Modules:
  0.0 284.5 jit_solution(11288106624917407846)
XLA Ops:
  8.0 1.2 broadcast_subtract_fusion.src_ref
  9.2 0.8 pad_add_fusion.1
  10.5 14.1 %gather_tables.1 = s32[32,1,128]{2,1,0:T(1,128)} custom-call(s32[1,128]{1,0:T(1,128)} %pad_bitcast_fusion.x_ref), custom_call_target="tpu_custom_call" | custom-call | tf_op jit(solution)/shard_map/gather_tables/pallas_call | solution.py:559
  24.6 4.2 %pack_pages.1 = (bf16[32,16,8,128]{3,2,1,0:T(8,128)(2,1)}, bf16[32,16,8,128]{3,2,1,0:T(8,128)(2,1)}) custom-call(s32[16]{0:T(128)} %broadcast_subtract_fusion.src_ref, bf16[112,2,16,8,128]{4,3,2,1,0:T(8,128)(2,1)} %bitcast.95, bf16[112,2,16,8,128]{4,3,2,1,0:T(8,128)(2,1)} %bitcast.98), custom_call_target="tpu_custom_call" | custom-call | tf_op jit(solution)/shard_map/pack_pages/pallas_call | solution.py:550
  28.8 4.6 %all-to-all-start = ((bf16[32,16,8,128]{3,2,1,0:T(8,128)(2,1)}), bf16[32,16,8,128]{3,2,1,0:T(8,128)(2,1)S(1)}, u32[]{:S(2)}, u32[]{:S(2)}) async-start(bf16[32,16,8,128]{3,2,1,0:T(8,128)(2,1)} %get-tuple-element.54), calls=%async_computation | async-start | bytes 2097152 | tf_op jit(solution)/shard_map/all_to_all | solution.py:568
  33.4 5.0 %fusion.15 = bf16[6,8,16,128]{3,1,2,0:T(8,128)(2,1)S(1)} fusion(bf16[48,2048]{1,0:T(8,128)(2,1)S(1)} %bitcast.121, bf16[2,2048,2048]{2,1,0:T(8,128)(2,1)} %param.16), kind=kOutput, calls=%fused_computation.14 | convolution fusion | flops 402751488 | bytes 8781824 | tf_op jit(solution)/shard_map/dot_general | solution.py:606
  38.5 1.5 convolution_convert_fusion.3
  40.0 1.5 convolution_convert_fusion.2
  42.3 6.1 %places.1 = (s32[640]{0:T(1024)}, s32[224]{0:T(256)S(1)}, s32[1]{0:T(128)}) custom-call(s32[3]{0:T(128)} %pad_add_fusion.who_ref, s32[32,128]{1,0:T(8,128)} %bitcast.124), custom_call_target="tpu_custom_call" | custom-call | tf_op jit(solution)/shard_map/places/pallas_call | solution.py:570
  49.1 0.9 all-to-all-done
  50.0 1.0 copy-done.3
  51.0 3.1 %regroup_pages_0.1 = bf16[32,20,8,128]{3,2,1,0:T(8,128)(2,1)} custom-call(s32[640]{0:T(1024)} %get-tuple-element.56.pages_ref, bf16[512,8,128]{2,1,0:T(8,128)(2,1)} %bitcast.108), custom_call_target="tpu_custom_call" | custom-call | tf_op jit(solution)/shard_map/regroup_pages_0/pallas_call | solution.py:578
  54.0 5.4 %all-to-all-start.1 = ((bf16[32,20,8,128]{3,2,1,0:T(8,128)(2,1)}), bf16[32,20,8,128]{3,2,1,0:T(8,128)(2,1)S(1)}, u32[]{:S(2)}, u32[]{:S(2)}) async-start(bf16[32,20,8,128]{3,2,1,0:T(8,128)(2,1)} %regroup_pages_0.1), calls=%async_computation.1 | async-start | bytes 2621440 | tf_op jit(solution)/shard_map/all_to_all | solution.py:584
  60.1 8.1 %cells.1 = (s32[448]{0:T(512)}, s32[1]{0:T(128)}) custom-call(s32[3]{0:T(128)} %pad_add_fusion.who_ref, s32[32,128]{1,0:T(8,128)} %bitcast.125, s32[3584]{0:T(1024)} %broadcast_in_dim.7.none_ref), custom_call_target="tpu_custom_call" | custom-call | tf_op jit(solution)/shard_map/cells/pallas_call | solution.py:619
  68.1 24.1 %gather_queries_0.1 = bf16[8,24,40,128]{3,2,1,0:T(8,128)(2,1)} custom-call(bf16[24,40,128]{2,1,0:T(8,128)(2,1)} %pad_maximum_fusion.1.x_ref), custom_call_target="tpu_custom_call" | custom-call | tf_op jit(solution)/shard_map/gather_queries_0/pallas_call | solution.py:631
  92.5 4.3 %all-to-all-start.2 = ((bf16[32,16,8,128]{3,2,1,0:T(8,128)(2,1)}), bf16[32,16,8,128]{3,2,1,0:T(8,128)(2,1)S(1)}, u32[]{:S(2)}, u32[]{:S(2)}) async-start(bf16[32,16,8,128]{3,2,1,0:T(8,128)(2,1)} %get-tuple-element.68), calls=%async_computation.2 | async-start | bytes 2097152 | tf_op jit(solution)/shard_map/all_to_all | solution.py:645
  97.5 11.0 %attend_0.1 = (bf16[112,32,8,128]{3,2,1,0:T(8,128)(2,1)}, bf16[112,32,8,128]{3,2,1,0:T(8,128)(2,1)}, f32[192,32,128]{2,1,0:T(8,128)}, f32[192,128]{1,0:T(8,128)}) custom-call(s32[3]{0:T(128)} %pad_add_fusion.who_ref, s32[224]{0:T(256)S(1)} %get-tuple-element.52.arrive_ref, s32[1]{0:T(128)} %get-tuple-element.53.most_ref, s32[448]{0:T(512)} %get-tuple-element.62.info_ref, ...), custom_call_target="tpu_custom_call" | custom-call | tf_op jit(solution)/shard_map/attend_0/pallas_call | solution.py:647
  108.5 36.5 %return_0.1 = bf16[2,24,16,128]{3,2,1,0:T(8,128)(2,1)} custom-call(f32[8,24,32,128]{3,2,1,0:T(8,128)} %bitcast.110, f32[8,24,128]{2,1,0:T(8,128)} %bitcast.131), custom_call_target="tpu_custom_call" | custom-call | tf_op jit(solution)/shard_map/return_0/pallas_call | solution.py:660
  145.0 1.7 copy.39
  146.6 1.0 copy-done.2
  147.6 3.1 %regroup_pages_1.1 = bf16[32,20,8,128]{3,2,1,0:T(8,128)(2,1)} custom-call(s32[640]{0:T(1024)} %get-tuple-element.56.pages_ref, bf16[512,8,128]{2,1,0:T(8,128)(2,1)} %bitcast.107), custom_call_target="tpu_custom_call" | custom-call | tf_op jit(solution)/shard_map/regroup_pages_1/pallas_call | solution.py:578
  150.7 6.0 %all-to-all-start.3 = ((bf16[32,20,8,128]{3,2,1,0:T(8,128)(2,1)}), bf16[32,20,8,128]{3,2,1,0:T(8,128)(2,1)S(1)}, u32[]{:S(2)}, u32[]{:S(2)}) async-start(bf16[32,20,8,128]{3,2,1,0:T(8,128)(2,1)} %regroup_pages_1.1), calls=%async_computation.3 | async-start | bytes 2621440 | tf_op jit(solution)/shard_map/all_to_all | solution.py:584
  156.7 21.8 %mlp_0.1.hid_ref = bf16[48,2048]{1,0:T(8,128)(2,1)} custom-call(bf16[48,2048]{1,0:T(8,128)(2,1)} %bitcast.111, bf16[48,2048]{1,0:T(8,128)(2,1)} %bitcast.120, bf16[2,2048,2048]{2,1,0:T(8,128)(2,1)} %wo_ref.3, bf16[2,2048,11008]{2,1,0:T(8,128)(2,1)} %up_ref.3, bf16[2,11008,2048]{2,1,0:T(8,128)(2,1)} %dn_ref.3), custom_call_target="tpu_custom_call" | custom-call | tf_op jit(solution)/shard_map/mlp_0/pallas_call | solution.py:675
  178.5 5.2 %fusion.12 = bf16[6,8,16,128]{3,1,2,0:T(8,128)(2,1)S(1)} fusion(bf16[48,2048]{1,0:T(8,128)(2,1)} %mlp_0.1.hid_ref, bf16[2,2048,2048]{2,1,0:T(8,128)(2,1)} %param.16), kind=kOutput, calls=%fused_computation.13 | convolution fusion | flops 402751488 | bytes 8781824 | tf_op jit(solution)/shard_map/dot_general | solution.py:606
  184.1 1.5 convolution_convert_fusion
  186.8 19.4 %gather_queries_1.1 = bf16[8,24,40,128]{3,2,1,0:T(8,128)(2,1)} custom-call(bf16[24,40,128]{2,1,0:T(8,128)(2,1)} %pad_maximum_fusion.2.x_ref), custom_call_target="tpu_custom_call" | custom-call | tf_op jit(solution)/shard_map/gather_queries_1/pallas_call | solution.py:631
  206.3 1.1 copy-done.4
  207.4 11.1 %attend_1.1 = (bf16[112,32,8,128]{3,2,1,0:T(8,128)(2,1)}, bf16[112,32,8,128]{3,2,1,0:T(8,128)(2,1)}, f32[192,32,128]{2,1,0:T(8,128)}, f32[192,128]{1,0:T(8,128)}) custom-call(s32[3]{0:T(128)} %pad_add_fusion.who_ref, s32[224]{0:T(256)S(1)} %get-tuple-element.52.arrive_ref, ...), custom_call_target="tpu_custom_call", output_to_operand_aliasing={{0}: (11, {}), {1}: (12, {})} | custom-call | tf_op jit(solution)/shard_map/attend_1/pallas_call | solution.py:647
  218.5 34.6 %return_1.1 = bf16[2,24,16,128]{3,2,1,0:T(8,128)(2,1)} custom-call(f32[8,24,32,128]{3,2,1,0:T(8,128)} %bitcast.109, f32[8,24,128]{2,1,0:T(8,128)} %bitcast.130), custom_call_target="tpu_custom_call" | custom-call | tf_op jit(solution)/shard_map/return_1/pallas_call | solution.py:660
  253.1 1.7 copy.38
  254.8 21.2 %mlp_1.1 = bf16[48,2048]{1,0:T(8,128)(2,1)} custom-call(bf16[48,2048]{1,0:T(8,128)(2,1)} %bitcast.113, bf16[48,2048]{1,0:T(8,128)(2,1)} %mlp_0.1.hid_ref, bf16[2,2048,2048]{2,1,0:T(8,128)(2,1)} %wo_ref.3, bf16[2,2048,11008]{2,1,0:T(8,128)(2,1)} %up_ref.3, bf16[2,11008,2048]{2,1,0:T(8,128)(2,1)} %dn_ref.3), custom_call_target="tpu_custom_call" | custom-call | tf_op jit(solution)/shard_map/mlp_1/pallas_call | solution.py:675
  276.0 1.6 copy.45
  (42 shorter events, 5.3 us)
Async XLA Ops:
  24.6 8.8 %copy-start.6 = (bf16[2,24,2048]{2,1,0:T(8,128)(2,1)S(1)}, bf16[2,24,2048]{2,1,0:T(8,128)(2,1)}, u32[]{:S(2)}) copy-start(bf16[2,24,2048]{2,1,0:T(8,128)(2,1)} %param.15) | copy-start | bytes 589828
  28.8 21.2 %all-to-all-start = ((bf16[32,16,8,128]{3,2,1,0:T(8,128)(2,1)}), bf16[32,16,8,128]{3,2,1,0:T(8,128)(2,1)S(1)}, u32[]{:S(2)}, u32[]{:S(2)}) async-start(bf16[32,16,8,128]{3,2,1,0:T(8,128)(2,1)} %get-tuple-element.54), calls=%async_computation | async-start | bytes 2097152 | tf_op jit(solution)/shard_map/all_to_all | solution.py:568
  50.0 1.0 copy-start.3
  54.0 38.2 %all-to-all-start.1 = ((bf16[32,20,8,128]{3,2,1,0:T(8,128)(2,1)}), bf16[32,20,8,128]{3,2,1,0:T(8,128)(2,1)S(1)}, u32[]{:S(2)}, u32[]{:S(2)}) async-start(bf16[32,20,8,128]{3,2,1,0:T(8,128)(2,1)} %regroup_pages_0.1), calls=%async_computation.1 | async-start | bytes 2621440 | tf_op jit(solution)/shard_map/all_to_all | solution.py:584
  92.3 5.2 %copy-start = (bf16[32,20,8,128]{3,2,1,0:T(8,128)(2,1)}, bf16[32,20,8,128]{3,2,1,0:T(8,128)(2,1)S(1)}, u32[]{:S(2)}) copy-start(bf16[32,20,8,128]{3,2,1,0:T(8,128)(2,1)S(1)} %all-to-all-done.1.own_ref) | copy-start | bytes 3932164
  92.3 5.2 %collective-permute-start = (bf16[32,20,8,128]{3,2,1,0:T(8,128)(2,1)S(1)}, bf16[32,20,8,128]{3,2,1,0:T(8,128)(2,1)}, u32[]{:S(2)}, u32[]{:S(2)}) collective-permute-start(bf16[32,20,8,128]{3,2,1,0:T(8,128)(2,1)S(1)} %all-to-all-done.1.own_ref), channel_id=1, source_target_pairs={{0,1},{1,0},{2,3},{3,2},{4,5},{5,4},{6,7},{7,6},{8,9},{9,8},{10,11... | collective-permute-start | bytes 3932168 | tf_op jit(solution)/shard_map/ppermute | solution.py:587
  92.5 54.1 %all-to-all-start.2 = ((bf16[32,16,8,128]{3,2,1,0:T(8,128)(2,1)}), bf16[32,16,8,128]{3,2,1,0:T(8,128)(2,1)S(1)}, u32[]{:S(2)}, u32[]{:S(2)}) async-start(bf16[32,16,8,128]{3,2,1,0:T(8,128)(2,1)} %get-tuple-element.68), calls=%async_computation.2 | async-start | bytes 2097152 | tf_op jit(solution)/shard_map/all_to_all | solution.py:645
  146.6 1.0 copy-start.2
  150.7 35.8 %all-to-all-start.3 = ((bf16[32,20,8,128]{3,2,1,0:T(8,128)(2,1)}), bf16[32,20,8,128]{3,2,1,0:T(8,128)(2,1)S(1)}, u32[]{:S(2)}, u32[]{:S(2)}) async-start(bf16[32,20,8,128]{3,2,1,0:T(8,128)(2,1)} %regroup_pages_1.1), calls=%async_computation.3 | async-start | bytes 2621440 | tf_op jit(solution)/shard_map/all_to_all | solution.py:584
  178.5 5.3 %copy-start.5 = (bf16[48,2048]{1,0:T(8,128)(2,1)S(1)}, bf16[48,2048]{1,0:T(8,128)(2,1)}, u32[]{:S(2)}) copy-start(bf16[48,2048]{1,0:T(8,128)(2,1)} %mlp_0.1.hid_ref) | copy-start | bytes 589828
  178.5 5.3 %copy-start.7 = (bf16[2,2048,256]{2,1,0:T(8,128)(2,1)S(1)}, bf16[2,2048,256]{2,1,0:T(8,128)(2,1)}, u32[]{:S(2)}) copy-start(bf16[2,2048,256]{2,1,0:T(8,128)(2,1)} %param.17) | copy-start | bytes 6291460
  186.4 19.8 %copy-start.1 = (bf16[32,20,8,128]{3,2,1,0:T(8,128)(2,1)}, bf16[32,20,8,128]{3,2,1,0:T(8,128)(2,1)S(1)}, u32[]{:S(2)}) copy-start(bf16[32,20,8,128]{3,2,1,0:T(8,128)(2,1)S(1)} %all-to-all-done.3.own_ref) | copy-start | bytes 3932164
  186.4 19.8 %collective-permute-start.1 = (bf16[32,20,8,128]{3,2,1,0:T(8,128)(2,1)S(1)}, bf16[32,20,8,128]{3,2,1,0:T(8,128)(2,1)S(1)}, u32[]{:S(2)}, u32[]{:S(2)}) collective-permute-start(bf16[32,20,8,128]{3,2,1,0:T(8,128)(2,1)S(1)} %all-to-all-done.3.own_ref), channel_id=1, source_target_pairs={{0,1},{1,0},{2,3},{3,2},{4,5},{5,4},{6,7},{7,6},{8,9},{9,8},{10,11... | collective-permute-start | bytes 3932168 | tf_op jit(solution)/shard_map/ppermute | solution.py:587
  206.3 1.1 copy-start.4

commit v5 on v4

--- a/solution.py
+++ b/solution.py
@@ -189,15 +189,13 @@
 
     @pl.loop(0, n_slots, unroll=8)
     def _(i):
-        arrive_ref[i] = -1
         arrive_ref[n_slots + i] = -1
 
     @pl.loop(0, n_dev * cap, unroll=8)
     def _(i):
         pages_ref[i] = 0
 
-    @pl.loop(0, n_dev)
-    def _(d):
+    def device(d, landed):
         for j in range(n_moves):
             dst = tab_ref[d, o_dst + j]
             m = d * n_moves + j
@@ -205,16 +203,16 @@
             chip = dd >> 1
             n = count[chip]
             count[chip] = n + 1
-
-            @pl.when(n < 2 * cap)
-            def _():
-                pages_ref[chip * 2 * cap + n] = m
-
-            @pl.when(dd == me)
-            def _():
-                arrive_ref[dst - base] = n
-                arrive_ref[n_slots + dst - base] = m
-
+            pages_ref[jnp.where(n < 2 * cap, chip * 2 * cap + n, n_dev * cap)] = m
+            mine = dd == me
+            s = dst - base
+            arrive_ref[jnp.where(mine, landed, 3 * n_slots)] = s
+            arrive_ref[jnp.where(mine, n_slots + s, 3 * n_slots)] = m
+            arrive_ref[jnp.where(mine, 2 * n_slots + s, 3 * n_slots)] = n
+            landed = landed + jnp.where(mine, 1, 0)
+        return landed
+
+    most_ref[1] = lax.fori_loop(0, n_dev, device, jnp.int32(0))
     most_ref[0] = lax.fori_loop(0, n_chips, lambda i, best: jnp.maximum(best, count[i]), jnp.int32(0))
 
 
@@ -225,6 +223,8 @@
     base = who_ref[0] * n_slots
     fill = pltpu.make_async_copy(none_ref, moved, sem)
     fill.start()
+
+    seen[n_cols * seq_dev] = 0
 
     @pl.loop(0, n_cols * seq_dev, unroll=8)
     def _(i):
@@ -254,23 +254,20 @@
                 mv = moved[e0]
                 s = jnp.where(mv >= 0, mv, e0) - base
 
-                @pl.when((e >= 0) & (s >= 0) & (s < n_slots))
-                def _():
-                    info_ref[n_slots + s] = b
-                    info_ref[2 * n_slots + s] = length - page * j
+                here = (e >= 0) & (s >= 0) & (s < n_slots)
+                info_ref[jnp.where(here, n_slots + s, 4 * n_slots)] = b
+                info_ref[jnp.where(here, 2 * n_slots + s, 4 * n_slots)] = length - page * j
 
     def visit(s, n):
         b = info_ref[n_slots + s]
-
-        @pl.when(b >= 0)
-        def _():
-            info_ref[n] = s
-            info_ref[3 * n_slots + s] = seen[b]
-            seen[b] = 1
-
-        return n + jnp.where(b >= 0, 1, 0)
-
-    used_ref[0] = lax.fori_loop(0, n_slots, visit, jnp.int32(0))
+        used = b >= 0
+        b = jnp.where(used, b, n_cols * seq_dev)
+        info_ref[jnp.where(used, n, 4 * n_slots)] = s
+        info_ref[3 * n_slots + s] = seen[b]
+        seen[b] = 1
+        return n + jnp.where(used, 1, 0)
+
+    used_ref[0] = lax.fori_loop(0, n_slots, visit, jnp.int32(0), unroll=4)
 
 
 def pack_kernel(n_moves, src_ref, k_ref, v_ref, *rest):
@@ -300,7 +297,7 @@
 
 def attend_kernel(dims, who_ref, arrive_ref, most_ref, info_ref, used_ref, q_ref, k_ref, v_ref, own_ref, mate_ref, slow_ref, *rest):
     layer, n_slots, cap, scale, quads, first = dims
-    ko_ref, vo_ref, o_ref, ml_ref, kbuf, vbuf, in_sem, out_sem = rest if first else rest[2:]
+    ko_ref, vo_ref, o_ref, ml_ref, kbuf, vbuf, in_sem, out_sem, arr_sem = rest if first else rest[2:]
     n_key, lanes = kbuf.shape[1] * kbuf.shape[2], kbuf.shape[3]
     n_ch = kbuf.shape[1]
     rows = o_ref.shape[1]
@@ -309,10 +306,22 @@
     bufs = (kbuf, vbuf)
     part = pl.ds(layer * n_ch, n_ch)
 
-    @pl.loop(0, n_slots)
-    def _(s):
-        n = arrive_ref[s]
-        has = n >= 0
+    slabs = [pltpu.make_async_copy((k_ref, v_ref)[a].at[:, part], bufs[a], in_sem.at[a]) for a in range(2)]
+    for c in slabs:
+        c.start()
+    o_ref[...] = jnp.zeros_like(o_ref)
+    ml_lane = lax.broadcasted_iota(jnp.int32, ml_ref.shape, 1)
+    ml_ref[...] = jnp.where(ml_lane < rows, NEG, 0.0)
+    for c in slabs:
+        c.wait()
+
+    def arrival(i, a, src):
+        return pltpu.make_async_copy(src, bufs[a].at[arrive_ref[i]], arr_sem.at[a, i])
+
+    @pl.loop(0, most_ref[1])
+    def _(i):
+        s = arrive_ref[i]
+        n = arrive_ref[2 * n_slots + s]
         half = jnp.where(n >= cap, 1, 0)
         pos = n - half * cap
 
@@ -320,19 +329,16 @@
             @pl.when(cond)
             def _():
                 for a in range(2):
-                    pltpu.make_async_copy(src_of(a), bufs[a].at[s], in_sem.at[a]).start()
-
-        fast = has & jnp.logical_not(over)
-        go(jnp.logical_not(has), lambda a: (k_ref, v_ref)[a].at[s, part])
-        go(has & over, lambda a: slow_ref.at[layer, s, pl.ds(a * n_ch, n_ch)])
-        go(fast & (half == core), lambda a: own_ref.at[pl.ds(a * n_ch, n_ch), pos])
-        go(fast & (half != core), lambda a: mate_ref.at[pl.ds(a * n_ch, n_ch), pos])
-
-    o_ref[...] = jnp.zeros_like(o_ref)
-    ml_lane = lax.broadcasted_iota(jnp.int32, ml_ref.shape, 1)
-    ml_ref[...] = jnp.where(ml_lane < rows, NEG, 0.0)
-    for a in range(2):
-        pltpu.make_async_copy((k_ref, v_ref)[a].at[:, part], bufs[a], in_sem.at[a]).wait()
+                    arrival(i, a, src_of(pl.ds(a * n_ch, n_ch))).start()
+
+        go(over, lambda some: slow_ref.at[layer, s, some])
+        go(jnp.logical_not(over) & (half == core), lambda some: own_ref.at[some, pos])
+        go(jnp.logical_not(over) & (half != core), lambda some: mate_ref.at[some, pos])
+
+    @pl.loop(0, most_ref[1])
+    def _(i):
+        for a in range(2):
+            arrival(i, a, own_ref.at[pl.ds(a * n_ch, n_ch), 0]).wait()
 
     n_used = used_ref[0]
     tile = kbuf.shape[2]
@@ -509,8 +515,8 @@
     return pltpu.SemaphoreType.DMA(shape)
 
 
-def comm(cid):
-    return pltpu.CompilerParams(collective_id=cid, has_side_effects=True)
+def comm(cid, mib=None):
+    return pltpu.CompilerParams(collective_id=cid, has_side_effects=True, **({'vmem_limit_bytes': mib << 20} if mib else {}))
 
 
 def solution(mesh):
@@ -569,8 +575,8 @@
         dims = (n_dev, n_cols, n_slots, seq_dev, n_moves, cap, page, magic, shift)
         pages, arrive, most = pl.pallas_call(
             functools.partial(places_kernel, dims),
-            out_shape=(jax.ShapeDtypeStruct((n_dev * cap,), jnp.int32), jax.ShapeDtypeStruct((2 * n_slots,), jnp.int32),
-                       jax.ShapeDtypeStruct((1,), jnp.int32)),
+            out_shape=(jax.ShapeDtypeStruct((n_dev * cap + 1,), jnp.int32), jax.ShapeDtypeStruct((3 * n_slots + 1,), jnp.int32),
+                       jax.ShapeDtypeStruct((2,), jnp.int32)),
             in_specs=[SMEM, SMEM], out_specs=(SMEM, SMEM, SMEM),
             scratch_shapes=[pltpu.SMEM((n_dev // 2,), jnp.int32)], name='places')(who, tab)
 
@@ -590,7 +596,7 @@
             found = []
             for p in packed:
                 everything = lax.all_gather(p.swapaxes(0, 1), ('kv2', 'kv'), tiled=True)
-                found.append(everything[jnp.maximum(arrive[n_slots:], 0)])
+                found.append(everything[jnp.maximum(arrive[n_slots:2 * n_slots], 0)])
             return jnp.stack(found)
 
         def no_pages():
@@ -618,9 +624,9 @@
                 own = deliver(grouped)
                 info, n_used = pl.pallas_call(
                     functools.partial(cells_kernel, dims),
-                    out_shape=(jax.ShapeDtypeStruct((4 * n_slots,), jnp.int32), jax.ShapeDtypeStruct((1,), jnp.int32)),
+                    out_shape=(jax.ShapeDtypeStruct((4 * n_slots + 1,), jnp.int32), jax.ShapeDtypeStruct((1,), jnp.int32)),
                     in_specs=[SMEM, SMEM, ANY], out_specs=(SMEM, SMEM),
-                    scratch_shapes=[pltpu.SMEM((n_dev * n_slots,), jnp.int32), pltpu.SMEM((row_seqs,), jnp.int32), pltpu.SemaphoreType.DMA],
+                    scratch_shapes=[pltpu.SMEM((n_dev * n_slots,), jnp.int32), pltpu.SMEM((row_seqs + 1,), jnp.int32), pltpu.SemaphoreType.DMA],
                     name='cells')(who, tab, jnp.full((n_dev * n_slots,), -1, jnp.int32))
                 pool_shape = jax.ShapeDtypeStruct(kp4.shape, BF16)
                 load, info = after((load, info))
@@ -633,7 +639,7 @@
                 out_shape=jax.ShapeDtypeStruct((n_cols, seq_dev, q_rows, head_dim), BF16),
                 in_specs=[VMEM], out_specs=VMEM,
                 scratch_shapes=[pltpu.SemaphoreType.DMA, sems(n_chips), sems(n_chips), sems(n_chips), sems(n_chips)],
-                compiler_params=comm(3 + layer), name=f'gather_queries_{layer}')(load)
+                compiler_params=comm(3 + layer, 40), name=f'gather_queries_{layer}')(load)
 
             first = layer == 0
             if first:
@@ -651,9 +657,9 @@
                 out_shape=[pool_shape, pool_shape, jax.ShapeDtypeStruct((row_seqs, rows, head_dim), F32),
                            jax.ShapeDtypeStruct((row_seqs, head_dim), F32)],
                 scratch_shapes=[pltpu.VMEM((n_slots, n_ch, tile, head_dim), BF16), pltpu.VMEM((n_slots, n_ch, tile, head_dim), BF16),
-                                sems(2), sems(2)],
+                                sems(2), sems(2), sems(2, n_slots)],
                 input_output_aliases={} if first else {11: 0, 12: 1},
-                name=f'attend_{layer}')(who, arrive, most, info, n_used, q_row.reshape(row_seqs, q_rows, head_dim), kp4, vp4,
+                compiler_params=pltpu.CompilerParams(vmem_limit_bytes=46 << 20), name=f'attend_{layer}')(who, arrive, most, info, n_used, q_row.reshape(row_seqs, q_rows, head_dim), kp4, vp4,
                                         own, mate, slow, *carried)
 
             parts, parts_ml = (n_chips, seq_dev, rows, head_dim), (n_chips, seq_dev, head_dim)
@@ -662,7 +668,7 @@
                 out_shape=jax.ShapeDtypeStruct((n_steps, seq_dev, heads, head_dim), BF16),
                 in_specs=[VMEM, VMEM], out_specs=VMEM,
                 scratch_shapes=[pltpu.VMEM(shape, F32) for _ in range(3) for shape in (parts, parts_ml)] + [sems(2, n_chips)] * 4,
-                compiler_params=comm(5 + layer), name=f'return_{layer}')(
+                compiler_params=comm(5 + layer, 40), name=f'return_{layer}')(
                     part.reshape(n_cols, seq_dev, rows, head_dim), ml.reshape(n_cols, seq_dev, head_dim))
             attn_out = attn.reshape(n_steps * seq_dev, heads * head_dim)
             n_tok = n_steps * seq_dev
@@ -680,7 +686,7 @@
                                 pltpu.VMEM((2, n_tok, width), BF16), pltpu.VMEM((2 * n_tok, wide), BF16),
                                 pltpu.VMEM((2, n_tok, width), F32), pltpu.VMEM((n_tok, width), F32),
                                 sems(depth), sems(depth), sems(2), sems(2)],
-                compiler_params=comm(7 + layer), name=f'mlp_{layer}')(attn_out, hidden, w_out, w_up, w_down)
+                compiler_params=comm(7 + layer, 57), name=f'mlp_{layer}')(attn_out, hidden, w_out, w_up, w_down)
         return hidden.reshape(x_embed.shape), k_out.reshape(k_pool.shape), v_out.reshape(v_pool.shape)
 
     return jax.shard_map(per_device, mesh=mesh, in_specs=(seq_spec, full_spec, full_spec, full_spec, full_spec, full_spec, full_spec, pool_spec, pool_spec, table_spec, vec_spec, vec_spec, vec_spec), out_specs=(seq_spec, pool_spec, pool_spec), check_vma=False)

time: 286 us -> 275 us (0.962)
  Pallas kernels: 218 us -> 213 us
  local copies, waits for them, and re-layouts: 10.2 us -> 6.88 us
    pallas_call x2, Pallas kernels: 43.6 us -> 40 us  [per_device(): pl.pallas_call(functools.partial(row_gather_kernel, n_cols), out_shape=ja...]
    unnamed x22 -> x20, local copies, waits for them, and re-layouts: 8.8 us -> 5.5 us
  transfers between devices with their start and end apart: 6 -> 6, of which waited for: 1 -> 1; matrix products, arithmetic and copies ran while one was open for 7% -> 6% of each run, Pallas kernels for 45% -> 45%
where the time goes in v5:
time: 275 us; the launch traced here: 274 us
  Pallas kernels  213 us (77%)
  starting transfers between devices  21 us (8%)
  matrix products  15 us (5%)
  between operations  14.5 us (5%)
  local copies, waits for them, and re-layouts  6.88 us (3%)
    pallas_call x2, Pallas kernels, per_device(): pl.pallas_call(functools.partial(return_kernel, n_cols), out_shape=jax.Sh...  70.7 us
    pallas_call x2, Pallas kernels, per_device(): pl.pallas_call(functools.partial(mlp_kernel, layer, depth), out_shape=jax...  43 us
    pallas_call x2, Pallas kernels, per_device(): pl.pallas_call(functools.partial(row_gather_kernel, n_cols), out_shape=ja...  40 us
    pallas_call x2, Pallas kernels, per_device(): pl.pallas_call(functools.partial(attend_kernel, (layer, n_slots, cap, hea...  20 us
    pallas_call x1, Pallas kernels, per_device(): pl.pallas_call(functools.partial(gather_all_kernel, n_dev, n_cols), out_s...  14.1 us
    all_to_all x2, starting transfers between devices, deliver(): return lax.all_to_all(grouped, ('kv2', 'kv'), 0, 0, tiled=True)  11.4 us
    dot_general x2, matrix products, per_device(): jnp.dot(hidden, w_query[layer], preferred_element_type=F32).astype(BF16)  10.2 us
    all_to_all x2, starting transfers between devices, per_device(): spread = lax.all_to_all(moving, ('kv2', 'kv'), 0, 0, tiled=True)  8.92 us
  transfers between devices with their start and end apart: 6, of which 1 were waited for; matrix products, arithmetic and copies ran while one was open for 6% of the time, Pallas kernels for 45%

profile of v5, /device:TPU:97, one launch (start us, length us, event | category | flops | bytes accessed | tf_op | source)
XLA Modules:
  0.0 273.9 jit_solution(2949583232410423436)
XLA Ops:
  7.2 0.8 copy.25
  8.0 1.2 broadcast_subtract_fusion.src_ref
  9.3 0.8 pad_add_fusion.1
  10.5 14.1 %gather_tables.1 = s32[32,1,128]{2,1,0:T(1,128)} custom-call(s32[1,128]{1,0:T(1,128)} %pad_bitcast_fusion.x_ref), custom_call_target="tpu_custom_call" | custom-call | tf_op jit(solution)/shard_map/gather_tables/pallas_call | solution.py:565
  24.6 4.1 %pack_pages.1 = (bf16[32,16,8,128]{3,2,1,0:T(8,128)(2,1)}, bf16[32,16,8,128]{3,2,1,0:T(8,128)(2,1)}) custom-call(s32[16]{0:T(128)} %broadcast_subtract_fusion.src_ref, bf16[112,2,16,8,128]{4,3,2,1,0:T(8,128)(2,1)} %bitcast.105, bf16[112,2,16,8,128]{4,3,2,1,0:T(8,128)(2,1)} %bitcast.108), custom_call_target="tpu_custom_call" | custom-call | tf_op jit(solution)/shard_map/pack_pages/pallas_call | solution.py:556
  28.8 4.6 %all-to-all-start = ((bf16[32,16,8,128]{3,2,1,0:T(8,128)(2,1)}), bf16[32,16,8,128]{3,2,1,0:T(8,128)(2,1)S(1)}, u32[]{:S(2)}, u32[]{:S(2)}) async-start(bf16[32,16,8,128]{3,2,1,0:T(8,128)(2,1)} %get-tuple-element.54), calls=%async_computation | async-start | bytes 2097152 | tf_op jit(solution)/shard_map/all_to_all | solution.py:574
  33.4 5.0 %fusion.15 = bf16[6,8,16,128]{3,1,2,0:T(8,128)(2,1)S(1)} fusion(bf16[48,2048]{1,0:T(8,128)(2,1)S(1)} %bitcast.125, bf16[2,2048,2048]{2,1,0:T(8,128)(2,1)} %param.16), kind=kOutput, calls=%fused_computation.14 | convolution fusion | flops 402751488 | bytes 8781824 | tf_op jit(solution)/shard_map/dot_general | solution.py:612
  38.5 1.5 convolution_convert_fusion.3
  40.0 1.5 convolution_convert_fusion.2
  41.6 0.6 pad_add_fusion.who_ref
  42.2 7.4 %places.1 = (s32[641]{0:T(1024)}, s32[337]{0:T(512)S(1)}, s32[2]{0:T(128)}) custom-call(s32[3]{0:T(128)} %pad_add_fusion.who_ref, s32[32,128]{1,0:T(8,128)} %bitcast.128), custom_call_target="tpu_custom_call" | custom-call | tf_op jit(solution)/shard_map/places/pallas_call | solution.py:576
  50.0 1.0 copy-done.3
  50.9 3.1 %regroup_pages_0.1 = bf16[32,20,8,128]{3,2,1,0:T(8,128)(2,1)} custom-call(s32[641]{0:T(1024)} %get-tuple-element.56.pages_ref, bf16[512,8,128]{2,1,0:T(8,128)(2,1)} %bitcast.116), custom_call_target="tpu_custom_call" | custom-call | tf_op jit(solution)/shard_map/regroup_pages_0/pallas_call | solution.py:584
  54.0 6.0 %all-to-all-start.1 = ((bf16[32,20,8,128]{3,2,1,0:T(8,128)(2,1)}), bf16[32,20,8,128]{3,2,1,0:T(8,128)(2,1)S(1)}, u32[]{:S(2)}, u32[]{:S(2)}) async-start(bf16[32,20,8,128]{3,2,1,0:T(8,128)(2,1)} %regroup_pages_0.1), calls=%async_computation.1 | async-start | bytes 2621440 | tf_op jit(solution)/shard_map/all_to_all | solution.py:590
  60.0 0.6 broadcast_in_dim.7.none_ref
  60.6 8.0 %cells.1 = (s32[449]{0:T(512)}, s32[1]{0:T(128)}) custom-call(s32[3]{0:T(128)} %pad_add_fusion.who_ref, s32[32,128]{1,0:T(8,128)} %bitcast.129, s32[3584]{0:T(1024)} %broadcast_in_dim.7.none_ref), custom_call_target="tpu_custom_call" | custom-call | tf_op jit(solution)/shard_map/cells/pallas_call | solution.py:625
  68.6 22.9 %gather_queries_0.1 = bf16[8,24,40,128]{3,2,1,0:T(8,128)(2,1)S(1)} custom-call(bf16[24,40,128]{2,1,0:T(8,128)(2,1)S(1)} %pad_maximum_fusion.1.x_ref), custom_call_target="tpu_custom_call" | custom-call | tf_op jit(solution)/shard_map/gather_queries_0/pallas_call | solution.py:637
  91.8 4.3 %all-to-all-start.2 = ((bf16[32,16,8,128]{3,2,1,0:T(8,128)(2,1)}), bf16[32,16,8,128]{3,2,1,0:T(8,128)(2,1)}, u32[]{:S(2)}, u32[]{:S(2)}) async-start(bf16[32,16,8,128]{3,2,1,0:T(8,128)(2,1)} %get-tuple-element.68), calls=%async_computation.2 | async-start | bytes 2097152 | tf_op jit(solution)/shard_map/all_to_all | solution.py:651
  96.8 10.0 %attend_0.1 = (bf16[112,32,8,128]{3,2,1,0:T(8,128)(2,1)}, bf16[112,32,8,128]{3,2,1,0:T(8,128)(2,1)}, f32[192,32,128]{2,1,0:T(8,128)S(1)}, f32[192,128]{1,0:T(8,128)S(1)}) custom-call(s32[3]{0:T(128)S(1)} %copy-done, s32[337]{0:T(512)S(1)} %get-tuple-element.52.arrive_ref, s32[2]{0:T(128)S(1)} %copy-done.2, s32[449]{0:T(512)S(1)} %copy-done.1, ...), custom_call_target="tpu_custom_call" | custom-call | tf_op jit(solution)/shard_map/attend_0/pallas_call | solution.py:653
  106.8 36.1 %return_0.1 = bf16[2,24,16,128]{3,2,1,0:T(8,128)(2,1)S(1)} custom-call(f32[8,24,32,128]{3,2,1,0:T(8,128)S(1)} %bitcast.99, f32[8,24,128]{2,1,0:T(8,128)S(1)} %bitcast.103), custom_call_target="tpu_custom_call" | custom-call | tf_op jit(solution)/shard_map/return_0/pallas_call | solution.py:666
  142.9 0.7 copy.39
  143.6 3.1 %regroup_pages_1.1 = bf16[32,20,8,128]{3,2,1,0:T(8,128)(2,1)} custom-call(s32[641]{0:T(1024)} %get-tuple-element.56.pages_ref, bf16[512,8,128]{2,1,0:T(8,128)(2,1)} %bitcast.28.x_ref), custom_call_target="tpu_custom_call" | custom-call | tf_op jit(solution)/shard_map/regroup_pages_1/pallas_call | solution.py:584
  146.7 5.4 %all-to-all-start.3 = ((bf16[32,20,8,128]{3,2,1,0:T(8,128)(2,1)}), bf16[32,20,8,128]{3,2,1,0:T(8,128)(2,1)S(1)}, u32[]{:S(2)}, u32[]{:S(2)}) async-start(bf16[32,20,8,128]{3,2,1,0:T(8,128)(2,1)} %regroup_pages_1.1), calls=%async_computation.3 | async-start | bytes 2621440 | tf_op jit(solution)/shard_map/all_to_all | solution.py:590
  152.1 21.8 %mlp_0.1.hid_ref = bf16[48,2048]{1,0:T(8,128)(2,1)} custom-call(bf16[48,2048]{1,0:T(8,128)(2,1)} %bitcast.117, bf16[48,2048]{1,0:T(8,128)(2,1)} %bitcast.124, bf16[2,2048,2048]{2,1,0:T(8,128)(2,1)} %wo_ref.3, bf16[2,2048,11008]{2,1,0:T(8,128)(2,1)} %up_ref.3, bf16[2,11008,2048]{2,1,0:T(8,128)(2,1)} %dn_ref.3), custom_call_target="tpu_custom_call" | custom-call | tf_op jit(solution)/shard_map/mlp_0/pallas_call | solution.py:681
  173.9 5.2 %fusion.12 = bf16[6,8,16,128]{3,1,2,0:T(8,128)(2,1)S(1)} fusion(bf16[48,2048]{1,0:T(8,128)(2,1)} %mlp_0.1.hid_ref, bf16[2,2048,2048]{2,1,0:T(8,128)(2,1)} %param.16), kind=kOutput, calls=%fused_computation.13 | convolution fusion | flops 402751488 | bytes 8781824 | tf_op jit(solution)/shard_map/dot_general | solution.py:612
  179.6 1.5 convolution_convert_fusion
  181.7 17.1 %gather_queries_1.1 = bf16[8,24,40,128]{3,2,1,0:T(8,128)(2,1)S(1)} custom-call(bf16[24,40,128]{2,1,0:T(8,128)(2,1)S(1)} %pad_maximum_fusion.2.x_ref), custom_call_target="tpu_custom_call" | custom-call | tf_op jit(solution)/shard_map/gather_queries_1/pallas_call | solution.py:637
  198.8 10.0 %attend_1.1 = (bf16[112,32,8,128]{3,2,1,0:T(8,128)(2,1)}, bf16[112,32,8,128]{3,2,1,0:T(8,128)(2,1)}, f32[192,32,128]{2,1,0:T(8,128)S(1)}, f32[192,128]{1,0:T(8,128)S(1)}) custom-call(s32[3]{0:T(128)S(1)} %copy-done, s32[337]{0:T(512)S(1)} %get-tuple-element.52.arrive_ref, s32[2]{0:T(128)S(1)} %copy-done.2, ...), custom_call_target="tpu_custom_call", output_to_operand_aliasing={{0}: (11, {}), {1}: (12, {})} | custom-call | tf_op jit(solution)/shard_map/attend_1/pallas_call | solution.py:653
  208.9 34.6 %return_1.1 = bf16[2,24,16,128]{3,2,1,0:T(8,128)(2,1)S(1)} custom-call(f32[8,24,32,128]{3,2,1,0:T(8,128)S(1)} %bitcast.98, f32[8,24,128]{2,1,0:T(8,128)S(1)} %bitcast.102), custom_call_target="tpu_custom_call" | custom-call | tf_op jit(solution)/shard_map/return_1/pallas_call | solution.py:666
  243.4 0.7 copy.38
  244.2 21.3 %mlp_1.1 = bf16[48,2048]{1,0:T(8,128)(2,1)} custom-call(bf16[48,2048]{1,0:T(8,128)(2,1)} %bitcast.119, bf16[48,2048]{1,0:T(8,128)(2,1)} %mlp_0.1.hid_ref, bf16[2,2048,2048]{2,1,0:T(8,128)(2,1)} %wo_ref.3, bf16[2,2048,11008]{2,1,0:T(8,128)(2,1)} %up_ref.3, bf16[2,11008,2048]{2,1,0:T(8,128)(2,1)} %dn_ref.3), custom_call_target="tpu_custom_call" | custom-call | tf_op jit(solution)/shard_map/mlp_1/pallas_call | solution.py:681
  265.4 1.6 copy.45
  (40 shorter events, 2.9 us)
Async XLA Ops:
  24.6 8.8 %copy-start.5 = (bf16[2,24,2048]{2,1,0:T(8,128)(2,1)S(1)}, bf16[2,24,2048]{2,1,0:T(8,128)(2,1)}, u32[]{:S(2)}) copy-start(bf16[2,24,2048]{2,1,0:T(8,128)(2,1)} %param.15) | copy-start | bytes 589828
  28.8 21.2 %all-to-all-start = ((bf16[32,16,8,128]{3,2,1,0:T(8,128)(2,1)}), bf16[32,16,8,128]{3,2,1,0:T(8,128)(2,1)S(1)}, u32[]{:S(2)}, u32[]{:S(2)}) async-start(bf16[32,16,8,128]{3,2,1,0:T(8,128)(2,1)} %get-tuple-element.54), calls=%async_computation | async-start | bytes 2097152 | tf_op jit(solution)/shard_map/all_to_all | solution.py:574
  49.6 46.5 %copy-start.2 = (s32[2]{0:T(128)S(1)}, s32[2]{0:T(128)}, u32[]{:S(2)}) copy-start(s32[2]{0:T(128)} %get-tuple-element.53.most_ref) | copy-start | bytes 28
  50.0 1.0 copy-start.3
  54.0 37.5 %all-to-all-start.1 = ((bf16[32,20,8,128]{3,2,1,0:T(8,128)(2,1)}), bf16[32,20,8,128]{3,2,1,0:T(8,128)(2,1)S(1)}, u32[]{:S(2)}, u32[]{:S(2)}) async-start(bf16[32,20,8,128]{3,2,1,0:T(8,128)(2,1)} %regroup_pages_0.1), calls=%async_computation.1 | async-start | bytes 2621440 | tf_op jit(solution)/shard_map/all_to_all | solution.py:590
  91.5 4.6 %collective-permute-start = (bf16[32,20,8,128]{3,2,1,0:T(8,128)(2,1)S(1)}, bf16[32,20,8,128]{3,2,1,0:T(8,128)(2,1)}, u32[]{:S(2)}, u32[]{:S(2)}) collective-permute-start(bf16[32,20,8,128]{3,2,1,0:T(8,128)(2,1)S(1)} %all-to-all-done.1.own_ref), channel_id=1, source_target_pairs={{0,1},{1,0},{2,3},{3,2},{4,5},{5,4},{6,7},{7,6},{8,9},{9,8},{10,11... | collective-permute-start | bytes 3932168 | tf_op jit(solution)/shard_map/ppermute | solution.py:593
  91.8 51.9 %all-to-all-start.2 = ((bf16[32,16,8,128]{3,2,1,0:T(8,128)(2,1)}), bf16[32,16,8,128]{3,2,1,0:T(8,128)(2,1)}, u32[]{:S(2)}, u32[]{:S(2)}) async-start(bf16[32,16,8,128]{3,2,1,0:T(8,128)(2,1)} %get-tuple-element.68), calls=%async_computation.2 | async-start | bytes 2097152 | tf_op jit(solution)/shard_map/all_to_all | solution.py:651
  96.1 0.6 copy-start
  96.1 0.7 copy-start.1
  146.7 34.4 %all-to-all-start.3 = ((bf16[32,20,8,128]{3,2,1,0:T(8,128)(2,1)}), bf16[32,20,8,128]{3,2,1,0:T(8,128)(2,1)S(1)}, u32[]{:S(2)}, u32[]{:S(2)}) async-start(bf16[32,20,8,128]{3,2,1,0:T(8,128)(2,1)} %regroup_pages_1.1), calls=%async_computation.3 | async-start | bytes 2621440 | tf_op jit(solution)/shard_map/all_to_all | solution.py:590
  173.9 5.3 %copy-start.4 = (bf16[48,2048]{1,0:T(8,128)(2,1)S(1)}, bf16[48,2048]{1,0:T(8,128)(2,1)}, u32[]{:S(2)}) copy-start(bf16[48,2048]{1,0:T(8,128)(2,1)} %mlp_0.1.hid_ref) | copy-start | bytes 589828
  173.9 5.3 %copy-start.6 = (bf16[2,2048,256]{2,1,0:T(8,128)(2,1)S(1)}, bf16[2,2048,256]{2,1,0:T(8,128)(2,1)}, u32[]{:S(2)}) copy-start(bf16[2,2048,256]{2,1,0:T(8,128)(2,1)} %param.17) | copy-start | bytes 6291460
  181.2 17.6 %collective-permute-start.1 = (bf16[32,20,8,128]{3,2,1,0:T(8,128)(2,1)S(1)}, bf16[32,20,8,128]{3,2,1,0:T(8,128)(2,1)S(1)}, u32[]{:S(2)}, u32[]{:S(2)}) collective-permute-start(bf16[32,20,8,128]{3,2,1,0:T(8,128)(2,1)S(1)} %all-to-all-done.3.own_ref), channel_id=1, source_target_pairs={{0,1},{1,0},{2,3},{3,2},{4,5},{5,4},{6,7},{7,6},{8,9},{9,8},{10,11... | collective-permute-start | bytes 3932168 | tf_op jit(solution)/shard_map/ppermute | solution.py:593

commit v6 on v5

--- a/solution.py
+++ b/solution.py
@@ -422,7 +422,13 @@
         c.wait()
 
 
-def mlp_kernel(layer, depth, attn_ref, hid_ref, wo_ref, up_ref, dn_ref, out_ref, abuf, bbuf, x_all, u, acc, got, a_sem, b_sem, send, recv):
+def mlp_kernel(layer, depth, more, attn_ref, hid_ref, wo_ref, up_ref, dn_ref, *rest):
+    if more:
+        wq_ref, wk_ref, wv_ref, out_ref, q_ref, k_ref, v_ref, abuf, bbuf, x_all, u, acc, got, a_sem, b_sem, send, recv, kvbuf, kv_sem = rest
+        n_query = wq_ref.shape[2] // abuf.shape[2]
+    else:
+        out_ref, abuf, bbuf, x_all, u, acc, got, a_sem, b_sem, send, recv = rest
+        n_query = 0
     kv = lax.axis_index('kv')
     core = kv % 2
     mate = kv + 1 - 2 * core
@@ -442,6 +448,13 @@
     def load_up(t):
         slot = (t + n_out) % depth
         return pltpu.make_async_copy(up_ref.at[layer, :, cols(t)], abuf.at[slot], a_sem.at[slot])
+
+    def load_query(j):
+        slot = (j + n_out + n_up) % depth
+        return pltpu.make_async_copy(wq_ref.at[layer + 1, :, pl.ds(pl.multiple_of(j * tile, tile), tile)], abuf.at[slot], a_sem.at[slot])
+
+    def load_kv(i):
+        return pltpu.make_async_copy((wk_ref, wv_ref)[i].at[layer + 1], kvbuf.at[i], kv_sem.at[i])
 
     def load_down(t):
         slot = t % depth
@@ -469,6 +482,9 @@
             load_out(later).start()
         else:
             load_up(later - n_out).start()
+    if more:
+        for i in range(2):
+            load_kv(i).start()
     share = across(x_all.at[core], x_all.at[core], 0)
     share.start()
     acc[...] = jnp.zeros_like(acc)
@@ -491,6 +507,11 @@
         def _():
             load_up(t + depth).start()
 
+        if more:
+            @pl.when((t + depth >= n_up) & (t + depth < n_up + n_query))
+            def _():
+                load_query(t + depth - n_up).start()
+
         load_down(t).wait()
         for c in range(width // tile):
             part = slice(c * tile, (c + 1) * tile)
@@ -504,7 +525,15 @@
     give = across(acc.at[1 - core], got, 1)
     give.start()
     give.wait()
-    out_ref[...] = (x_all[core].astype(F32) + (acc[core] + got[...])).astype(BF16)
+    h = (x_all[core].astype(F32) + (acc[core] + got[...])).astype(BF16)
+    out_ref[...] = h
+    for j in range(n_query):
+        load_query(j).wait()
+        q_ref[:, j * tile:(j + 1) * tile] = jnp.dot(h, abuf[(j + n_out + n_up) % depth], preferred_element_type=F32).astype(BF16)
+    if more:
+        for i, o in enumerate((k_ref, v_ref)):
+            load_kv(i).wait()
+            o[...] = jnp.dot(h, kvbuf[i], preferred_element_type=F32).astype(BF16)
 
 
 def blank_kernel(o_ref):
@@ -584,7 +613,7 @@
             return pl.pallas_call(
                 functools.partial(regroup_kernel, cap),
                 out_shape=jax.ShapeDtypeStruct((n_dev, cap, tile, head_dim), BF16),
-                in_specs=[SMEM, VMEM], out_specs=VMEM, name=name)(pages, spread.reshape(n_dev * n_moves, tile, head_dim))
+                in_specs=[SMEM, VMEM], out_specs=VMEM, compiler_params=pltpu.CompilerParams(vmem_limit_bytes=46 << 20), name=name)(pages, spread.reshape(n_dev * n_moves, tile, head_dim))
 
         def deliver(grouped):
             return lax.all_to_all(grouped, ('kv2', 'kv'), 0, 0, tiled=True)
@@ -609,9 +638,8 @@
         hidden = x_embed.reshape(n_steps * seq_dev, width)
         k_out = v_out = None
         for layer in range(layers):
-            query = jnp.dot(hidden, w_query[layer], preferred_element_type=F32).astype(BF16)
-            k_new = jnp.dot(hidden, w_key[layer], preferred_element_type=F32).astype(BF16)
-            v_new = jnp.dot(hidden, w_value[layer], preferred_element_type=F32).astype(BF16)
+            if layer == 0:
+                query, k_new, v_new = (jnp.dot(hidden, w[layer], preferred_element_type=F32).astype(BF16) for w in (w_query, w_key, w_value))
 
             def by_seq(x):
                 return x.reshape(n_steps, seq_dev, -1, head_dim).swapaxes(0, 1).reshape(seq_dev, -1, head_dim)
@@ -678,15 +706,22 @@
                 own = deliver(grouped)
             depth, wide = 4, 512
             assert w_up.shape[2] % 256 == 0 and width % wide == 0
-            hidden = pl.pallas_call(
-                functools.partial(mlp_kernel, layer, depth),
-                out_shape=jax.ShapeDtypeStruct((n_tok, width), BF16),
-                in_specs=[VMEM, VMEM, ANY, ANY, ANY], out_specs=VMEM,
+            kv_width = w_key.shape[2]
+            extra = () if last else (w_query, w_key, w_value)
+            assert w_query.shape[2] // wide == depth
+            hidden, *proj = pl.pallas_call(
+                functools.partial(mlp_kernel, layer, depth, not last),
+                out_shape=[jax.ShapeDtypeStruct((n_tok, n), BF16)
+                           for n in ((width,) if last else (width, w_query.shape[2], kv_width, kv_width))],
+                in_specs=[VMEM, VMEM, ANY, ANY, ANY] + [ANY] * len(extra), out_specs=[VMEM] * (1 if last else 4),
                 scratch_shapes=[pltpu.VMEM((depth, width, wide), BF16), pltpu.VMEM((depth, wide, width), BF16),
                                 pltpu.VMEM((2, n_tok, width), BF16), pltpu.VMEM((2 * n_tok, wide), BF16),
                                 pltpu.VMEM((2, n_tok, width), F32), pltpu.VMEM((n_tok, width), F32),
-                                sems(depth), sems(depth), sems(2), sems(2)],
-                compiler_params=comm(7 + layer, 57), name=f'mlp_{layer}')(attn_out, hidden, w_out, w_up, w_down)
+                                sems(depth), sems(depth), sems(2), sems(2)]
+                               + ([] if last else [pltpu.VMEM((2, width, kv_width), BF16), sems(2)]),
+                compiler_params=comm(7 + layer, 52), name=f'mlp_{layer}')(attn_out, hidden, w_out, w_up, w_down, *extra)
+            if not last:
+                query, k_new, v_new = proj
         return hidden.reshape(x_embed.shape), k_out.reshape(k_pool.shape), v_out.reshape(v_pool.shape)
 
     return jax.shard_map(per_device, mesh=mesh, in_specs=(seq_spec, full_spec, full_spec, full_spec, full_spec, full_spec, full_spec, pool_spec, pool_spec, table_spec, vec_spec, vec_spec, vec_spec), out_specs=(seq_spec, pool_spec, pool_spec), check_vma=False)

time: 275 us -> 265 us (0.964)
  matrix products: 15 us -> 6.76 us
    dot_general x6 -> x3, matrix products: 15 us -> 6.76 us  [per_device(): jnp.dot(hidden, w[layer], preferred_element_type=F32).astype(BF16)]
    unnamed x20 -> x22, local copies, waits for them, and re-layouts: 5.5 us -> 2.91 us
  transfers between devices with their start and end apart: 6 -> 6, of which waited for: 1 -> 0; matrix products, arithmetic and copies ran while one was open for 6% -> 4% of each run, Pallas kernels for 45% -> 47%
where the time goes in v6:
time: 265 us; the launch traced here: 264 us
  Pallas kernels  213 us (80%)
  starting transfers between devices  20.6 us (8%)
  between operations  14.5 us (5%)
  matrix products  6.76 us (3%)
  local copies, waits for them, and re-layouts  5.58 us (2%)
  other arithmetic  3.62 us (1%)
    pallas_call x2, Pallas kernels, per_device(): pl.pallas_call(functools.partial(return_kernel, n_cols), out_shape=jax.Sh...  71 us
    pallas_call x2, Pallas kernels, per_device(): pl.pallas_call(functools.partial(mlp_kernel, layer, depth, not last), out...  42.7 us
    pallas_call x2, Pallas kernels, per_device(): pl.pallas_call(functools.partial(row_gather_kernel, n_cols), out_shape=ja...  40 us
    pallas_call x2, Pallas kernels, per_device(): pl.pallas_call(functools.partial(attend_kernel, (layer, n_slots, cap, hea...  20 us
    pallas_call x1, Pallas kernels, per_device(): pl.pallas_call(functools.partial(gather_all_kernel, n_dev, n_cols), out_s...  14.1 us
    all_to_all x2, starting transfers between devices, deliver(): return lax.all_to_all(grouped, ('kv2', 'kv'), 0, 0, tiled=True)  11.3 us
    all_to_all x2, starting transfers between devices, per_device(): spread = lax.all_to_all(moving, ('kv2', 'kv'), 0, 0, tiled=True)  8.92 us
    pallas_call x1, Pallas kernels, per_device(): pl.pallas_call(functools.partial(cells_kernel, dims), out_shape=(jax.Shap...  7.99 us
  transfers between devices with their start and end apart: 6, of which 0 were waited for; matrix products, arithmetic and copies ran while one was open for 4% of the time, Pallas kernels for 47%

profile of v6, /device:TPU:97, one launch (start us, length us, event | category | flops | bytes accessed | tf_op | source)
XLA Modules:
  0.0 263.9 jit_solution(2736933204994457394)
XLA Ops:
  7.2 0.8 copy.25
  8.0 1.2 broadcast_subtract_fusion.src_ref
  9.2 0.8 pad_add_fusion.1
  10.0 0.5 pad_bitcast_fusion.x_ref
  10.5 14.1 %gather_tables.1 = s32[32,1,128]{2,1,0:T(1,128)} custom-call(s32[1,128]{1,0:T(1,128)} %pad_bitcast_fusion.x_ref), custom_call_target="tpu_custom_call" | custom-call | tf_op jit(solution)/shard_map/gather_tables/pallas_call | solution.py:594
  24.6 4.1 %pack_pages.1 = (bf16[32,16,8,128]{3,2,1,0:T(8,128)(2,1)}, bf16[32,16,8,128]{3,2,1,0:T(8,128)(2,1)}) custom-call(s32[16]{0:T(128)} %broadcast_subtract_fusion.src_ref, bf16[112,2,16,8,128]{4,3,2,1,0:T(8,128)(2,1)} %bitcast.97, bf16[112,2,16,8,128]{4,3,2,1,0:T(8,128)(2,1)} %bitcast.100), custom_call_target="tpu_custom_call" | custom-call | tf_op jit(solution)/shard_map/pack_pages/pallas_call | solution.py:585
  28.8 4.6 %all-to-all-start = ((bf16[32,16,8,128]{3,2,1,0:T(8,128)(2,1)}), bf16[32,16,8,128]{3,2,1,0:T(8,128)(2,1)S(1)}, u32[]{:S(2)}, u32[]{:S(2)}) async-start(bf16[32,16,8,128]{3,2,1,0:T(8,128)(2,1)} %get-tuple-element.58), calls=%async_computation | async-start | bytes 2097152 | tf_op jit(solution)/shard_map/all_to_all | solution.py:603
  33.4 5.0 %fusion.6 = bf16[6,8,16,128]{3,1,2,0:T(8,128)(2,1)S(1)} fusion(bf16[48,2048]{1,0:T(8,128)(2,1)S(1)} %bitcast.89, bf16[2,2048,2048]{2,1,0:T(8,128)(2,1)} %rest_0_.1), kind=kOutput, calls=%fused_computation.9 | convolution fusion | flops 402751488 | bytes 8781824 | tf_op jit(solution)/shard_map/dot_general | solution.py:642
  38.4 0.7 copy.26
  39.1 1.5 convolution_convert_fusion.1
  40.6 0.6 copy.27
  41.6 0.7 pad_add_fusion.who_ref
  42.3 7.4 %places.1 = (s32[641]{0:T(1024)}, s32[337]{0:T(512)S(1)}, s32[2]{0:T(128)}) custom-call(s32[3]{0:T(128)} %pad_add_fusion.who_ref, s32[32,128]{1,0:T(8,128)} %bitcast.112), custom_call_target="tpu_custom_call" | custom-call | tf_op jit(solution)/shard_map/places/pallas_call | solution.py:605
  49.7 1.0 pad_maximum_fusion.1.x_ref
  50.7 0.7 copy-done.2
  51.3 2.4 regroup_pages_0.1
  53.8 6.3 %all-to-all-start.1 = ((bf16[32,20,8,128]{3,2,1,0:T(8,128)(2,1)}), bf16[32,20,8,128]{3,2,1,0:T(8,128)(2,1)S(1)}, u32[]{:S(2)}, u32[]{:S(2)}) async-start(bf16[32,20,8,128]{3,2,1,0:T(8,128)(2,1)} %regroup_pages_0.1), calls=%async_computation.1 | async-start | bytes 2621440 | tf_op jit(solution)/shard_map/all_to_all | solution.py:619
  60.1 0.6 broadcast_in_dim.7.none_ref
  60.7 8.0 %cells.1 = (s32[449]{0:T(512)}, s32[1]{0:T(128)}) custom-call(s32[3]{0:T(128)} %pad_add_fusion.who_ref, s32[32,128]{1,0:T(8,128)} %bitcast.113, s32[3584]{0:T(1024)} %broadcast_in_dim.7.none_ref), custom_call_target="tpu_custom_call" | custom-call | tf_op jit(solution)/shard_map/cells/pallas_call | solution.py:653
  68.7 22.9 %gather_queries_0.1 = bf16[8,24,40,128]{3,2,1,0:T(8,128)(2,1)S(1)} custom-call(bf16[24,40,128]{2,1,0:T(8,128)(2,1)S(1)} %pad_maximum_fusion.1.x_ref), custom_call_target="tpu_custom_call" | custom-call | tf_op jit(solution)/shard_map/gather_queries_0/pallas_call | solution.py:665
  91.8 4.3 %all-to-all-start.2 = ((bf16[32,16,8,128]{3,2,1,0:T(8,128)(2,1)}), bf16[32,16,8,128]{3,2,1,0:T(8,128)(2,1)}, u32[]{:S(2)}, u32[]{:S(2)}) async-start(bf16[32,16,8,128]{3,2,1,0:T(8,128)(2,1)} %get-tuple-element.72), calls=%async_computation.2 | async-start | bytes 2097152 | tf_op jit(solution)/shard_map/all_to_all | solution.py:679
  96.3 0.6 copy-done.4
  96.9 10.0 %attend_0.1 = (bf16[112,32,8,128]{3,2,1,0:T(8,128)(2,1)}, bf16[112,32,8,128]{3,2,1,0:T(8,128)(2,1)}, f32[192,32,128]{2,1,0:T(8,128)S(1)}, f32[192,128]{1,0:T(8,128)S(1)}) custom-call(s32[3]{0:T(128)S(1)} %copy-done.4, s32[337]{0:T(512)S(1)} %get-tuple-element.56.arrive_ref, s32[2]{0:T(128)S(1)} %copy-done.6, s32[449]{0:T(512)S(1)} %copy-done.5, ...), custom_call_target="tpu_custom_call" | custom-call | tf_op jit(solution)/shard_map/attend_0/pallas_call | solution.py:681
  106.9 36.2 %return_0.1 = bf16[2,24,16,128]{3,2,1,0:T(8,128)(2,1)S(1)} custom-call(f32[8,24,32,128]{3,2,1,0:T(8,128)S(1)} %bitcast.83, f32[8,24,128]{2,1,0:T(8,128)S(1)} %bitcast.95), custom_call_target="tpu_custom_call" | custom-call | tf_op jit(solution)/shard_map/return_0/pallas_call | solution.py:694
  143.1 3.1 %regroup_pages_1.1 = bf16[32,20,8,128]{3,2,1,0:T(8,128)(2,1)} custom-call(s32[641]{0:T(1024)S(1)} %copy-done.3, bf16[512,8,128]{2,1,0:T(8,128)(2,1)} %bitcast.28.x_ref), custom_call_target="tpu_custom_call" | custom-call | tf_op jit(solution)/shard_map/regroup_pages_1/pallas_call | solution.py:613
  146.2 4.9 %all-to-all-start.3 = ((bf16[32,20,8,128]{3,2,1,0:T(8,128)(2,1)}), bf16[32,20,8,128]{3,2,1,0:T(8,128)(2,1)S(1)}, u32[]{:S(2)}, u32[]{:S(2)}) async-start(bf16[32,20,8,128]{3,2,1,0:T(8,128)(2,1)} %regroup_pages_1.1), calls=%async_computation.3 | async-start | bytes 2621440 | tf_op jit(solution)/shard_map/all_to_all | solution.py:619
  151.2 23.1 %mlp_0.1 = (bf16[48,2048]{1,0:T(8,128)(2,1)S(1)}, bf16[48,2048]{1,0:T(8,128)(2,1)S(1)}, bf16[48,256]{1,0:T(8,128)(2,1)S(1)}, bf16[48,256]{1,0:T(8,128)(2,1)S(1)}) custom-call(bf16[48,2048]{1,0:T(8,128)(2,1)S(1)} %bitcast.84, bf16[48,2048]{1,0:T(8,128)(2,1)S(1)} %bitcast.92, bf16[2,2048,2048]{2,1,0:T(8,128)(2,1)} %wo_ref.3, bf16[2,2048,11008]{2,1,0:T(8,128)(2,1)} %up_ref.3, ...), custom_call_target="tpu_custom_call" | custom-call | tf_op jit(solution)/shard_map/mlp_0/pallas_call | solution.py:712
  174.8 17.1 %gather_queries_1.1 = bf16[8,24,40,128]{3,2,1,0:T(8,128)(2,1)S(1)} custom-call(bf16[24,40,128]{2,1,0:T(8,128)(2,1)S(1)} %pad_maximum_fusion.2.x_ref), custom_call_target="tpu_custom_call" | custom-call | tf_op jit(solution)/shard_map/gather_queries_1/pallas_call | solution.py:665
  191.9 10.0 %attend_1.1 = (bf16[112,32,8,128]{3,2,1,0:T(8,128)(2,1)}, bf16[112,32,8,128]{3,2,1,0:T(8,128)(2,1)}, f32[192,32,128]{2,1,0:T(8,128)S(1)}, f32[192,128]{1,0:T(8,128)S(1)}) custom-call(s32[3]{0:T(128)S(1)} %copy-done.4, s32[337]{0:T(512)S(1)} %get-tuple-element.56.arrive_ref, s32[2]{0:T(128)S(1)} %copy-done.6, ...), custom_call_target="tpu_custom_call", output_to_operand_aliasing={{0}: (11, {}), {1}: (12, {})} | custom-call | tf_op jit(solution)/shard_map/attend_1/pallas_call | solution.py:681
  202.0 34.8 %return_1.1 = bf16[2,24,16,128]{3,2,1,0:T(8,128)(2,1)S(1)} custom-call(f32[8,24,32,128]{3,2,1,0:T(8,128)S(1)} %bitcast.82, f32[8,24,128]{2,1,0:T(8,128)S(1)} %bitcast.94), custom_call_target="tpu_custom_call" | custom-call | tf_op jit(solution)/shard_map/return_1/pallas_call | solution.py:694
  236.8 19.5 %mlp_1.1 = bf16[48,2048]{1,0:T(8,128)(2,1)S(1)} custom-call(bf16[48,2048]{1,0:T(8,128)(2,1)S(1)} %bitcast.85, bf16[48,2048]{1,0:T(8,128)(2,1)S(1)} %get-tuple-element.90.hid_ref, bf16[2,2048,2048]{2,1,0:T(8,128)(2,1)} %wo_ref.3, bf16[2,2048,11008]{2,1,0:T(8,128)(2,1)} %up_ref.3, bf16[2,11008,2048]{2,1,0:T(8,128)(2,1)} %dn_ref.3), custom_call_target="tpu_custom_call" | custom-call | tf_op jit(solution)/shard_map/mlp_1/pallas_call | solution.py:712
  256.4 0.7 copy.45
  (39 shorter events, 1.3 us)
Async XLA Ops:
  24.6 8.8 %copy-start = (bf16[2,24,2048]{2,1,0:T(8,128)(2,1)S(1)}, bf16[2,24,2048]{2,1,0:T(8,128)(2,1)}, u32[]{:S(2)}) copy-start(bf16[2,24,2048]{2,1,0:T(8,128)(2,1)} %param.15) | copy-start | bytes 589828
  28.8 12.5 %copy-start.7 = (bf16[2,2048,256]{2,1,0:T(8,128)(2,1)S(1)}, bf16[2,2048,256]{2,1,0:T(8,128)(2,1)}, u32[]{:S(2)}) copy-start(bf16[2,2048,256]{2,1,0:T(8,128)(2,1)} %rest_2_.1) | copy-start | bytes 6291460
  28.8 21.9 %all-to-all-start = ((bf16[32,16,8,128]{3,2,1,0:T(8,128)(2,1)}), bf16[32,16,8,128]{3,2,1,0:T(8,128)(2,1)S(1)}, u32[]{:S(2)}, u32[]{:S(2)}) async-start(bf16[32,16,8,128]{3,2,1,0:T(8,128)(2,1)} %get-tuple-element.58), calls=%async_computation | async-start | bytes 2097152 | tf_op jit(solution)/shard_map/all_to_all | solution.py:603
  49.6 46.5 %copy-start.6 = (s32[2]{0:T(128)S(1)}, s32[2]{0:T(128)}, u32[]{:S(2)}) copy-start(s32[2]{0:T(128)} %get-tuple-element.57.most_ref) | copy-start | bytes 28
  50.7 0.7 copy-start.2
  53.8 37.8 %all-to-all-start.1 = ((bf16[32,20,8,128]{3,2,1,0:T(8,128)(2,1)}), bf16[32,20,8,128]{3,2,1,0:T(8,128)(2,1)S(1)}, u32[]{:S(2)}, u32[]{:S(2)}) async-start(bf16[32,20,8,128]{3,2,1,0:T(8,128)(2,1)} %regroup_pages_0.1), calls=%async_computation.1 | async-start | bytes 2621440 | tf_op jit(solution)/shard_map/all_to_all | solution.py:619
  91.6 4.6 %collective-permute-start = (bf16[32,20,8,128]{3,2,1,0:T(8,128)(2,1)S(1)}, bf16[32,20,8,128]{3,2,1,0:T(8,128)(2,1)}, u32[]{:S(2)}, u32[]{:S(2)}) collective-permute-start(bf16[32,20,8,128]{3,2,1,0:T(8,128)(2,1)S(1)} %all-to-all-done.1.own_ref), channel_id=1, source_target_pairs={{0,1},{1,0},{2,3},{3,2},{4,5},{5,4},{6,7},{7,6},{8,9},{9,8},{10,11... | collective-permute-start | bytes 3932168 | tf_op jit(solution)/shard_map/ppermute | solution.py:622
  91.8 51.3 %all-to-all-start.2 = ((bf16[32,16,8,128]{3,2,1,0:T(8,128)(2,1)}), bf16[32,16,8,128]{3,2,1,0:T(8,128)(2,1)}, u32[]{:S(2)}, u32[]{:S(2)}) async-start(bf16[32,16,8,128]{3,2,1,0:T(8,128)(2,1)} %get-tuple-element.72), calls=%async_computation.2 | async-start | bytes 2097152 | tf_op jit(solution)/shard_map/all_to_all | solution.py:679
  96.2 0.7 copy-start.4
  96.2 0.7 copy-start.5
  96.9 46.3 %copy-start.3 = (s32[641]{0:T(1024)S(1)}, s32[641]{0:T(1024)}, u32[]{:S(2)}) copy-start(s32[641]{0:T(1024)} %get-tuple-element.60.pages_ref) | copy-start | bytes 7696
  106.8 44.3 %copy-start.1 = (bf16[2,24,2048]{2,1,0:T(8,128)(2,1)S(1)}, bf16[2,24,2048]{2,1,0:T(8,128)(2,1)}, u32[]{:S(2)}) copy-start(bf16[2,24,2048]{2,1,0:T(8,128)(2,1)} %param.15) | copy-start | bytes 589828
  146.2 28.3 %all-to-all-start.3 = ((bf16[32,20,8,128]{3,2,1,0:T(8,128)(2,1)}), bf16[32,20,8,128]{3,2,1,0:T(8,128)(2,1)S(1)}, u32[]{:S(2)}, u32[]{:S(2)}) async-start(bf16[32,20,8,128]{3,2,1,0:T(8,128)(2,1)} %regroup_pages_1.1), calls=%async_computation.3 | async-start | bytes 2621440 | tf_op jit(solution)/shard_map/all_to_all | solution.py:619
  174.5 17.4 %collective-permute-start.1 = (bf16[32,20,8,128]{3,2,1,0:T(8,128)(2,1)S(1)}, bf16[32,20,8,128]{3,2,1,0:T(8,128)(2,1)S(1)}, u32[]{:S(2)}, u32[]{:S(2)}) collective-permute-start(bf16[32,20,8,128]{3,2,1,0:T(8,128)(2,1)S(1)} %all-to-all-done.3.own_ref), channel_id=1, source_target_pairs={{0,1},{1,0},{2,3},{3,2},{4,5},{5,4},{6,7},{7,6},{8,9},{9,8},{10,11... | collective-permute-start | bytes 3932168 | tf_op jit(solution)/shard_map/ppermute | solution.py:622
